TPU v7x, 128 devices: a whole 4x4x4 slice. The times are simulated.
128 devices in a mesh: tile: 64 (over x, z, y), lev: 2 (over core).
Axes of the slice: x: 4, y: 4, z: 4, core: 2. Of those that a mesh axis runs over, the one named last changes fastest.
Arguments:
- increments: bfloat16 [136, 1024, 1024], P('lev', 'tile'), may hold values from -30 to 30
- projection: bfloat16 [80, 136], replicated, may hold values from -0.5 to 0.5
- helmholtz: float32 [80], P('lev'), may hold values from 0.05 to 4
Outputs:
- solution: float32 [80, 1024, 1024], P('lev', 'tile')
- residual: float32 [80, 1024, 1024], P('lev', 'tile')
All inputs are finite; a program needn't handle non-finite values.
Results may differ from a plain program's by a relative error of at most 0.00075.
Values may be sent and summed in bfloat16 or wider, within the bound.
No kernel may reach another device: no remote copies, remote signals or barrier semaphores. Data moves between devices by JAX's collectives and lax.ppermute only.
A program may use at most 192 MiB of HBM per device.

v0:
```python
import functools

import jax
import jax.numpy as jnp
from jax import lax
from jax.experimental import pallas as pl
from jax.experimental.pallas import tpu as pltpu
from jax.sharding import PartitionSpec as P

STEPS = 8
MOMENTS = 2 * STEPS + 1
ROWS = 16
HALO = 8
MODES = 40
GROUPS = 5
LANES = 128
COLS = 1024
BLOCKS = COLS // LANES
TILES = 64
CODE_BITS = 31
CODE = 2.0 ** CODE_BITS

f32 = jnp.float32
bf16 = jnp.bfloat16


def limits(mib):
    return pltpu.CompilerParams(vmem_limit_bytes=mib * 2**20)


def build_left(proj_ref, left_ref, level0):
    lev = lax.axis_index("lev")
    depth = left_ref.shape[1]
    pick = (
        lax.broadcasted_iota(jnp.int32, (MODES, 2 * MODES), 1)
        == lax.broadcasted_iota(jnp.int32, (MODES, 2 * MODES), 0) + lev * MODES
    ).astype(bf16)
    own = jnp.dot(pick, proj_ref[...], preferred_element_type=f32).astype(bf16)
    levels = proj_ref.shape[1]
    spread = (
        lax.broadcasted_iota(jnp.int32, (levels, depth), 0)
        == (lax.broadcasted_iota(jnp.int32, (levels, depth), 1) >> 4) + level0
    ).astype(bf16)
    wide = jnp.dot(own, spread, preferred_element_type=f32)
    row_of = lax.broadcasted_iota(jnp.int32, (8, depth), 1) & (ROWS - 1)
    for group in range(GROUPS):
        part = wide[group * 8:(group + 1) * 8]
        for row in range(0, ROWS, 2):
            two = jnp.concatenate(
                [jnp.where(row_of == row, part, 0.0), jnp.where(row_of == row + 1, part, 0.0)],
                axis=0,
            )
            at = group * 8 * ROWS + row * 8
            left_ref[at:at + 16, :] = two.astype(bf16)


def own_levels_kernel(proj_ref, inc_ref, acc_ref, other_left_ref, left_ref):
    lev = lax.axis_index("lev")
    count = proj_ref.shape[1] // 2

    @pl.when(pl.program_id(0) == 0)
    def _():
        build_left(proj_ref, left_ref, lev * count)
        build_left(proj_ref, other_left_ref, (1 - lev) * count)

    acc_ref[...] = jnp.dot(left_ref[...], inc_ref[...], preferred_element_type=f32)


def other_levels_kernel(left_ref, inc_ref, acc_ref, modal_ref, a_ref, b_ref):
    even = (lax.axis_index("tile") & 1) == 0
    modal_ref[...] = acc_ref[...] + jnp.dot(
        left_ref[...], inc_ref[...], preferred_element_type=f32
    )
    half = 8 * HALO
    for group in range(GROUPS):
        at = group * 2 * half
        low = modal_ref[at:at + half, :]
        high = modal_ref[at + half:at + 2 * half, :]
        for ref, value in (
            (a_ref, jnp.where(even, high, low)),
            (b_ref, jnp.where(even, low, high)),
        ):
            scaled = value * CODE
            ref[group * half:(group + 1) * half, :] = (scaled * scaled * scaled).astype(bf16)


def modal_product(increments, projection):
    levels = increments.shape[0]
    depth = levels * ROWS
    flat = increments.reshape(depth, COLS)
    arrived = lax.ppermute(flat, "lev", [(0, 1), (1, 0)])
    width = 256
    grid = (COLS // width,)
    total = MODES * ROWS
    acc, other_left = pl.pallas_call(
        own_levels_kernel,
        grid=grid,
        in_specs=[
            pl.BlockSpec(projection.shape, lambda c: (0, 0)),
            pl.BlockSpec((depth, width), lambda c: (0, c)),
        ],
        out_specs=[
            pl.BlockSpec((total, width), lambda c: (0, c)),
            pl.BlockSpec((total, depth), lambda c: (0, 0)),
        ],
        out_shape=[
            jax.ShapeDtypeStruct((total, COLS), f32),
            jax.ShapeDtypeStruct((total, depth), bf16),
        ],
        scratch_shapes=[pltpu.VMEM((total, depth), bf16)],
        compiler_params=limits(20),
        name="own_levels",
    )(projection, flat)
    half = total // 2
    return pl.pallas_call(
        other_levels_kernel,
        grid=grid,
        in_specs=[
            pl.BlockSpec((total, depth), lambda c: (0, 0)),
            pl.BlockSpec((depth, width), lambda c: (0, c)),
            pl.BlockSpec((total, width), lambda c: (0, c)),
        ],
        out_specs=[
            pl.BlockSpec((total, width), lambda c: (0, c)),
            pl.BlockSpec((half, width), lambda c: (0, c)),
            pl.BlockSpec((half, width), lambda c: (0, c)),
        ],
        out_shape=[
            jax.ShapeDtypeStruct((total, COLS), f32),
            jax.ShapeDtypeStruct((half, COLS), bf16),
            jax.ShapeDtypeStruct((half, COLS), bf16),
        ],
        compiler_params=limits(20),
        name="other_levels",
    )(other_left, arrived, acc)


def decoded(value):
    value = value.astype(f32)
    root = jnp.exp2(jnp.log2(jnp.abs(value)) * (1.0 / 3.0) - CODE_BITS)
    return jnp.where(value < 0.0, -root, root)


def basis_kernel(modal_ref, a_ref, b_ref, basis_ref, moment_ref, low_ref, high_ref, sums_ref):
    tile = lax.axis_index("tile")
    even = (tile & 1) == 0
    group = pl.program_id(0)
    for row in range(0, HALO, 2):
        part = slice(row * 8, row * 8 + 16)
        a = decoded(a_ref[part, :])
        b = decoded(b_ref[part, :])
        low_ref[0, part, :] = jnp.where(even, b, a)
        high_ref[0, part, :] = jnp.where(even, a, b)
    lane = lax.broadcasted_iota(jnp.int32, (8, LANES), 1)
    first = lane == 0
    last = lane == LANES - 1
    half_low = jnp.where(tile == 0, 0.0, 0.5)
    half_high = jnp.where(tile == TILES - 1, 0.0, 0.5)

    def load(order, row):
        if row < 0:
            at = (row + HALO) * 8
            return [low_ref[order % 3, at:at + 8, b * LANES:(b + 1) * LANES] for b in range(BLOCKS)]
        if row >= ROWS:
            at = (row - ROWS) * 8
            return [high_ref[order % 3, at:at + 8, b * LANES:(b + 1) * LANES] for b in range(BLOCKS)]
        at = row * 8
        if order == 0:
            return [modal_ref[at:at + 8, b * LANES:(b + 1) * LANES] for b in range(BLOCKS)]
        return [basis_ref[order - 1, at:at + 8, b * LANES:(b + 1) * LANES] for b in range(BLOCKS)]

    def store(order, row, values):
        for b, value in enumerate(values):
            cols = slice(b * LANES, (b + 1) * LANES)
            if row < 0:
                at = (row + HALO) * 8
                low_ref[order % 3, at:at + 8, cols] = value
            elif row >= ROWS:
                at = (row - ROWS) * 8
                high_ref[order % 3, at:at + 8, cols] = value
            else:
                basis_ref[order - 1, row * 8:row * 8 + 8, cols] = value

    def diagonal(field, below):
        turned = [pltpu.roll(v, LANES - 1, 1) for v in below]
        out = []
        for b in range(BLOCKS):
            edge = turned[b + 1] if b + 1 < BLOCKS else 0.0
            out.append(field[b] + jnp.where(last, edge, turned[b]))
        return out

    def total(values):
        while len(values) > 1:
            values = [values[i] + values[i + 1] for i in range(0, len(values), 2)]
        return values[0]

    square0 = jnp.zeros((8, LANES), f32)
    for order in range(1, STEPS + 1):
        square = jnp.zeros((8, LANES), f32)
        cross = jnp.zeros((8, LANES), f32)
        begin, end = order - HALO, ROWS + HALO - order
        before = load(order - 1, begin - 1)
        here = load(order - 1, begin)
        upper = diagonal(before, here)
        for row in range(begin, end):
            below = load(order - 1, row + 1)
            lower = diagonal(here, below)
            turned = [pltpu.roll(v, 1, 1) for v in lower]
            new = []
            if order == 1:
                factor = 0.25 if 0 <= row < ROWS else (half_low if row < 0 else half_high) * 0.5
                older = None
            else:
                factor = 0.5 if 0 <= row < ROWS else (half_low if row < 0 else half_high)
                older = load(order - 2, row)
            for b in range(BLOCKS):
                edge = turned[b - 1] if b else below[0]
                value = (upper[b] + jnp.where(first, edge, turned[b])) * factor
                if older is not None:
                    value = value - older[b]
                new.append(value)
            store(order, row, new)
            if 0 <= row < ROWS:
                square = square + total([v * v for v in new])
                cross = cross + total([v * w for v, w in zip(new, here)])
                if order == 1:
                    square0 = square0 + total([v * v for v in here])
            upper, here = lower, below
        if order == 1:
            sums_ref[0] = square0
        sums_ref[2 * order - 1] = cross
        sums_ref[2 * order] = square

    @pl.when(group == 0)
    def _():
        moment_ref[...] = jnp.zeros_like(moment_ref)

    packed = moment_ref[...]
    for index in range(MOMENTS):
        value = jnp.sum(sums_ref[index], axis=1, keepdims=True)
        packed = jnp.where(lane == index * GROUPS + group, value, packed)
    moment_ref[...] = packed


def basis_and_moments(modal, a, b):
    rows = 8 * ROWS
    halo = 8 * HALO
    return pl.pallas_call(
        basis_kernel,
        grid=(GROUPS,),
        in_specs=[
            pl.BlockSpec((rows, COLS), lambda g: (g, 0)),
            pl.BlockSpec((halo, COLS), lambda g: (g, 0)),
            pl.BlockSpec((halo, COLS), lambda g: (g, 0)),
        ],
        out_specs=[
            pl.BlockSpec((STEPS, rows, COLS), lambda g: (0, g, 0)),
            pl.BlockSpec((8, LANES), lambda g: (0, 0)),
        ],
        out_shape=[
            jax.ShapeDtypeStruct((STEPS, MODES * ROWS, COLS), f32),
            jax.ShapeDtypeStruct((8, LANES), f32),
        ],
        scratch_shapes=[
            pltpu.VMEM((3, halo, COLS), f32),
            pltpu.VMEM((3, halo, COLS), f32),
            pltpu.VMEM((MOMENTS, 8, LANES), f32),
        ],
        compiler_params=limits(20),
        name="basis",
    )(modal, a, b)


def coefficients(nu, tau):
    half = 0.5 * tau
    rho = list(nu)
    pi = list(nu)
    one, zero = jnp.ones_like(tau), None
    r = [one]
    p = [one]
    x = [None] * STEPS
    rr = nu[0]

    def plus(a, b):
        if a is None:
            return b
        if b is None:
            return a
        return a + b

    def inner(c, v):
        terms = [ci * vi for ci, vi in zip(c, v)]
        while len(terms) > 1:
            terms = [sum(terms[i:i + 2]) for i in range(0, len(terms), 2)]
        return terms[0]

    for step in range(STEPS):
        top = MOMENTS - 1 - step
        image = []
        for l in range(top):
            near = pi[l + 1] + pi[abs(l - 1)]
            image.append(pi[l] - half * near)
        alpha = rr / inner(p, image)
        x = [plus(x[i], alpha * p[i]) if i < len(p) else x[i] for i in range(STEPS)]
        shifted = [None] * (len(p) + 1)
        for k, value in enumerate(p):
            if k == 0:
                shifted[1] = plus(shifted[1], tau * value)
            else:
                scaled = half * value
                shifted[k + 1] = plus(shifted[k + 1], scaled)
                shifted[k - 1] = plus(shifted[k - 1], scaled)
        moved = []
        for k in range(len(p) + 1):
            own = p[k] if k < len(p) else None
            if shifted[k] is None:
                moved.append(own)
            elif own is None:
                moved.append(-shifted[k])
            else:
                moved.append(own - shifted[k])
        r = [
            (r[k] - alpha * moved[k]) if k < len(r) else -(alpha * moved[k])
            for k in range(len(moved))
        ]
        if step == STEPS - 1:
            break
        rho = [rho[l] - alpha * image[l] for l in range(top)]
        fresh = inner(r, rho)
        beta = fresh / rr
        pi = [rho[l] + beta * pi[l] for l in range(top)]
        p = [plus(r[k], beta * p[k] if k < len(p) else None) for k in range(len(r))]
        rr = fresh
    return x, r


def solve_kernel(sums_ref, helm_ref, modal_ref, basis_ref, x_ref, r_ref, coef_ref):
    group = pl.program_id(0)

    @pl.when(group == 0)
    def _():
        parts = [sums_ref[i] for i in range(TILES)]
        while len(parts) > 1:
            parts = [parts[i] + parts[i + 1] for i in range(0, len(parts), 2)]
        moments = parts[0]
        raw = [moments if k == 0 else pltpu.roll(moments, LANES - GROUPS * k, 1) for k in range(MOMENTS)]
        nu = raw[:2]
        for k in range(2, MOMENTS):
            nu.append(2.0 * raw[k] - nu[k & 1])
        tau = 4.0 / (4.0 + helm_ref[...])
        x, r = coefficients(nu, tau)
        for g in range(GROUPS):
            for k, value in enumerate(x + r):
                coef_ref[g, k] = jnp.broadcast_to(value[:, g:g + 1], (8, LANES))

    for b in range(BLOCKS):
        cols = slice(b * LANES, (b + 1) * LANES)
        cx = [coef_ref[group, k] for k in range(STEPS)]
        cr = [coef_ref[group, STEPS + k] for k in range(STEPS + 1)]
        for top in range(0, ROWS, 8):
            xs, rs = [], []
            for row in range(top, top + 8):
                at = slice(row * 8, row * 8 + 8)
                field = modal_ref[at, cols]
                x = cx[0] * field
                r = cr[0] * field
                for k in range(1, STEPS + 1):
                    field = basis_ref[k - 1, at, cols]
                    if k < STEPS:
                        x = x + cx[k] * field
                    r = r + cr[k] * field
                xs.append(x)
                rs.append(r)
            x_ref[:, top:top + 8, cols] = jnp.swapaxes(jnp.stack(xs), 0, 1)
            r_ref[:, top:top + 8, cols] = jnp.swapaxes(jnp.stack(rs), 0, 1)


def solve(sums, helm, modal, basis):
    rows = 8 * ROWS
    out = jax.ShapeDtypeStruct((MODES, ROWS, COLS), f32)
    return pl.pallas_call(
        solve_kernel,
        grid=(GROUPS,),
        in_specs=[
            pl.BlockSpec((TILES, 8, LANES), lambda g: (0, 0, 0)),
            pl.BlockSpec((8, LANES), lambda g: (0, 0)),
            pl.BlockSpec((rows, COLS), lambda g: (g, 0)),
            pl.BlockSpec((STEPS, rows, COLS), lambda g: (0, g, 0)),
        ],
        out_specs=[
            pl.BlockSpec((8, ROWS, COLS), lambda g: (g, 0, 0)),
            pl.BlockSpec((8, ROWS, COLS), lambda g: (g, 0, 0)),
        ],
        out_shape=[out, out],
        scratch_shapes=[pltpu.VMEM((GROUPS, MOMENTS, 8, LANES), f32)],
        compiler_params=limits(20),
        name="solve",
    )(sums, helm, modal, basis)


def shards(increments, projection, helmholtz):
    modal, a, b = modal_product(increments, projection)
    swap_a = [(i, i ^ 1) for i in range(TILES)]
    swap_b = [(i, i + 1) for i in range(1, TILES - 1, 2)]
    swap_b += [(target, source) for source, target in swap_b]
    a = lax.ppermute(a, "tile", swap_a)
    b = lax.ppermute(b, "tile", swap_b)
    basis, moments = basis_and_moments(modal, a, b)
    spread = jnp.broadcast_to(moments[None], (TILES, 8, LANES))
    sums = lax.all_to_all(spread, "tile", 0, 0, tiled=True)
    helm = jnp.pad(helmholtz.reshape(GROUPS, 8).T, ((0, 0), (0, LANES - GROUPS)))
    return tuple(solve(sums, helm, modal, basis))


def solution(mesh):
    in_specs = (P("lev", "tile", None), P(), P("lev"))
    out_specs = (P("lev", "tile", None), P("lev", "tile", None))
    return jax.shard_map(shards, mesh=mesh, in_specs=in_specs, out_specs=out_specs, check_vma=False)
```

profile of v0, /device:TPU:0, one launch (start us, length us, event | category | flops | bytes accessed | tf_op | source)
XLA Modules:
  0.0 152.8 jit_solution(17718477738471766960)
XLA Ops:
  0.6 0.1 collective-permute-start
  0.7 0.8 copy.5.proj_ref
  1.6 0.0 copy-start.2
  1.6 1.6 %copy-done.2 = bf16[68,16,1024]{2,1,0:T(8,128)(2,1)S(1)} copy-done((bf16[68,16,1024]{2,1,0:T(8,128)(2,1)S(1)}, bf16[68,16,1024]{2,1,0:T(8,128)(2,1)}, u32[]{:S(2)}) %copy-start.2) | copy-done | bytes 2228248
  3.2 3.7 %own_levels.1 = (f32[640,1024]{1,0:T(8,128)S(1)}, bf16[640,1088]{1,0:T(8,128)(2,1)S(1)}) custom-call(bf16[80,136]{1,0:T(8,128)(2,1)S(1)} %copy.5.proj_ref, bf16[1088,1024]{1,0:T(8,128)(2,1)S(1)} %bitcast.3), custom_call_target="tpu_custom_call" | custom-call | tf_op jit(solution)/shard_map/own_levels/pallas_call | solution.py:95
  6.9 0.0 collective-permute-done.inc_ref
  6.9 0.0 copy-start.3
  7.0 1.4 copy-done.3
  8.3 0.0 copy-start.4
  8.3 1.6 %copy-done.4 = bf16[1088,1024]{1,0:T(8,128)(2,1)S(1)} copy-done((bf16[1088,1024]{1,0:T(8,128)(2,1)S(1)}, bf16[1088,1024]{1,0:T(8,128)(2,1)}, u32[]{:S(2)}) %copy-start.4) | copy-done | bytes 2228248
  9.9 3.3 %other_levels.1 = (f32[640,1024]{1,0:T(8,128)S(1)}, bf16[320,1024]{1,0:T(8,128)(2,1)S(1)}, bf16[320,1024]{1,0:T(8,128)(2,1)S(1)}) custom-call(bf16[640,1088]{1,0:T(8,128)(2,1)S(1)} %get-tuple-element.9.left_ref, bf16[1088,1024]{1,0:T(8,128)(2,1)S(1)} %copy-done.4, f32[640,1024]{1,0:T(8,128)S(1)} %get-tuple-element.10.acc_ref), custom_call_target="tpu_custom_call" | custom-call | tf_op jit(solution)/shard_map/other_levels/pallas_call | solution.py:115
  13.2 0.0 copy-start.5
  13.3 1.8 %collective-permute-start.1 = (bf16[320,1024]{1,0:T(8,128)(2,1)S(1)}, bf16[320,1024]{1,0:T(8,128)(2,1)S(1)}, u32[]{:S(2)}, u32[]{:S(2)}) collective-permute-start(bf16[320,1024]{1,0:T(8,128)(2,1)S(1)} %get-tuple-element.12), channel_id=1, source_target_pairs={{0,2},{2,0},{4,6},{6,4},{8,10},{10,8},{12,14},{14,12},{16,18},{18,... | collective-permute-start | bytes 1966088 | tf_op jit(solution)/shard_map/ppermute | solution.py:406
  15.0 0.7 collective-permute-start.2
  15.7 14.7 %collective-permute-done.1.a_ref = bf16[320,1024]{1,0:T(8,128)(2,1)S(1)} collective-permute-done((bf16[320,1024]{1,0:T(8,128)(2,1)S(1)}, bf16[320,1024]{1,0:T(8,128)(2,1)S(1)}, u32[]{:S(2)}, u32[]{:S(2)}) %collective-permute-start.1) | collective-permute-done | bytes 655392 | tf_op jit(solution)/shard_map/ppermute | solution.py:406
  30.5 0.0 collective-permute-done.2.b_ref
  30.5 71.9 %basis.1 = (f32[8,640,1024]{2,1,0:T(8,128)S(1)}, f32[8,128]{1,0:T(8,128)S(1)}) custom-call(f32[640,1024]{1,0:T(8,128)S(1)} %get-tuple-element.11.modal_ref, bf16[320,1024]{1,0:T(8,128)(2,1)S(1)} %collective-permute-done.1.a_ref, bf16[320,1024]{1,0:T(8,128)(2,1)S(1)} %collective-permute-done.2.b_ref), custom_call_target="tpu_custom_call" | custom-call | tf_op jit(solution)/shard_map/basis/pallas_call | solution.py:248
  102.4 0.0 copy-start
  102.4 7.0 %copy-done = f32[8,640,1024]{2,1,0:T(8,128)} copy-done((f32[8,640,1024]{2,1,0:T(8,128)}, f32[8,640,1024]{2,1,0:T(8,128)S(1)}, u32[]{:S(2)}) %copy-start) | copy-done | bytes 20971544
  109.4 0.7 broadcast_in_dim.2
  110.1 17.9 %all-to-all-start = ((f32[64,8,128]{2,1,0:T(8,128)}), f32[64,8,128]{2,1,0:T(8,128)S(1)}, u32[]{:S(2)}, u32[]{:S(2)}) async-start(f32[64,8,128]{2,1,0:T(8,128)} %broadcast_in_dim.2), calls=%async_computation | async-start | bytes 524288 | tf_op jit(solution)/shard_map/all_to_all | solution.py:410
  128.0 0.0 copy-done.5
  128.0 0.1 reshape.12
  128.1 0.1 copy.6
  128.2 10.2 %all-to-all-done.sums_ref = f32[64,8,128]{2,1,0:T(8,128)S(1)} async-done(((f32[64,8,128]{2,1,0:T(8,128)}), f32[64,8,128]{2,1,0:T(8,128)S(1)}, u32[]{:S(2)}, u32[]{:S(2)}) %all-to-all-start) | async-done | bytes 262176 | tf_op jit(solution)/shard_map/all_to_all | solution.py:410
  138.5 0.0 copy-start.1
  138.5 7.0 %copy-done.1 = f32[8,640,1024]{2,1,0:T(8,128)S(1)} copy-done((f32[8,640,1024]{2,1,0:T(8,128)S(1)}, f32[8,640,1024]{2,1,0:T(8,128)}, u32[]{:S(2)}) %copy-start.1) | copy-done | bytes 20971544
  145.4 7.4 %solve.1 = (f32[40,16,1024]{2,1,0:T(8,128)}, f32[40,16,1024]{2,1,0:T(8,128)}) custom-call(f32[64,8,128]{2,1,0:T(8,128)S(1)} %all-to-all-done.sums_ref, f32[8,128]{1,0:T(8,128)S(1)} %pad.4.helm_ref, f32[640,1024]{1,0:T(8,128)S(1)} %get-tuple-element.11.modal_ref, f32[8,640,1024]{2,1,0:T(8,128)S(1)} %copy-done.1), custom_call_target="tpu_custom_call" | custom-call | tf_op jit(solution)/shard_map/solve/pallas_call | solution.py:381
  (1 shorter events, 0.0 us)
Async XLA Ops:
  0.6 6.3 %collective-permute-start = (bf16[1088,1024]{1,0:T(8,128)(2,1)}, bf16[1088,1024]{1,0:T(8,128)(2,1)S(1)}, u32[]{:S(2)}, u32[]{:S(2)}) collective-permute-start(bf16[1088,1024]{1,0:T(8,128)(2,1)} %bitcast.2), channel_id=1, source_target_pairs={{0,1},{1,0},{2,3},{3,2},{4,5},{5,4},{6,7},{7,6},{8,9},{9,8},{10,11... | collective-permute-start | bytes 6684680 | tf_op jit(solution)/shard_map/ppermute | solution.py:91
  1.6 1.6 %copy-start.2 = (bf16[68,16,1024]{2,1,0:T(8,128)(2,1)S(1)}, bf16[68,16,1024]{2,1,0:T(8,128)(2,1)}, u32[]{:S(2)}) copy-start(bf16[68,16,1024]{2,1,0:T(8,128)(2,1)} %param.3) | copy-start | bytes 6684676
  6.9 1.4 copy-start.3
  8.3 1.6 %copy-start.4 = (bf16[1088,1024]{1,0:T(8,128)(2,1)S(1)}, bf16[1088,1024]{1,0:T(8,128)(2,1)}, u32[]{:S(2)}) copy-start(bf16[1088,1024]{1,0:T(8,128)(2,1)} %copy-done.3) | copy-start | bytes 6684676
  13.2 114.8 %copy-start.5 = (f32[40]{0:T(128)S(1)}, f32[40]{0:T(128)}, u32[]{:S(2)}) copy-start(f32[40]{0:T(128)} %param.5) | copy-start | bytes 484
  13.3 17.2 %collective-permute-start.1 = (bf16[320,1024]{1,0:T(8,128)(2,1)S(1)}, bf16[320,1024]{1,0:T(8,128)(2,1)S(1)}, u32[]{:S(2)}, u32[]{:S(2)}) collective-permute-start(bf16[320,1024]{1,0:T(8,128)(2,1)S(1)} %get-tuple-element.12), channel_id=1, source_target_pairs={{0,2},{2,0},{4,6},{6,4},{8,10},{10,8},{12,14},{14,12},{16,18},{18,... | collective-permute-start | bytes 1966088 | tf_op jit(solution)/shard_map/ppermute | solution.py:406
  15.0 15.4 %collective-permute-start.2 = (bf16[320,1024]{1,0:T(8,128)(2,1)S(1)}, bf16[320,1024]{1,0:T(8,128)(2,1)S(1)}, u32[]{:S(2)}, u32[]{:S(2)}) collective-permute-start(bf16[320,1024]{1,0:T(8,128)(2,1)S(1)} %get-tuple-element.13), channel_id=1, source_target_pairs={{2,4},{6,8},{10,12},{14,16},{18,20},{22,24},{26,28},{30,32},{34,36... | collective-permute-start | bytes 1966088 | tf_op jit(solution)/shard_map/ppermute | solution.py:407
  102.4 7.0 %copy-start = (f32[8,640,1024]{2,1,0:T(8,128)}, f32[8,640,1024]{2,1,0:T(8,128)S(1)}, u32[]{:S(2)}) copy-start(f32[8,640,1024]{2,1,0:T(8,128)S(1)} %get-tuple-element.15.basis_ref) | copy-start | bytes 62914564
  110.1 28.3 %all-to-all-start = ((f32[64,8,128]{2,1,0:T(8,128)}), f32[64,8,128]{2,1,0:T(8,128)S(1)}, u32[]{:S(2)}, u32[]{:S(2)}) async-start(f32[64,8,128]{2,1,0:T(8,128)} %broadcast_in_dim.2), calls=%async_computation | async-start | bytes 524288 | tf_op jit(solution)/shard_map/all_to_all | solution.py:410
  138.5 7.0 %copy-start.1 = (f32[8,640,1024]{2,1,0:T(8,128)S(1)}, f32[8,640,1024]{2,1,0:T(8,128)}, u32[]{:S(2)}) copy-start(f32[8,640,1024]{2,1,0:T(8,128)} %copy-done) | copy-start | bytes 62914564
where the time goes:
time: 153 us
  Pallas kernels  86.3 us (56%)
  waiting for transfers between devices  25 us (16%)
  starting transfers between devices  20.5 us (13%)
  local copies, waits for them, and re-layouts  20.3 us (13%)
    pallas_call x1, Pallas kernels, basis_and_moments(): pl.pallas_call(basis_kernel, grid=(GROUPS,), in_specs=[pl.BlockSpec((rows...  71.9 us
    unnamed x13, local copies, waits for them, and re-layouts  19.4 us
    all_to_all x1, starting transfers between devices, shards(): sums = lax.all_to_all(spread, 'tile', 0, 0, tiled=True)  17.9 us
    ppermute x1, waiting for transfers between devices, shards(): a = lax.ppermute(a, 'tile', swap_a)  14.7 us
    all_to_all x1, waiting for transfers between devices, shards(): sums = lax.all_to_all(spread, 'tile', 0, 0, tiled=True)  10.2 us
    pallas_call x1, Pallas kernels, solve(): pl.pallas_call(solve_kernel, grid=(GROUPS,), in_specs=[pl.BlockSpec((TILE...  7.36 us
    pallas_call x1, Pallas kernels, modal_product(): pl.pallas_call(own_levels_kernel, grid=grid, in_specs=[pl.BlockSpec(proje...  3.72 us
    pallas_call x1, Pallas kernels, modal_product(): pl.pallas_call(other_levels_kernel, grid=grid, in_specs=[pl.BlockSpec((to...  3.3 us
  transfers between devices with their start and end apart: 4, of which 2 were waited for; matrix products, arithmetic and copies ran while one was open for 1% of the time, Pallas kernels for 2%

commit v1 on v0

v1 whole, which is shorter than its diff:
```python
import functools

import jax
import jax.numpy as jnp
from jax import lax
from jax.experimental import pallas as pl
from jax.experimental.pallas import tpu as pltpu
from jax.sharding import PartitionSpec as P

STEPS = 8
MOMENTS = 2 * STEPS + 1
ROWS = 16
HALO = 8
MODES = 40
GROUPS = 5
LANES = 128
COLS = 1024
BLOCKS = COLS // LANES
TILES = 64
CHUNKS = (3, 2)

f32 = jnp.float32
bf16 = jnp.bfloat16


def limits(mib):
    return pltpu.CompilerParams(vmem_limit_bytes=mib * 2**20)


def build_left(proj_ref, left_refs, level0):
    lev = lax.axis_index("lev")
    depth = left_refs[0].shape[1]
    pick = (
        lax.broadcasted_iota(jnp.int32, (MODES, 2 * MODES), 1)
        == lax.broadcasted_iota(jnp.int32, (MODES, 2 * MODES), 0) + lev * MODES
    ).astype(bf16)
    own = lax.dot_general(
        pick, proj_ref[...], (((1,), (1,)), ((), ())), preferred_element_type=f32
    ).astype(bf16)
    levels = proj_ref.shape[0]
    spread = (
        lax.broadcasted_iota(jnp.int32, (levels, depth), 0)
        == (lax.broadcasted_iota(jnp.int32, (levels, depth), 1) >> 4) + level0
    ).astype(bf16)
    wide = jnp.dot(own, spread, preferred_element_type=f32)
    row_of = lax.broadcasted_iota(jnp.int32, (8, depth), 1) & (ROWS - 1)
    group = 0
    for ref in left_refs:
        for at in range(0, ref.shape[0], 8 * ROWS):
            part = wide[group * 8:(group + 1) * 8]
            for row in range(0, ROWS, 2):
                two = jnp.concatenate(
                    [jnp.where(row_of == row, part, 0.0), jnp.where(row_of == row + 1, part, 0.0)],
                    axis=0,
                )
                ref[at + row * 8:at + row * 8 + 16, :] = two.astype(bf16)
            group += 1


def own_levels_kernel(proj_ref, inc_ref, *refs):
    lev = lax.axis_index("lev")
    count = proj_ref.shape[0] // 2
    parts = len(CHUNKS)
    acc_refs, other_refs, left_refs = refs[:parts], refs[parts:2 * parts], refs[2 * parts:]

    @pl.when(pl.program_id(0) == 0)
    def _():
        build_left(proj_ref, left_refs, lev * count)
        build_left(proj_ref, other_refs, (1 - lev) * count)

    for acc_ref, left_ref in zip(acc_refs, left_refs):
        acc_ref[...] = jnp.dot(left_ref[...], inc_ref[...], preferred_element_type=f32)


def coded(x):
    t = x * 2.0 ** 13
    square = t * t
    eight = t * 8.0
    y = jnp.where(square < 1.0, eight * jnp.abs(eight), (square * 8.0) * ((square * 8.0) * t))
    return y.astype(bf16)


def decoded(y):
    y = y.astype(f32)
    exponent = jnp.log2(jnp.abs(y)) - 6.0
    root = jnp.exp2(exponent * jnp.where(exponent < 0.0, 0.5, 0.2) - 13.0)
    return jnp.where(y < 0.0, -root, root)


def other_levels_kernel(left_ref, inc_ref, acc_ref, modal_ref, a_ref, b_ref):
    even = (lax.axis_index("tile") & 1) == 0
    modal_ref[...] = acc_ref[...] + jnp.dot(
        left_ref[...], inc_ref[...], preferred_element_type=f32
    )
    half = 8 * HALO
    for at in range(0, a_ref.shape[0], half):
        low = coded(modal_ref[2 * at:2 * at + half, :])
        high = coded(modal_ref[2 * at + half:2 * at + 2 * half, :])
        a_ref[at:at + half, :] = jnp.where(even, high, low)
        b_ref[at:at + half, :] = jnp.where(even, low, high)


def modal_product(increments, projection):
    levels = increments.shape[0]
    depth = levels * ROWS
    flat = increments.reshape(depth, COLS)
    arrived = lax.ppermute(flat, "lev", [(0, 1), (1, 0)])
    width = 256
    grid = (COLS // width,)
    sizes = [groups * 8 * ROWS for groups in CHUNKS]
    column = lambda rows: pl.BlockSpec((rows, width), lambda c: (0, c))
    whole = lambda rows, cols: pl.BlockSpec((rows, cols), lambda c: (0, 0))
    made = pl.pallas_call(
        own_levels_kernel,
        grid=grid,
        in_specs=[whole(2 * levels, 2 * MODES), column(depth)],
        out_specs=[column(n) for n in sizes] + [whole(n, depth) for n in sizes],
        out_shape=[jax.ShapeDtypeStruct((n, COLS), f32) for n in sizes]
        + [jax.ShapeDtypeStruct((n, depth), bf16) for n in sizes],
        scratch_shapes=[pltpu.VMEM((n, depth), bf16) for n in sizes],
        compiler_params=limits(20),
        name="own_levels",
    )(projection.T, flat)
    out = []
    for part, n in enumerate(sizes):
        out.append(pl.pallas_call(
            other_levels_kernel,
            grid=grid,
            in_specs=[whole(n, depth), column(depth), column(n)],
            out_specs=[column(n), column(n // 2), column(n // 2)],
            out_shape=[
                jax.ShapeDtypeStruct((n, COLS), f32),
                jax.ShapeDtypeStruct((n // 2, COLS), bf16),
                jax.ShapeDtypeStruct((n // 2, COLS), bf16),
            ],
            compiler_params=limits(20),
            name="other_levels",
        )(made[len(sizes) + part], arrived, made[part]))
    return out


def is_inner(order, row):
    return order <= row < ROWS - order


INNER_SLOTS, OUTER_SLOTS = {}, {}
for order_ in range(STEPS + 1):
    for row_ in range(ROWS):
        slots_ = INNER_SLOTS if is_inner(order_, row_) else OUTER_SLOTS
        slots_[order_, row_] = len(slots_) * 8
INNER_ROWS, OUTER_ROWS = 8 * len(INNER_SLOTS), 8 * len(OUTER_SLOTS)


def registers(ref, lead, at):
    return [ref[lead, at:at + 8, b * LANES:(b + 1) * LANES] for b in range(BLOCKS)]


def keep(ref, lead, at, values):
    for b, value in enumerate(values):
        ref[lead, at:at + 8, b * LANES:(b + 1) * LANES] = value


class Stencil:
    def __init__(self):
        self.lane = lax.broadcasted_iota(jnp.int32, (8, LANES), 1)
        self.first = self.lane == 0
        self.last = self.lane == LANES - 1

    def beside(self, field):
        right = [pltpu.roll(v, 1, 1) for v in field]
        left = [pltpu.roll(v, LANES - 1, 1) for v in field]
        out = []
        for b in range(BLOCKS):
            lower = jnp.where(self.first, right[b - 1] if b else 0.0, right[b])
            upper = jnp.where(self.last, left[b + 1] if b + 1 < BLOCKS else 0.0, left[b])
            out.append(lower + upper)
        return out

    def next(self, above, here, below, older, factor):
        sides = self.beside(here)
        new = []
        for b in range(BLOCKS):
            value = ((above[b] + below[b]) + sides[b]) * factor
            new.append(value if older is None else value - older[b])
        return new


def total(values):
    while len(values) > 1:
        values = [values[i] + values[i + 1] for i in range(0, len(values), 2)]
    return values[0]


def product(left, right):
    return total([v * w for v, w in zip(left, right)])


def add_moments(moment_ref, sums, lane, group):
    packed = moment_ref[...]
    for index, value in sums.items():
        value = jnp.sum(value, axis=1, keepdims=True)
        packed = packed + jnp.where(lane == index * GROUPS + group, value, 0.0)
    moment_ref[...] = packed


def accumulate(sums, index, value):
    sums[index] = sums[index] + value if index in sums else value


def inner_kernel(*refs):
    modal_refs, (inner_ref, moment_ref) = refs[:-2], refs[-2:]
    step = pl.program_id(0)

    @pl.when(step == 0)
    def _():
        moment_ref[...] = jnp.zeros_like(moment_ref)

    start = 0
    for modal_ref, groups in zip(modal_refs, CHUNKS):
        @pl.when((step >= start) & (step < start + groups))
        def _():
            inner_ref[0, 0:8 * ROWS] = modal_ref[...]
        start += groups
    stencil = Stencil()

    def load(order, row):
        return registers(inner_ref, 0, INNER_SLOTS[order, row])

    sums = {}
    for row in range(ROWS):
        field = load(0, row)
        accumulate(sums, 0, product(field, field))
    for order in range(1, STEPS):
        above, here = load(order - 1, order - 1), load(order - 1, order)
        for row in range(order, ROWS - order):
            below = load(order - 1, row + 1)
            older = None if order == 1 else load(order - 2, row)
            new = stencil.next(above, here, below, older, 0.25 if order == 1 else 0.5)
            keep(inner_ref, 0, INNER_SLOTS[order, row], new)
            accumulate(sums, 2 * order, product(new, new))
            accumulate(sums, 2 * order - 1, product(new, here))
            above, here = here, below
    add_moments(moment_ref, sums, stencil.lane, step)


def inner_basis(modals):
    rows = 8 * ROWS
    starts = [sum(CHUNKS[:c]) for c in range(len(CHUNKS))]
    clamp = lambda s, n: (lambda g: (jnp.clip(g - s, 0, n - 1), 0))
    return pl.pallas_call(
        inner_kernel,
        grid=(GROUPS,),
        in_specs=[pl.BlockSpec((rows, COLS), clamp(s, n)) for s, n in zip(starts, CHUNKS)],
        out_specs=[
            pl.BlockSpec((1, INNER_ROWS, COLS), lambda g: (g, 0, 0)),
            pl.BlockSpec((8, LANES), lambda g: (0, 0)),
        ],
        out_shape=[
            jax.ShapeDtypeStruct((GROUPS, INNER_ROWS, COLS), f32),
            jax.ShapeDtypeStruct((8, LANES), f32),
        ],
        compiler_params=limits(16),
        name="inner",
    )(*modals)


def outer_kernel(start, inner_ref, a_ref, b_ref, known_ref, outer_ref, moment_ref, halo_ref):
    tile = lax.axis_index("tile")
    even = (tile & 1) == 0
    step = pl.program_id(0)

    @pl.when(step == 0)
    def _():
        moment_ref[...] = known_ref[...]

    for row in range(0, HALO, 2):
        part = slice(row * 8, row * 8 + 16)
        a = decoded(a_ref[part, :])
        b = decoded(b_ref[part, :])
        halo_ref[0, part, :] = jnp.where(even, b, a)
        halo_ref[3, part, :] = jnp.where(even, a, b)
    stencil = Stencil()
    half_low = jnp.where(tile == 0, 0.0, 0.5)
    half_high = jnp.where(tile == TILES - 1, 0.0, 0.5)

    def place(order, row):
        if row < 0:
            return halo_ref, order % 3, (row + HALO) * 8
        if row >= ROWS:
            return halo_ref, 3 + order % 3, (row - ROWS) * 8
        if is_inner(order, row):
            return inner_ref, 0, INNER_SLOTS[order, row]
        return outer_ref, 0, OUTER_SLOTS[order, row]

    def load(order, row):
        return registers(*place(order, row))

    sums = {}
    for order in range(1, STEPS + 1):
        for begin, end in ((order - HALO, order), (ROWS - order, ROWS + HALO - order)):
            above, here = load(order - 1, begin - 1), load(order - 1, begin)
            for row in range(begin, end):
                below = load(order - 1, row + 1)
                own = 0 <= row < ROWS
                factor = 0.5 if own else half_low if row < 0 else half_high
                older = None
                if order == 1:
                    factor = factor * 0.5
                else:
                    older = load(order - 2, row)
                new = stencil.next(above, here, below, older, factor)
                keep(*place(order, row), new)
                if own:
                    accumulate(sums, 2 * order, product(new, new))
                    accumulate(sums, 2 * order - 1, product(new, here))
                above, here = here, below
    add_moments(moment_ref, sums, stencil.lane, step + start)


def outer_basis(inner, a, b, known, start, groups):
    halo = 8 * HALO
    return pl.pallas_call(
        functools.partial(outer_kernel, start),
        grid=(groups,),
        in_specs=[
            pl.BlockSpec((1, INNER_ROWS, COLS), lambda g: (g + start, 0, 0)),
            pl.BlockSpec((halo, COLS), lambda g: (g, 0)),
            pl.BlockSpec((halo, COLS), lambda g: (g, 0)),
            pl.BlockSpec((8, LANES), lambda g: (0, 0)),
        ],
        out_specs=[
            pl.BlockSpec((1, OUTER_ROWS, COLS), lambda g: (g, 0, 0)),
            pl.BlockSpec((8, LANES), lambda g: (0, 0)),
        ],
        out_shape=[
            jax.ShapeDtypeStruct((groups, OUTER_ROWS, COLS), f32),
            jax.ShapeDtypeStruct((8, LANES), f32),
        ],
        scratch_shapes=[pltpu.VMEM((6, halo, COLS), f32)],
        compiler_params=limits(16),
        name="outer",
    )(inner, a, b, known)


def coefficients(nu, tau):
    half = 0.5 * tau
    rho = list(nu)
    pi = list(nu)
    one, zero = jnp.ones_like(tau), None
    r = [one]
    p = [one]
    x = [None] * STEPS
    rr = nu[0]

    def plus(a, b):
        if a is None:
            return b
        if b is None:
            return a
        return a + b

    def inner(c, v):
        terms = [ci * vi for ci, vi in zip(c, v)]
        while len(terms) > 1:
            terms = [sum(terms[i:i + 2]) for i in range(0, len(terms), 2)]
        return terms[0]

    for step in range(STEPS):
        top = MOMENTS - 1 - step
        image = []
        for l in range(top):
            near = pi[l + 1] + pi[abs(l - 1)]
            image.append(pi[l] - half * near)
        alpha = rr / inner(p, image)
        x = [plus(x[i], alpha * p[i]) if i < len(p) else x[i] for i in range(STEPS)]
        shifted = [None] * (len(p) + 1)
        for k, value in enumerate(p):
            if k == 0:
                shifted[1] = plus(shifted[1], tau * value)
            else:
                scaled = half * value
                shifted[k + 1] = plus(shifted[k + 1], scaled)
                shifted[k - 1] = plus(shifted[k - 1], scaled)
        moved = []
        for k in range(len(p) + 1):
            own = p[k] if k < len(p) else None
            if shifted[k] is None:
                moved.append(own)
            elif own is None:
                moved.append(-shifted[k])
            else:
                moved.append(own - shifted[k])
        r = [
            (r[k] - alpha * moved[k]) if k < len(r) else -(alpha * moved[k])
            for k in range(len(moved))
        ]
        if step == STEPS - 1:
            break
        rho = [rho[l] - alpha * image[l] for l in range(top)]
        fresh = inner(r, rho)
        beta = fresh / rr
        pi = [rho[l] + beta * pi[l] for l in range(top)]
        p = [plus(r[k], beta * p[k] if k < len(p) else None) for k in range(len(r))]
        rr = fresh
    return x, r


def solve_kernel(sums_ref, helm_ref, inner_ref, *refs):
    outer_refs, (x_ref, r_ref, coef_ref) = refs[:-3], refs[-3:]
    group = pl.program_id(0)

    @pl.when(group == 0)
    def _():
        lane = lax.broadcasted_iota(jnp.int32, (8, LANES), 1)
        sub = lax.broadcasted_iota(jnp.int32, (8, LANES), 0)
        moments = sums_ref[...]
        raw = [moments if k == 0 else pltpu.roll(moments, LANES - GROUPS * k, 1) for k in range(MOMENTS)]
        nu = raw[:2]
        for k in range(2, MOMENTS):
            nu.append(2.0 * raw[k] - nu[k & 1])
        given = jnp.broadcast_to(helm_ref[...], (8, LANES))
        helm = jnp.zeros((8, LANES), f32)
        for g in range(GROUPS):
            value = jnp.sum(jnp.where(lane == sub + 8 * g, given, 0.0), axis=1, keepdims=True)
            helm = jnp.where(lane == g, value, helm)
        x, r = coefficients(nu, 4.0 / (4.0 + helm))
        for g in range(GROUPS):
            for k, value in enumerate(x + r):
                coef_ref[g, k] = jnp.broadcast_to(value[:, g:g + 1], (8, LANES))

    def combine(outer_ref):
        cx = [coef_ref[group, k] for k in range(STEPS)]
        cr = [coef_ref[group, STEPS + k] for k in range(STEPS + 1)]
        for b in range(BLOCKS):
            cols = slice(b * LANES, (b + 1) * LANES)
            for top in range(0, ROWS, 8):
                xs, rs = [], []
                for row in range(top, top + 8):
                    x = r = None
                    for k in range(STEPS + 1):
                        if is_inner(k, row):
                            at = INNER_SLOTS[k, row]
                            field = inner_ref[0, at:at + 8, cols]
                        else:
                            at = OUTER_SLOTS[k, row]
                            field = outer_ref[0, at:at + 8, cols]
                        if k < STEPS:
                            x = cx[k] * field if x is None else x + cx[k] * field
                        r = cr[k] * field if r is None else r + cr[k] * field
                    xs.append(x)
                    rs.append(r)
                x_ref[:, top:top + 8, cols] = jnp.swapaxes(jnp.stack(xs), 0, 1)
                r_ref[:, top:top + 8, cols] = jnp.swapaxes(jnp.stack(rs), 0, 1)

    start = 0
    for outer_ref, groups in zip(outer_refs, CHUNKS):
        pl.when((group >= start) & (group < start + groups))(
            functools.partial(combine, outer_ref)
        )
        start += groups


def solve(sums, helm, inner, outers):
    starts = [sum(CHUNKS[:c]) for c in range(len(CHUNKS))]
    clamp = lambda s, n: (lambda g: (jnp.clip(g - s, 0, n - 1), 0, 0))
    out = jax.ShapeDtypeStruct((MODES, ROWS, COLS), f32)
    return pl.pallas_call(
        solve_kernel,
        grid=(GROUPS,),
        in_specs=[
            pl.BlockSpec((8, LANES), lambda g: (0, 0)),
            pl.BlockSpec((1, LANES), lambda g: (0, 0)),
            pl.BlockSpec((1, INNER_ROWS, COLS), lambda g: (g, 0, 0)),
        ]
        + [pl.BlockSpec((1, OUTER_ROWS, COLS), clamp(s, n)) for s, n in zip(starts, CHUNKS)],
        out_specs=[
            pl.BlockSpec((8, ROWS, COLS), lambda g: (g, 0, 0)),
            pl.BlockSpec((8, ROWS, COLS), lambda g: (g, 0, 0)),
        ],
        out_shape=[out, out],
        scratch_shapes=[pltpu.VMEM((GROUPS, MOMENTS, 8, LANES), f32)],
        compiler_params=limits(16),
        name="solve",
    )(sums, helm, inner, *outers)


def of_everyone(value):
    for mask in (1, 3, 4, 12, 16, 48):
        value = value + lax.ppermute(value, "tile", [(i, i ^ mask) for i in range(TILES)])
    return value


def shards(increments, projection, helmholtz):
    swap_a = [(i, i ^ 1) for i in range(TILES)]
    swap_b = [(i, i + 1) for i in range(1, TILES - 1, 2)]
    swap_b += [(target, source) for source, target in swap_b]
    modals, halos = [], []
    for modal, a, b in modal_product(increments, projection):
        modals.append(modal)
        halos.append((lax.ppermute(a, "tile", swap_a), lax.ppermute(b, "tile", swap_b)))
    inner, moments = inner_basis(modals)
    outers = []
    for part, (a, b) in enumerate(halos):
        outer, moments = outer_basis(inner, a, b, moments, sum(CHUNKS[:part]), CHUNKS[part])
        outers.append(outer)
    helm = jnp.pad(helmholtz[None], ((0, 0), (0, LANES - MODES)))
    return tuple(solve(of_everyone(moments), helm, inner, outers))


def solution(mesh):
    in_specs = (P("lev", "tile", None), P(), P("lev"))
    out_specs = (P("lev", "tile", None), P("lev", "tile", None))
    return jax.shard_map(shards, mesh=mesh, in_specs=in_specs, out_specs=out_specs, check_vma=False)
```

time: 153 us -> 74.7 us (0.49)
  Pallas kernels: 86.3 us -> 33.2 us
  local copies, waits for them, and re-layouts: 20.3 us -> 2.39 us
  waiting for transfers between devices: 25 us -> 9.62 us
  starting transfers between devices: 20.5 us -> 28.2 us
    pallas_call x4 -> x7, Pallas kernels: 86.3 us -> 33.2 us  [the longest x2 12.7 us: outer_basis(): pl.pallas_call(functools.partial(outer_kernel, start), grid=(groups,), in...]
    ppermute x2 -> x10, starting transfers between devices: 2.46 us -> 28.1 us  [the longest x6 20.8 us: of_everyone(): lax.ppermute(value, 'tile', [(i, i ^ mask) for i in range(TILES)])]
    all_to_all x1 -> x0, starting transfers between devices: 17.9 us -> none  [shards(): sums = lax.all_to_all(spread, 'tile', 0, 0, tiled=True)]
    unnamed x13 -> x6, local copies, waits for them, and re-layouts: 19.4 us -> 2.39 us
    all_to_all x1 -> x0, waiting for transfers between devices: 10.2 us -> none  [shards(): sums = lax.all_to_all(spread, 'tile', 0, 0, tiled=True)]
    ppermute x2 -> x10, waiting for transfers between devices: 14.7 us -> 9.62 us  [the longest x6 9.61 us: of_everyone(): lax.ppermute(value, 'tile', [(i, i ^ mask) for i in range(TILES)])]
  transfers between devices with their start and end apart: 4 -> 11, of which waited for: 2 -> 6; matrix products, arithmetic and copies ran while one was open for 1% -> 0% of each run, Pallas kernels for 2% -> 26%
where the time goes in v1:
time: 74.7 us; the launch traced here: 74.1 us
  Pallas kernels  33.2 us (44%)
  starting transfers between devices  28.2 us (38%)
  waiting for transfers between devices  9.62 us (13%)
  local copies, waits for them, and re-layouts  2.39 us (3%)
    ppermute x6, starting transfers between devices, of_everyone(): lax.ppermute(value, 'tile', [(i, i ^ mask) for i in range(TILES)])  20.8 us
    pallas_call x2, Pallas kernels, outer_basis(): pl.pallas_call(functools.partial(outer_kernel, start), grid=(groups,), in...  12.7 us
    ppermute x6, waiting for transfers between devices, of_everyone(): lax.ppermute(value, 'tile', [(i, i ^ mask) for i in range(TILES)])  9.61 us
    pallas_call x1, Pallas kernels, solve(): pl.pallas_call(solve_kernel, grid=(GROUPS,), in_specs=[pl.BlockSpec((8, L...  6.13 us
    ppermute x2, starting transfers between devices, shards(): lax.ppermute(a, 'tile', swap_a)  5.93 us
    pallas_call x1, Pallas kernels, inner_basis(): pl.pallas_call(inner_kernel, grid=(GROUPS,), in_specs=[pl.BlockSpec((rows...  5.92 us
    pallas_call x2, Pallas kernels, modal_product(): pl.pallas_call(other_levels_kernel, grid=grid, in_specs=[whole(n, depth),...  4.77 us
    pallas_call x1, Pallas kernels, modal_product(): pl.pallas_call(own_levels_kernel, grid=grid, in_specs=[whole(2 * levels,...  3.69 us
  transfers between devices with their start and end apart: 11, of which 6 were waited for; matrix products, arithmetic and copies ran while one was open for 0% of the time, Pallas kernels for 26%

profile of v1, /device:TPU:0, one launch (start us, length us, event | category | flops | bytes accessed | tf_op | source)
XLA Modules:
  0.0 74.1 jit_solution(10778821595501540391)
XLA Ops:
  0.6 0.1 collective-permute-start
  0.7 0.0 copy-start
  0.7 1.6 %copy-done = bf16[68,16,1024]{2,1,0:T(8,128)(2,1)S(1)} copy-done((bf16[68,16,1024]{2,1,0:T(8,128)(2,1)S(1)}, bf16[68,16,1024]{2,1,0:T(8,128)(2,1)}, u32[]{:S(2)}) %copy-start) | copy-done | bytes 2228248
  2.4 0.0 copy-start.1
  2.4 0.8 %copy-done.1 = bf16[80,136]{0,1:T(8,128)(2,1)S(1)} copy-done((bf16[80,136]{0,1:T(8,128)(2,1)S(1)}, bf16[80,136]{0,1:T(8,128)(2,1)}, u32[]{:S(2)}) %copy-start.1) | copy-done | bytes 21784
  3.1 3.7 %own_levels.1 = (f32[384,1024]{1,0:T(8,128)S(1)}, f32[256,1024]{1,0:T(8,128)S(1)}, bf16[384,1088]{1,0:T(8,128)(2,1)S(1)}, bf16[256,1088]{1,0:T(8,128)(2,1)S(1)}) custom-call(bf16[136,80]{1,0:T(8,128)(2,1)S(1)} %bitcast.5, bf16[1088,1024]{1,0:T(8,128)(2,1)S(1)} %bitcast.4), custom_call_target="tpu_custom_call" | custom-call | tf_op jit(solution)/shard_map/own_levels/pallas_call | solution.py:113
  6.8 0.0 collective-permute-done.inc_ref
  6.8 2.7 %other_levels.2 = (f32[384,1024]{1,0:T(8,128)S(1)}, bf16[192,1024]{1,0:T(8,128)(2,1)S(1)}, bf16[192,1024]{1,0:T(8,128)(2,1)S(1)}) custom-call(bf16[384,1088]{1,0:T(8,128)(2,1)S(1)} %get-tuple-element.18.left_ref, bf16[1088,1024]{1,0:T(8,128)(2,1)S(1)} %collective-permute-done.inc_ref, f32[384,1024]{1,0:T(8,128)S(1)} %get-tuple-element.19.acc_ref), custom_call_target="tpu_custom_call" | custom-call | tf_op jit(solution)/shard_map/other_levels/pallas_call | solution.py:126
  9.5 1.8 %collective-permute-start.3 = (bf16[192,1024]{1,0:T(8,128)(2,1)S(1)}, bf16[192,1024]{1,0:T(8,128)(2,1)S(1)}, u32[]{:S(2)}, u32[]{:S(2)}) collective-permute-start(bf16[192,1024]{1,0:T(8,128)(2,1)S(1)} %get-tuple-element.27), channel_id=1, source_target_pairs={{0,2},{2,0},{4,6},{6,4},{8,10},{10,8},{12,14},{14,12},{16,18},{18,... | collective-permute-start | bytes 1179656 | tf_op jit(solution)/shard_map/ppermute | solution.py:500
  11.3 0.7 collective-permute-start.4
  11.9 2.1 %other_levels.3 = (f32[256,1024]{1,0:T(8,128)S(1)}, bf16[128,1024]{1,0:T(8,128)(2,1)S(1)}, bf16[128,1024]{1,0:T(8,128)(2,1)S(1)}) custom-call(bf16[256,1088]{1,0:T(8,128)(2,1)S(1)} %get-tuple-element.21.left_ref, bf16[1088,1024]{1,0:T(8,128)(2,1)S(1)} %collective-permute-done.inc_ref, f32[256,1024]{1,0:T(8,128)S(1)} %get-tuple-element.22.acc_ref), custom_call_target="tpu_custom_call" | custom-call | tf_op jit(solution)/shard_map/other_levels/pallas_call | solution.py:126
  14.1 4.2 %collective-permute-start.1 = (bf16[128,1024]{1,0:T(8,128)(2,1)S(1)}, bf16[128,1024]{1,0:T(8,128)(2,1)S(1)}, u32[]{:S(2)}, u32[]{:S(2)}) collective-permute-start(bf16[128,1024]{1,0:T(8,128)(2,1)S(1)} %get-tuple-element.25), channel_id=1, source_target_pairs={{0,2},{2,0},{4,6},{6,4},{8,10},{10,8},{12,14},{14,12},{16,18},{18,... | collective-permute-start | bytes 786440 | tf_op jit(solution)/shard_map/ppermute | solution.py:500
  18.2 0.7 collective-permute-start.2
  18.9 5.9 %inner.1 = (f32[5,576,1024]{2,1,0:T(8,128)S(1)}, f32[8,128]{1,0:T(8,128)S(1)}) custom-call(f32[384,1024]{1,0:T(8,128)S(1)} %get-tuple-element.20.refs_0_, f32[256,1024]{1,0:T(8,128)S(1)} %get-tuple-element.23.refs_1_), custom_call_target="tpu_custom_call" | custom-call | tf_op jit(solution)/shard_map/inner/pallas_call | solution.py:250
  24.8 0.0 collective-permute-done.3.a_ref
  24.8 0.0 collective-permute-done.4.b_ref
  24.8 7.6 %outer.2 = (f32[3,576,1024]{2,1,0:T(8,128)S(1)}, f32[8,128]{1,0:T(8,128)S(1)}) custom-call(f32[5,576,1024]{2,1,0:T(8,128)S(1)} %get-tuple-element.24.inner_ref, bf16[192,1024]{1,0:T(8,128)(2,1)S(1)} %collective-permute-done.3.a_ref, bf16[192,1024]{1,0:T(8,128)(2,1)S(1)} %collective-permute-done.4.b_ref, f32[8,128]{1,0:T(8,128)S(1)} %get-tuple-element.29.known_ref), custom_call_target="tpu_custom_call" | custom-call | tf_op jit(solution)/shard_map/outer/pallas_call | solution.py:322
  32.4 0.0 collective-permute-done.1.a_ref
  32.4 0.0 collective-permute-done.2.b_ref
  32.4 0.0 copy-start.2
  32.4 5.1 %outer.3 = (f32[2,576,1024]{2,1,0:T(8,128)S(1)}, f32[8,128]{1,0:T(8,128)S(1)}) custom-call(f32[5,576,1024]{2,1,0:T(8,128)S(1)} %get-tuple-element.24.inner_ref, bf16[128,1024]{1,0:T(8,128)(2,1)S(1)} %collective-permute-done.1.a_ref, bf16[128,1024]{1,0:T(8,128)(2,1)S(1)} %collective-permute-done.2.b_ref, f32[8,128]{1,0:T(8,128)S(1)} %get-tuple-element.30.known_ref), custom_call_target="tpu_custom_call" | custom-call | tf_op jit(solution)/shard_map/outer/pallas_call | solution.py:322
  37.5 4.4 %collective-permute-start.5 = (f32[8,128]{1,0:T(8,128)S(1)}, f32[8,128]{1,0:T(8,128)S(1)}, u32[]{:S(2)}, u32[]{:S(2)}) collective-permute-start(f32[8,128]{1,0:T(8,128)S(1)} %get-tuple-element.31), channel_id=1, source_target_pairs={{0,2},{2,0},{4,6},{6,4},{8,10},{10,8},{12,14},{14,12},{16,18},{18,... | collective-permute-start | bytes 12296 | tf_op jit(solution)/shard_map/ppermute | solution.py:489
  41.9 1.6 %collective-permute-done.5 = f32[8,128]{1,0:T(8,128)S(1)} collective-permute-done((f32[8,128]{1,0:T(8,128)S(1)}, f32[8,128]{1,0:T(8,128)S(1)}, u32[]{:S(2)}, u32[]{:S(2)}) %collective-permute-start.5) | collective-permute-done | bytes 4128 | tf_op jit(solution)/shard_map/ppermute | solution.py:489
  43.5 3.5 %collective-permute-start.6 = (f32[8,128]{1,0:T(8,128)S(1)}, f32[8,128]{1,0:T(8,128)S(1)}, u32[]{:S(2)}, u32[]{:S(2)}) collective-permute-start(f32[8,128]{1,0:T(8,128)S(1)} %add.20), channel_id=1, source_target_pairs={{0,6},{2,4},{4,2},{6,0},{8,14},{10,12},{12,10},{14,8},{16,22},{18,... | collective-permute-start | bytes 12296 | tf_op jit(solution)/shard_map/ppermute | solution.py:489
  47.0 1.6 %collective-permute-done.6 = f32[8,128]{1,0:T(8,128)S(1)} collective-permute-done((f32[8,128]{1,0:T(8,128)S(1)}, f32[8,128]{1,0:T(8,128)S(1)}, u32[]{:S(2)}, u32[]{:S(2)}) %collective-permute-start.6) | collective-permute-done | bytes 4128 | tf_op jit(solution)/shard_map/ppermute | solution.py:489
  48.6 1.9 %collective-permute-start.7 = (f32[8,128]{1,0:T(8,128)S(1)}, f32[8,128]{1,0:T(8,128)S(1)}, u32[]{:S(2)}, u32[]{:S(2)}) collective-permute-start(f32[8,128]{1,0:T(8,128)S(1)} %add.21), channel_id=1, source_target_pairs={{0,8},{2,10},{4,12},{6,14},{8,0},{10,2},{12,4},{14,6},{16,24},{18,... | collective-permute-start | bytes 12296 | tf_op jit(solution)/shard_map/ppermute | solution.py:489
  50.5 1.7 %collective-permute-done.7 = f32[8,128]{1,0:T(8,128)S(1)} collective-permute-done((f32[8,128]{1,0:T(8,128)S(1)}, f32[8,128]{1,0:T(8,128)S(1)}, u32[]{:S(2)}, u32[]{:S(2)}) %collective-permute-start.7) | collective-permute-done | bytes 4128 | tf_op jit(solution)/shard_map/ppermute | solution.py:489
  52.2 5.0 %collective-permute-start.8 = (f32[8,128]{1,0:T(8,128)S(1)}, f32[8,128]{1,0:T(8,128)S(1)}, u32[]{:S(2)}, u32[]{:S(2)}) collective-permute-start(f32[8,128]{1,0:T(8,128)S(1)} %add.22), channel_id=1, source_target_pairs={{0,24},{2,26},{4,28},{6,30},{8,16},{10,18},{12,20},{14,22},{16,8},... | collective-permute-start | bytes 12296 | tf_op jit(solution)/shard_map/ppermute | solution.py:489
  57.2 1.6 %collective-permute-done.8 = f32[8,128]{1,0:T(8,128)S(1)} collective-permute-done((f32[8,128]{1,0:T(8,128)S(1)}, f32[8,128]{1,0:T(8,128)S(1)}, u32[]{:S(2)}, u32[]{:S(2)}) %collective-permute-start.8) | collective-permute-done | bytes 4128 | tf_op jit(solution)/shard_map/ppermute | solution.py:489
  58.8 2.4 %collective-permute-start.9 = (f32[8,128]{1,0:T(8,128)S(1)}, f32[8,128]{1,0:T(8,128)S(1)}, u32[]{:S(2)}, u32[]{:S(2)}) collective-permute-start(f32[8,128]{1,0:T(8,128)S(1)} %add.23), channel_id=1, source_target_pairs={{0,32},{2,34},{4,36},{6,38},{8,40},{10,42},{12,44},{14,46},{16,48}... | collective-permute-start | bytes 12296 | tf_op jit(solution)/shard_map/ppermute | solution.py:489
  61.2 1.6 %collective-permute-done.9 = f32[8,128]{1,0:T(8,128)S(1)} collective-permute-done((f32[8,128]{1,0:T(8,128)S(1)}, f32[8,128]{1,0:T(8,128)S(1)}, u32[]{:S(2)}, u32[]{:S(2)}) %collective-permute-start.9) | collective-permute-done | bytes 4128 | tf_op jit(solution)/shard_map/ppermute | solution.py:489
  62.8 3.6 %collective-permute-start.10 = (f32[8,128]{1,0:T(8,128)S(1)}, f32[8,128]{1,0:T(8,128)S(1)}, u32[]{:S(2)}, u32[]{:S(2)}) collective-permute-start(f32[8,128]{1,0:T(8,128)S(1)} %add.24), channel_id=1, source_target_pairs={{0,96},{2,98},{4,100},{6,102},{8,104},{10,106},{12,108},{14,110},{... | collective-permute-start | bytes 12296 | tf_op jit(solution)/shard_map/ppermute | solution.py:489
  66.4 0.0 copy-done.2
  66.4 1.6 %collective-permute-done.10 = f32[8,128]{1,0:T(8,128)S(1)} collective-permute-done((f32[8,128]{1,0:T(8,128)S(1)}, f32[8,128]{1,0:T(8,128)S(1)}, u32[]{:S(2)}, u32[]{:S(2)}) %collective-permute-start.10) | collective-permute-done | bytes 4128 | tf_op jit(solution)/shard_map/ppermute | solution.py:489
  68.0 6.1 %solve.1 = (f32[40,16,1024]{2,1,0:T(8,128)}, f32[40,16,1024]{2,1,0:T(8,128)}) custom-call(f32[8,128]{1,0:T(8,128)S(1)} %add.25.sums_ref, f32[1,128]{1,0:T(1,128)S(1)} %pad.4.helm_ref, f32[5,576,1024]{2,1,0:T(8,128)S(1)} %get-tuple-element.24.inner_ref, f32[3,576,1024]{2,1,0:T(8,128)S(1)} %get-tuple-element.32.refs_0_, ...), custom_call_target="tpu_custom_call" | custom-call | tf_op jit(solution)/shard_map/solve/pallas_call | solution.py:467
  (7 shorter events, 0.0 us)
Async XLA Ops:
  0.6 6.2 %collective-permute-start = (bf16[1088,1024]{1,0:T(8,128)(2,1)}, bf16[1088,1024]{1,0:T(8,128)(2,1)S(1)}, u32[]{:S(2)}, u32[]{:S(2)}) collective-permute-start(bf16[1088,1024]{1,0:T(8,128)(2,1)} %bitcast.3), channel_id=1, source_target_pairs={{0,1},{1,0},{2,3},{3,2},{4,5},{5,4},{6,7},{7,6},{8,9},{9,8},{10,11... | collective-permute-start | bytes 6684680 | tf_op jit(solution)/shard_map/ppermute | solution.py:107
  0.7 1.6 %copy-start = (bf16[68,16,1024]{2,1,0:T(8,128)(2,1)S(1)}, bf16[68,16,1024]{2,1,0:T(8,128)(2,1)}, u32[]{:S(2)}) copy-start(bf16[68,16,1024]{2,1,0:T(8,128)(2,1)} %param.3) | copy-start | bytes 6684676
  2.4 0.8 %copy-start.1 = (bf16[80,136]{0,1:T(8,128)(2,1)S(1)}, bf16[80,136]{0,1:T(8,128)(2,1)}, u32[]{:S(2)}) copy-start(bf16[80,136]{0,1:T(8,128)(2,1)} %param.4) | copy-start | bytes 65284
  9.5 15.3 %collective-permute-start.3 = (bf16[192,1024]{1,0:T(8,128)(2,1)S(1)}, bf16[192,1024]{1,0:T(8,128)(2,1)S(1)}, u32[]{:S(2)}, u32[]{:S(2)}) collective-permute-start(bf16[192,1024]{1,0:T(8,128)(2,1)S(1)} %get-tuple-element.27), channel_id=1, source_target_pairs={{0,2},{2,0},{4,6},{6,4},{8,10},{10,8},{12,14},{14,12},{16,18},{18,... | collective-permute-start | bytes 1179656 | tf_op jit(solution)/shard_map/ppermute | solution.py:500
  11.3 13.6 %collective-permute-start.4 = (bf16[192,1024]{1,0:T(8,128)(2,1)S(1)}, bf16[192,1024]{1,0:T(8,128)(2,1)S(1)}, u32[]{:S(2)}, u32[]{:S(2)}) collective-permute-start(bf16[192,1024]{1,0:T(8,128)(2,1)S(1)} %get-tuple-element.28), channel_id=1, source_target_pairs={{2,4},{6,8},{10,12},{14,16},{18,20},{22,24},{26,28},{30,32},{34,36... | collective-permute-start | bytes 1179656 | tf_op jit(solution)/shard_map/ppermute | solution.py:500
  14.1 18.4 %collective-permute-start.1 = (bf16[128,1024]{1,0:T(8,128)(2,1)S(1)}, bf16[128,1024]{1,0:T(8,128)(2,1)S(1)}, u32[]{:S(2)}, u32[]{:S(2)}) collective-permute-start(bf16[128,1024]{1,0:T(8,128)(2,1)S(1)} %get-tuple-element.25), channel_id=1, source_target_pairs={{0,2},{2,0},{4,6},{6,4},{8,10},{10,8},{12,14},{14,12},{16,18},{18,... | collective-permute-start | bytes 786440 | tf_op jit(solution)/shard_map/ppermute | solution.py:500
  18.2 14.2 %collective-permute-start.2 = (bf16[128,1024]{1,0:T(8,128)(2,1)S(1)}, bf16[128,1024]{1,0:T(8,128)(2,1)S(1)}, u32[]{:S(2)}, u32[]{:S(2)}) collective-permute-start(bf16[128,1024]{1,0:T(8,128)(2,1)S(1)} %get-tuple-element.26), channel_id=1, source_target_pairs={{2,4},{6,8},{10,12},{14,16},{18,20},{22,24},{26,28},{30,32},{34,36... | collective-permute-start | bytes 786440 | tf_op jit(solution)/shard_map/ppermute | solution.py:500
  32.4 34.0 %copy-start.2 = (f32[40]{0:T(128)S(1)}, f32[40]{0:T(128)}, u32[]{:S(2)}) copy-start(f32[40]{0:T(128)} %param.5) | copy-start | bytes 484
  37.5 6.0 %collective-permute-start.5 = (f32[8,128]{1,0:T(8,128)S(1)}, f32[8,128]{1,0:T(8,128)S(1)}, u32[]{:S(2)}, u32[]{:S(2)}) collective-permute-start(f32[8,128]{1,0:T(8,128)S(1)} %get-tuple-element.31), channel_id=1, source_target_pairs={{0,2},{2,0},{4,6},{6,4},{8,10},{10,8},{12,14},{14,12},{16,18},{18,... | collective-permute-start | bytes 12296 | tf_op jit(solution)/shard_map/ppermute | solution.py:489
  43.5 5.0 %collective-permute-start.6 = (f32[8,128]{1,0:T(8,128)S(1)}, f32[8,128]{1,0:T(8,128)S(1)}, u32[]{:S(2)}, u32[]{:S(2)}) collective-permute-start(f32[8,128]{1,0:T(8,128)S(1)} %add.20), channel_id=1, source_target_pairs={{0,6},{2,4},{4,2},{6,0},{8,14},{10,12},{12,10},{14,8},{16,22},{18,... | collective-permute-start | bytes 12296 | tf_op jit(solution)/shard_map/ppermute | solution.py:489
  48.6 3.6 %collective-permute-start.7 = (f32[8,128]{1,0:T(8,128)S(1)}, f32[8,128]{1,0:T(8,128)S(1)}, u32[]{:S(2)}, u32[]{:S(2)}) collective-permute-start(f32[8,128]{1,0:T(8,128)S(1)} %add.21), channel_id=1, source_target_pairs={{0,8},{2,10},{4,12},{6,14},{8,0},{10,2},{12,4},{14,6},{16,24},{18,... | collective-permute-start | bytes 12296 | tf_op jit(solution)/shard_map/ppermute | solution.py:489
  52.2 6.6 %collective-permute-start.8 = (f32[8,128]{1,0:T(8,128)S(1)}, f32[8,128]{1,0:T(8,128)S(1)}, u32[]{:S(2)}, u32[]{:S(2)}) collective-permute-start(f32[8,128]{1,0:T(8,128)S(1)} %add.22), channel_id=1, source_target_pairs={{0,24},{2,26},{4,28},{6,30},{8,16},{10,18},{12,20},{14,22},{16,8},... | collective-permute-start | bytes 12296 | tf_op jit(solution)/shard_map/ppermute | solution.py:489
  58.8 4.0 %collective-permute-start.9 = (f32[8,128]{1,0:T(8,128)S(1)}, f32[8,128]{1,0:T(8,128)S(1)}, u32[]{:S(2)}, u32[]{:S(2)}) collective-permute-start(f32[8,128]{1,0:T(8,128)S(1)} %add.23), channel_id=1, source_target_pairs={{0,32},{2,34},{4,36},{6,38},{8,40},{10,42},{12,44},{14,46},{16,48}... | collective-permute-start | bytes 12296 | tf_op jit(solution)/shard_map/ppermute | solution.py:489
  62.8 5.2 %collective-permute-start.10 = (f32[8,128]{1,0:T(8,128)S(1)}, f32[8,128]{1,0:T(8,128)S(1)}, u32[]{:S(2)}, u32[]{:S(2)}) collective-permute-start(f32[8,128]{1,0:T(8,128)S(1)} %add.24), channel_id=1, source_target_pairs={{0,96},{2,98},{4,100},{6,102},{8,104},{10,106},{12,108},{14,110},{... | collective-permute-start | bytes 12296 | tf_op jit(solution)/shard_map/ppermute | solution.py:489

commit v2 on v1

--- a/solution.py
+++ b/solution.py
@@ -27,9 +27,9 @@
     return pltpu.CompilerParams(vmem_limit_bytes=mib * 2**20)
 
 
-def build_left(proj_ref, left_refs, level0):
+def build_left(proj_ref, left_ref, level0):
     lev = lax.axis_index("lev")
-    depth = left_refs[0].shape[1]
+    depth = left_ref.shape[1]
     pick = (
         lax.broadcasted_iota(jnp.int32, (MODES, 2 * MODES), 1)
         == lax.broadcasted_iota(jnp.int32, (MODES, 2 * MODES), 0) + lev * MODES
@@ -44,32 +44,27 @@
     ).astype(bf16)
     wide = jnp.dot(own, spread, preferred_element_type=f32)
     row_of = lax.broadcasted_iota(jnp.int32, (8, depth), 1) & (ROWS - 1)
-    group = 0
-    for ref in left_refs:
-        for at in range(0, ref.shape[0], 8 * ROWS):
-            part = wide[group * 8:(group + 1) * 8]
-            for row in range(0, ROWS, 2):
-                two = jnp.concatenate(
-                    [jnp.where(row_of == row, part, 0.0), jnp.where(row_of == row + 1, part, 0.0)],
-                    axis=0,
-                )
-                ref[at + row * 8:at + row * 8 + 16, :] = two.astype(bf16)
-            group += 1
-
-
-def own_levels_kernel(proj_ref, inc_ref, *refs):
+    for group in range(GROUPS):
+        part = wide[group * 8:(group + 1) * 8]
+        for row in range(0, ROWS, 2):
+            two = jnp.concatenate(
+                [jnp.where(row_of == row, part, 0.0), jnp.where(row_of == row + 1, part, 0.0)],
+                axis=0,
+            )
+            at = group * 8 * ROWS + row * 8
+            left_ref[at:at + 16, :] = two.astype(bf16)
+
+
+def own_levels_kernel(proj_ref, inc_ref, acc_ref, other_left_ref, left_ref):
     lev = lax.axis_index("lev")
     count = proj_ref.shape[0] // 2
-    parts = len(CHUNKS)
-    acc_refs, other_refs, left_refs = refs[:parts], refs[parts:2 * parts], refs[2 * parts:]
 
     @pl.when(pl.program_id(0) == 0)
     def _():
-        build_left(proj_ref, left_refs, lev * count)
-        build_left(proj_ref, other_refs, (1 - lev) * count)
-
-    for acc_ref, left_ref in zip(acc_refs, left_refs):
-        acc_ref[...] = jnp.dot(left_ref[...], inc_ref[...], preferred_element_type=f32)
+        build_left(proj_ref, left_ref, lev * count)
+        build_left(proj_ref, other_left_ref, (1 - lev) * count)
+
+    acc_ref[...] = jnp.dot(left_ref[...], inc_ref[...], preferred_element_type=f32)
 
 
 def coded(x):
@@ -87,17 +82,21 @@
     return jnp.where(y < 0.0, -root, root)
 
 
-def other_levels_kernel(left_ref, inc_ref, acc_ref, modal_ref, a_ref, b_ref):
+def other_levels_kernel(left_ref, inc_ref, acc_ref, modal_ref, *halo_refs):
     even = (lax.axis_index("tile") & 1) == 0
     modal_ref[...] = acc_ref[...] + jnp.dot(
         left_ref[...], inc_ref[...], preferred_element_type=f32
     )
     half = 8 * HALO
-    for at in range(0, a_ref.shape[0], half):
-        low = coded(modal_ref[2 * at:2 * at + half, :])
-        high = coded(modal_ref[2 * at + half:2 * at + 2 * half, :])
-        a_ref[at:at + half, :] = jnp.where(even, high, low)
-        b_ref[at:at + half, :] = jnp.where(even, low, high)
+    group = 0
+    for a_ref, b_ref in zip(halo_refs[::2], halo_refs[1::2]):
+        for at in range(0, a_ref.shape[0], half):
+            start = group * 2 * half
+            low = coded(modal_ref[start:start + half, :])
+            high = coded(modal_ref[start + half:start + 2 * half, :])
+            a_ref[at:at + half, :] = jnp.where(even, high, low)
+            b_ref[at:at + half, :] = jnp.where(even, low, high)
+            group += 1
 
 
 def modal_product(increments, projection):
@@ -107,36 +106,34 @@
     arrived = lax.ppermute(flat, "lev", [(0, 1), (1, 0)])
     width = 256
     grid = (COLS // width,)
-    sizes = [groups * 8 * ROWS for groups in CHUNKS]
+    count = MODES * ROWS
     column = lambda rows: pl.BlockSpec((rows, width), lambda c: (0, c))
     whole = lambda rows, cols: pl.BlockSpec((rows, cols), lambda c: (0, 0))
-    made = pl.pallas_call(
+    acc, other_left = pl.pallas_call(
         own_levels_kernel,
         grid=grid,
         in_specs=[whole(2 * levels, 2 * MODES), column(depth)],
-        out_specs=[column(n) for n in sizes] + [whole(n, depth) for n in sizes],
-        out_shape=[jax.ShapeDtypeStruct((n, COLS), f32) for n in sizes]
-        + [jax.ShapeDtypeStruct((n, depth), bf16) for n in sizes],
-        scratch_shapes=[pltpu.VMEM((n, depth), bf16) for n in sizes],
+        out_specs=[column(count), whole(count, depth)],
+        out_shape=[
+            jax.ShapeDtypeStruct((count, COLS), f32),
+            jax.ShapeDtypeStruct((count, depth), bf16),
+        ],
+        scratch_shapes=[pltpu.VMEM((count, depth), bf16)],
         compiler_params=limits(20),
         name="own_levels",
-    )(projection.T, flat)
-    out = []
-    for part, n in enumerate(sizes):
-        out.append(pl.pallas_call(
-            other_levels_kernel,
-            grid=grid,
-            in_specs=[whole(n, depth), column(depth), column(n)],
-            out_specs=[column(n), column(n // 2), column(n // 2)],
-            out_shape=[
-                jax.ShapeDtypeStruct((n, COLS), f32),
-                jax.ShapeDtypeStruct((n // 2, COLS), bf16),
-                jax.ShapeDtypeStruct((n // 2, COLS), bf16),
-            ],
-            compiler_params=limits(20),
-            name="other_levels",
-        )(made[len(sizes) + part], arrived, made[part]))
-    return out
+    )(projection.T, pltpu.with_memory_space_constraint(flat, pltpu.HBM))
+    halos = [8 * HALO * n for n in CHUNKS for _ in range(2)]
+    modal, *coded_rows = pl.pallas_call(
+        other_levels_kernel,
+        grid=grid,
+        in_specs=[whole(count, depth), column(depth), column(count)],
+        out_specs=[column(count)] + [column(n) for n in halos],
+        out_shape=[jax.ShapeDtypeStruct((count, COLS), f32)]
+        + [jax.ShapeDtypeStruct((n, COLS), bf16) for n in halos],
+        compiler_params=limits(20),
+        name="other_levels",
+    )(other_left, arrived, acc)
+    return modal, list(zip(coded_rows[::2], coded_rows[1::2]))
 
 
 def is_inner(order, row):
@@ -207,20 +204,14 @@
     sums[index] = sums[index] + value if index in sums else value
 
 
-def inner_kernel(*refs):
-    modal_refs, (inner_ref, moment_ref) = refs[:-2], refs[-2:]
+def inner_kernel(modal_ref, inner_ref, moment_ref):
     step = pl.program_id(0)
 
     @pl.when(step == 0)
     def _():
         moment_ref[...] = jnp.zeros_like(moment_ref)
 
-    start = 0
-    for modal_ref, groups in zip(modal_refs, CHUNKS):
-        @pl.when((step >= start) & (step < start + groups))
-        def _():
-            inner_ref[0, 0:8 * ROWS] = modal_ref[...]
-        start += groups
+    inner_ref[0, 0:8 * ROWS] = modal_ref[...]
     stencil = Stencil()
 
     def load(order, row):
@@ -243,14 +234,11 @@
     add_moments(moment_ref, sums, stencil.lane, step)
 
 
-def inner_basis(modals):
-    rows = 8 * ROWS
-    starts = [sum(CHUNKS[:c]) for c in range(len(CHUNKS))]
-    clamp = lambda s, n: (lambda g: (jnp.clip(g - s, 0, n - 1), 0))
+def inner_basis(modal):
     return pl.pallas_call(
         inner_kernel,
         grid=(GROUPS,),
-        in_specs=[pl.BlockSpec((rows, COLS), clamp(s, n)) for s, n in zip(starts, CHUNKS)],
+        in_specs=[pl.BlockSpec((8 * ROWS, COLS), lambda g: (g, 0))],
         out_specs=[
             pl.BlockSpec((1, INNER_ROWS, COLS), lambda g: (g, 0, 0)),
             pl.BlockSpec((8, LANES), lambda g: (0, 0)),
@@ -261,7 +249,7 @@
         ],
         compiler_params=limits(16),
         name="inner",
-    )(*modals)
+    )(modal)
 
 
 def outer_kernel(start, inner_ref, a_ref, b_ref, known_ref, outer_ref, moment_ref, halo_ref):
@@ -485,8 +473,12 @@
 
 
 def of_everyone(value):
-    for mask in (1, 3, 4, 12, 16, 48):
-        value = value + lax.ppermute(value, "tile", [(i, i ^ mask) for i in range(TILES)])
+    for stride in (1, 4, 16):
+        one, three, two = [
+            lax.ppermute(value, "tile", [(i, i ^ (mask * stride)) for i in range(TILES)])
+            for mask in (1, 3, 2)
+        ]
+        value = value + (one + three + two)
     return value
 
 
@@ -494,11 +486,11 @@
     swap_a = [(i, i ^ 1) for i in range(TILES)]
     swap_b = [(i, i + 1) for i in range(1, TILES - 1, 2)]
     swap_b += [(target, source) for source, target in swap_b]
-    modals, halos = [], []
-    for modal, a, b in modal_product(increments, projection):
-        modals.append(modal)
-        halos.append((lax.ppermute(a, "tile", swap_a), lax.ppermute(b, "tile", swap_b)))
-    inner, moments = inner_basis(modals)
+    modal, halos = modal_product(increments, projection)
+    halos = [
+        (lax.ppermute(a, "tile", swap_a), lax.ppermute(b, "tile", swap_b)) for a, b in halos
+    ]
+    inner, moments = inner_basis(modal)
     outers = []
     for part, (a, b) in enumerate(halos):
         outer, moments = outer_basis(inner, a, b, moments, sum(CHUNKS[:part]), CHUNKS[part])

time: 74.7 us -> 70.7 us (0.946)
  starting transfers between devices: 28.2 us -> 26.1 us
  local copies, waits for them, and re-layouts: 2.39 us -> 0.77 us
    ppermute x6 -> x9, starting transfers between devices: 20.8 us -> 18.8 us  [of_everyone(): lax.ppermute(value, 'tile', [(i, i ^ mask * stride) for i in range(TILES)])]
    unnamed x6 -> x4, local copies, waits for them, and re-layouts: 2.39 us -> 0.76 us
    pallas_call x1, Pallas kernels: 3.69 us -> 4.94 us  [modal_product(): pl.pallas_call(own_levels_kernel, grid=grid, in_specs=[whole(2 * levels,...]
    pallas_call x3 -> x2, Pallas kernels: 10.7 us -> 9.54 us  [the longest x1 5.78 us: inner_basis(): pl.pallas_call(inner_kernel, grid=(GROUPS,), in_specs=[pl.BlockSpec((8 *...]
    ppermute x6 -> x9, waiting for transfers between devices: 9.61 us -> 9.47 us  [of_everyone(): lax.ppermute(value, 'tile', [(i, i ^ mask * stride) for i in range(TILES)])]
  transfers between devices with their start and end apart: 11 -> 14, of which waited for: 6 -> 6; matrix products, arithmetic and copies ran while one was open for 0% -> 0% of each run, Pallas kernels for 26% -> 26%
where the time goes in v2:
time: 70.7 us; the launch traced here: 70.4 us
  Pallas kernels  33.3 us (47%)
  starting transfers between devices  26.1 us (37%)
  waiting for transfers between devices  9.48 us (13%)
  local copies, waits for them, and re-layouts  0.77 us (1%)
  between operations  0.71 us (1%)
    ppermute x9, starting transfers between devices, of_everyone(): lax.ppermute(value, 'tile', [(i, i ^ mask * stride) for i in range(TILES)])  18.8 us
    pallas_call x2, Pallas kernels, outer_basis(): pl.pallas_call(functools.partial(outer_kernel, start), grid=(groups,), in...  12.7 us
    ppermute x9, waiting for transfers between devices, of_everyone(): lax.ppermute(value, 'tile', [(i, i ^ mask * stride) for i in range(TILES)])  9.47 us
    pallas_call x1, Pallas kernels, solve(): pl.pallas_call(solve_kernel, grid=(GROUPS,), in_specs=[pl.BlockSpec((8, L...  6.17 us
    ppermute x2, starting transfers between devices, shards(): lax.ppermute(a, 'tile', swap_a)  5.93 us
    pallas_call x1, Pallas kernels, inner_basis(): pl.pallas_call(inner_kernel, grid=(GROUPS,), in_specs=[pl.BlockSpec((8 *...  5.78 us
    pallas_call x1, Pallas kernels, modal_product(): pl.pallas_call(own_levels_kernel, grid=grid, in_specs=[whole(2 * levels,...  4.94 us
    pallas_call x1, Pallas kernels, modal_product(): pl.pallas_call(other_levels_kernel, grid=grid, in_specs=[whole(count, dep...  3.76 us
  transfers between devices with their start and end apart: 14, of which 6 were waited for; matrix products, arithmetic and copies ran while one was open for 0% of the time, Pallas kernels for 26%

profile of v2, /device:TPU:0, one launch (start us, length us, event | category | flops | bytes accessed | tf_op | source)
XLA Modules:
  0.0 70.4 jit_solution(18067305298640525958)
XLA Ops:
  0.6 0.1 collective-permute-start
  0.7 0.0 copy-start
  0.7 0.8 %copy-done = bf16[80,136]{0,1:T(8,128)(2,1)S(1)} copy-done((bf16[80,136]{0,1:T(8,128)(2,1)S(1)}, bf16[80,136]{0,1:T(8,128)(2,1)}, u32[]{:S(2)}) %copy-start) | copy-done | bytes 21784
  1.5 4.9 %own_levels.1 = (f32[640,1024]{1,0:T(8,128)S(1)}, bf16[640,1088]{1,0:T(8,128)(2,1)S(1)}) custom-call(bf16[136,80]{1,0:T(8,128)(2,1)S(1)} %bitcast.3, bf16[1088,1024]{1,0:T(8,128)(2,1)} %bitcast.5), custom_call_target="tpu_custom_call" | custom-call | tf_op jit(solution)/shard_map/own_levels/pallas_call | solution.py:112
  6.4 0.0 collective-permute-done.inc_ref
  6.4 3.8 %other_levels.1 = (f32[640,1024]{1,0:T(8,128)S(1)}, bf16[192,1024]{1,0:T(8,128)(2,1)S(1)}, bf16[192,1024]{1,0:T(8,128)(2,1)S(1)}, bf16[128,1024]{1,0:T(8,128)(2,1)S(1)}, bf16[128,1024]{1,0:T(8,128)(2,1)S(1)}) custom-call(bf16[640,1088]{1,0:T(8,128)(2,1)S(1)} %get-tuple-element.15.left_ref, bf16[1088,1024]{1,0:T(8,128)(2,1)S(1)} %collective-permute-done.inc_ref, ...), custom_call_target="tpu_custom_call" | custom-call | tf_op jit(solution)/shard_map/other_levels/pallas_call | solution.py:126
  10.2 1.8 %collective-permute-start.3 = (bf16[192,1024]{1,0:T(8,128)(2,1)S(1)}, bf16[192,1024]{1,0:T(8,128)(2,1)S(1)}, u32[]{:S(2)}, u32[]{:S(2)}) collective-permute-start(bf16[192,1024]{1,0:T(8,128)(2,1)S(1)} %get-tuple-element.21), channel_id=1, source_target_pairs={{0,2},{2,0},{4,6},{6,4},{8,10},{10,8},{12,14},{14,12},{16,18},{18,... | collective-permute-start | bytes 1179656 | tf_op jit(solution)/shard_map/ppermute | solution.py:491
  12.0 0.7 collective-permute-start.4
  12.7 4.2 %collective-permute-start.1 = (bf16[128,1024]{1,0:T(8,128)(2,1)S(1)}, bf16[128,1024]{1,0:T(8,128)(2,1)S(1)}, u32[]{:S(2)}, u32[]{:S(2)}) collective-permute-start(bf16[128,1024]{1,0:T(8,128)(2,1)S(1)} %get-tuple-element.19), channel_id=1, source_target_pairs={{0,2},{2,0},{4,6},{6,4},{8,10},{10,8},{12,14},{14,12},{16,18},{18,... | collective-permute-start | bytes 786440 | tf_op jit(solution)/shard_map/ppermute | solution.py:491
  16.8 0.7 collective-permute-start.2
  17.5 5.8 %inner.1 = (f32[5,576,1024]{2,1,0:T(8,128)S(1)}, f32[8,128]{1,0:T(8,128)S(1)}) custom-call(f32[640,1024]{1,0:T(8,128)S(1)} %get-tuple-element.17.modal_ref), custom_call_target="tpu_custom_call" | custom-call | tf_op jit(solution)/shard_map/inner/pallas_call | solution.py:238
  23.3 0.0 collective-permute-done.3.a_ref
  23.3 0.0 collective-permute-done.4.b_ref
  23.3 7.6 %outer.2 = (f32[3,576,1024]{2,1,0:T(8,128)S(1)}, f32[8,128]{1,0:T(8,128)S(1)}) custom-call(f32[5,576,1024]{2,1,0:T(8,128)S(1)} %get-tuple-element.18.inner_ref, bf16[192,1024]{1,0:T(8,128)(2,1)S(1)} %collective-permute-done.3.a_ref, bf16[192,1024]{1,0:T(8,128)(2,1)S(1)} %collective-permute-done.4.b_ref, f32[8,128]{1,0:T(8,128)S(1)} %get-tuple-element.23.known_ref), custom_call_target="tpu_custom_call" | custom-call | tf_op jit(solution)/shard_map/outer/pallas_call | solution.py:310
  30.9 0.0 collective-permute-done.1.a_ref
  30.9 0.0 collective-permute-done.2.b_ref
  30.9 0.0 copy-start.1
  30.9 5.1 %outer.3 = (f32[2,576,1024]{2,1,0:T(8,128)S(1)}, f32[8,128]{1,0:T(8,128)S(1)}) custom-call(f32[5,576,1024]{2,1,0:T(8,128)S(1)} %get-tuple-element.18.inner_ref, bf16[128,1024]{1,0:T(8,128)(2,1)S(1)} %collective-permute-done.1.a_ref, bf16[128,1024]{1,0:T(8,128)(2,1)S(1)} %collective-permute-done.2.b_ref, f32[8,128]{1,0:T(8,128)S(1)} %get-tuple-element.24.known_ref), custom_call_target="tpu_custom_call" | custom-call | tf_op jit(solution)/shard_map/outer/pallas_call | solution.py:310
  36.0 5.5 %collective-permute-start.7 = (f32[8,128]{1,0:T(8,128)S(1)}, f32[8,128]{1,0:T(8,128)S(1)}, u32[]{:S(2)}, u32[]{:S(2)}) collective-permute-start(f32[8,128]{1,0:T(8,128)S(1)} %get-tuple-element.25), channel_id=1, source_target_pairs={{0,4},{2,6},{4,0},{6,2},{8,12},{10,14},{12,8},{14,10},{16,20},{18,... | collective-permute-start | bytes 12296 | tf_op jit(solution)/shard_map/ppermute | solution.py:478
  41.5 1.6 %collective-permute-start.6 = (f32[8,128]{1,0:T(8,128)S(1)}, f32[8,128]{1,0:T(8,128)S(1)}, u32[]{:S(2)}, u32[]{:S(2)}) collective-permute-start(f32[8,128]{1,0:T(8,128)S(1)} %get-tuple-element.25), channel_id=1, source_target_pairs={{0,6},{2,4},{4,2},{6,0},{8,14},{10,12},{12,10},{14,8},{16,22},{18,... | collective-permute-start | bytes 12296 | tf_op jit(solution)/shard_map/ppermute | solution.py:478
  43.1 0.6 collective-permute-start.5
  43.7 0.0 collective-permute-done.7
  43.7 2.6 %collective-permute-done.6 = f32[8,128]{1,0:T(8,128)S(1)} collective-permute-done((f32[8,128]{1,0:T(8,128)S(1)}, f32[8,128]{1,0:T(8,128)S(1)}, u32[]{:S(2)}, u32[]{:S(2)}) %collective-permute-start.6) | collective-permute-done | bytes 4128 | tf_op jit(solution)/shard_map/ppermute | solution.py:478
  46.3 0.4 collective-permute-done.5
  46.7 3.7 %collective-permute-start.10 = (f32[8,128]{1,0:T(8,128)S(1)}, f32[8,128]{1,0:T(8,128)S(1)}, u32[]{:S(2)}, u32[]{:S(2)}) collective-permute-start(f32[8,128]{1,0:T(8,128)S(1)} %add_add_fusion.2), channel_id=1, source_target_pairs={{0,16},{2,18},{4,20},{6,22},{8,24},{10,26},{12,28},{14,30},{16,0},... | collective-permute-start | bytes 12296 | tf_op jit(solution)/shard_map/ppermute | solution.py:478
  50.4 2.4 %collective-permute-start.9 = (f32[8,128]{1,0:T(8,128)S(1)}, f32[8,128]{1,0:T(8,128)S(1)}, u32[]{:S(2)}, u32[]{:S(2)}) collective-permute-start(f32[8,128]{1,0:T(8,128)S(1)} %add_add_fusion.2), channel_id=1, source_target_pairs={{0,24},{2,26},{4,28},{6,30},{8,16},{10,18},{12,20},{14,22},{16,8},... | collective-permute-start | bytes 12296 | tf_op jit(solution)/shard_map/ppermute | solution.py:478
  52.8 0.8 %collective-permute-start.8 = (f32[8,128]{1,0:T(8,128)S(1)}, f32[8,128]{1,0:T(8,128)S(1)}, u32[]{:S(2)}, u32[]{:S(2)}) collective-permute-start(f32[8,128]{1,0:T(8,128)S(1)} %add_add_fusion.2), channel_id=1, source_target_pairs={{0,8},{2,10},{4,12},{6,14},{8,0},{10,2},{12,4},{14,6},{16,24},{18,... | collective-permute-start | bytes 12296 | tf_op jit(solution)/shard_map/ppermute | solution.py:478
  53.6 0.0 collective-permute-done.10
  53.6 1.7 %collective-permute-done.9 = f32[8,128]{1,0:T(8,128)S(1)} collective-permute-done((f32[8,128]{1,0:T(8,128)S(1)}, f32[8,128]{1,0:T(8,128)S(1)}, u32[]{:S(2)}, u32[]{:S(2)}) %collective-permute-start.9) | collective-permute-done | bytes 4128 | tf_op jit(solution)/shard_map/ppermute | solution.py:478
  55.2 1.1 %collective-permute-done.8 = f32[8,128]{1,0:T(8,128)S(1)} collective-permute-done((f32[8,128]{1,0:T(8,128)S(1)}, f32[8,128]{1,0:T(8,128)S(1)}, u32[]{:S(2)}, u32[]{:S(2)}) %collective-permute-start.8) | collective-permute-done | bytes 4128 | tf_op jit(solution)/shard_map/ppermute | solution.py:478
  56.4 3.0 %collective-permute-start.13 = (f32[8,128]{1,0:T(8,128)S(1)}, f32[8,128]{1,0:T(8,128)S(1)}, u32[]{:S(2)}, u32[]{:S(2)}) collective-permute-start(f32[8,128]{1,0:T(8,128)S(1)} %add_add_fusion.1), channel_id=1, source_target_pairs={{0,64},{2,66},{4,68},{6,70},{8,72},{10,74},{12,76},{14,78},{16,80}... | collective-permute-start | bytes 12296 | tf_op jit(solution)/shard_map/ppermute | solution.py:478
  59.4 1.1 %collective-permute-start.12 = (f32[8,128]{1,0:T(8,128)S(1)}, f32[8,128]{1,0:T(8,128)S(1)}, u32[]{:S(2)}, u32[]{:S(2)}) collective-permute-start(f32[8,128]{1,0:T(8,128)S(1)} %add_add_fusion.1), channel_id=1, source_target_pairs={{0,96},{2,98},{4,100},{6,102},{8,104},{10,106},{12,108},{14,110},{... | collective-permute-start | bytes 12296 | tf_op jit(solution)/shard_map/ppermute | solution.py:478
  60.6 0.0 collective-permute-start.11
  60.6 0.0 copy-done.1
  60.6 0.9 %collective-permute-done.13 = f32[8,128]{1,0:T(8,128)S(1)} collective-permute-done((f32[8,128]{1,0:T(8,128)S(1)}, f32[8,128]{1,0:T(8,128)S(1)}, u32[]{:S(2)}, u32[]{:S(2)}) %collective-permute-start.13) | collective-permute-done | bytes 4128 | tf_op jit(solution)/shard_map/ppermute | solution.py:478
  61.5 2.7 %collective-permute-done.12 = f32[8,128]{1,0:T(8,128)S(1)} collective-permute-done((f32[8,128]{1,0:T(8,128)S(1)}, f32[8,128]{1,0:T(8,128)S(1)}, u32[]{:S(2)}, u32[]{:S(2)}) %collective-permute-start.12) | collective-permute-done | bytes 4128 | tf_op jit(solution)/shard_map/ppermute | solution.py:478
  64.2 0.0 collective-permute-done.11
  64.2 6.2 %solve.1 = (f32[40,16,1024]{2,1,0:T(8,128)}, f32[40,16,1024]{2,1,0:T(8,128)}) custom-call(f32[8,128]{1,0:T(8,128)S(1)} %add_add_fusion.sums_ref, f32[1,128]{1,0:T(1,128)S(1)} %pad.4.helm_ref, f32[5,576,1024]{2,1,0:T(8,128)S(1)} %get-tuple-element.18.inner_ref, f32[3,576,1024]{2,1,0:T(8,128)S(1)} %get-tuple-element.26.refs_0_, ...), custom_call_target="tpu_custom_call" | custom-call | tf_op jit(solution)/shard_map/solve/pallas_call | solution.py:455
  (4 shorter events, 0.0 us)
Async XLA Ops:
  0.6 5.8 %collective-permute-start = (bf16[1088,1024]{1,0:T(8,128)(2,1)}, bf16[1088,1024]{1,0:T(8,128)(2,1)S(1)}, u32[]{:S(2)}, u32[]{:S(2)}) collective-permute-start(bf16[1088,1024]{1,0:T(8,128)(2,1)} %bitcast.4), channel_id=1, source_target_pairs={{0,1},{1,0},{2,3},{3,2},{4,5},{5,4},{6,7},{7,6},{8,9},{9,8},{10,11... | collective-permute-start | bytes 6684680 | tf_op jit(solution)/shard_map/ppermute | solution.py:106
  0.7 0.8 %copy-start = (bf16[80,136]{0,1:T(8,128)(2,1)S(1)}, bf16[80,136]{0,1:T(8,128)(2,1)}, u32[]{:S(2)}) copy-start(bf16[80,136]{0,1:T(8,128)(2,1)} %param.4) | copy-start | bytes 65284
  10.2 13.1 %collective-permute-start.3 = (bf16[192,1024]{1,0:T(8,128)(2,1)S(1)}, bf16[192,1024]{1,0:T(8,128)(2,1)S(1)}, u32[]{:S(2)}, u32[]{:S(2)}) collective-permute-start(bf16[192,1024]{1,0:T(8,128)(2,1)S(1)} %get-tuple-element.21), channel_id=1, source_target_pairs={{0,2},{2,0},{4,6},{6,4},{8,10},{10,8},{12,14},{14,12},{16,18},{18,... | collective-permute-start | bytes 1179656 | tf_op jit(solution)/shard_map/ppermute | solution.py:491
  12.0 11.3 %collective-permute-start.4 = (bf16[192,1024]{1,0:T(8,128)(2,1)S(1)}, bf16[192,1024]{1,0:T(8,128)(2,1)S(1)}, u32[]{:S(2)}, u32[]{:S(2)}) collective-permute-start(bf16[192,1024]{1,0:T(8,128)(2,1)S(1)} %get-tuple-element.22), channel_id=1, source_target_pairs={{2,4},{6,8},{10,12},{14,16},{18,20},{22,24},{26,28},{30,32},{34,36... | collective-permute-start | bytes 1179656 | tf_op jit(solution)/shard_map/ppermute | solution.py:491
  12.7 18.2 %collective-permute-start.1 = (bf16[128,1024]{1,0:T(8,128)(2,1)S(1)}, bf16[128,1024]{1,0:T(8,128)(2,1)S(1)}, u32[]{:S(2)}, u32[]{:S(2)}) collective-permute-start(bf16[128,1024]{1,0:T(8,128)(2,1)S(1)} %get-tuple-element.19), channel_id=1, source_target_pairs={{0,2},{2,0},{4,6},{6,4},{8,10},{10,8},{12,14},{14,12},{16,18},{18,... | collective-permute-start | bytes 786440 | tf_op jit(solution)/shard_map/ppermute | solution.py:491
  16.8 14.0 %collective-permute-start.2 = (bf16[128,1024]{1,0:T(8,128)(2,1)S(1)}, bf16[128,1024]{1,0:T(8,128)(2,1)S(1)}, u32[]{:S(2)}, u32[]{:S(2)}) collective-permute-start(bf16[128,1024]{1,0:T(8,128)(2,1)S(1)} %get-tuple-element.20), channel_id=1, source_target_pairs={{2,4},{6,8},{10,12},{14,16},{18,20},{22,24},{26,28},{30,32},{34,36... | collective-permute-start | bytes 786440 | tf_op jit(solution)/shard_map/ppermute | solution.py:491
  30.9 29.7 %copy-start.1 = (f32[40]{0:T(128)S(1)}, f32[40]{0:T(128)}, u32[]{:S(2)}) copy-start(f32[40]{0:T(128)} %param.5) | copy-start | bytes 484
  36.0 7.8 %collective-permute-start.7 = (f32[8,128]{1,0:T(8,128)S(1)}, f32[8,128]{1,0:T(8,128)S(1)}, u32[]{:S(2)}, u32[]{:S(2)}) collective-permute-start(f32[8,128]{1,0:T(8,128)S(1)} %get-tuple-element.25), channel_id=1, source_target_pairs={{0,4},{2,6},{4,0},{6,2},{8,12},{10,14},{12,8},{14,10},{16,20},{18,... | collective-permute-start | bytes 12296 | tf_op jit(solution)/shard_map/ppermute | solution.py:478
  41.5 4.8 %collective-permute-start.6 = (f32[8,128]{1,0:T(8,128)S(1)}, f32[8,128]{1,0:T(8,128)S(1)}, u32[]{:S(2)}, u32[]{:S(2)}) collective-permute-start(f32[8,128]{1,0:T(8,128)S(1)} %get-tuple-element.25), channel_id=1, source_target_pairs={{0,6},{2,4},{4,2},{6,0},{8,14},{10,12},{12,10},{14,8},{16,22},{18,... | collective-permute-start | bytes 12296 | tf_op jit(solution)/shard_map/ppermute | solution.py:478
  43.1 3.6 %collective-permute-start.5 = (f32[8,128]{1,0:T(8,128)S(1)}, f32[8,128]{1,0:T(8,128)S(1)}, u32[]{:S(2)}, u32[]{:S(2)}) collective-permute-start(f32[8,128]{1,0:T(8,128)S(1)} %get-tuple-element.25), channel_id=1, source_target_pairs={{0,2},{2,0},{4,6},{6,4},{8,10},{10,8},{12,14},{14,12},{16,18},{18,... | collective-permute-start | bytes 12296 | tf_op jit(solution)/shard_map/ppermute | solution.py:478
  46.7 6.9 %collective-permute-start.10 = (f32[8,128]{1,0:T(8,128)S(1)}, f32[8,128]{1,0:T(8,128)S(1)}, u32[]{:S(2)}, u32[]{:S(2)}) collective-permute-start(f32[8,128]{1,0:T(8,128)S(1)} %add_add_fusion.2), channel_id=1, source_target_pairs={{0,16},{2,18},{4,20},{6,22},{8,24},{10,26},{12,28},{14,30},{16,0},... | collective-permute-start | bytes 12296 | tf_op jit(solution)/shard_map/ppermute | solution.py:478
  50.4 4.8 %collective-permute-start.9 = (f32[8,128]{1,0:T(8,128)S(1)}, f32[8,128]{1,0:T(8,128)S(1)}, u32[]{:S(2)}, u32[]{:S(2)}) collective-permute-start(f32[8,128]{1,0:T(8,128)S(1)} %add_add_fusion.2), channel_id=1, source_target_pairs={{0,24},{2,26},{4,28},{6,30},{8,16},{10,18},{12,20},{14,22},{16,8},... | collective-permute-start | bytes 12296 | tf_op jit(solution)/shard_map/ppermute | solution.py:478
  52.8 3.6 %collective-permute-start.8 = (f32[8,128]{1,0:T(8,128)S(1)}, f32[8,128]{1,0:T(8,128)S(1)}, u32[]{:S(2)}, u32[]{:S(2)}) collective-permute-start(f32[8,128]{1,0:T(8,128)S(1)} %add_add_fusion.2), channel_id=1, source_target_pairs={{0,8},{2,10},{4,12},{6,14},{8,0},{10,2},{12,4},{14,6},{16,24},{18,... | collective-permute-start | bytes 12296 | tf_op jit(solution)/shard_map/ppermute | solution.py:478
  56.4 5.1 %collective-permute-start.13 = (f32[8,128]{1,0:T(8,128)S(1)}, f32[8,128]{1,0:T(8,128)S(1)}, u32[]{:S(2)}, u32[]{:S(2)}) collective-permute-start(f32[8,128]{1,0:T(8,128)S(1)} %add_add_fusion.1), channel_id=1, source_target_pairs={{0,64},{2,66},{4,68},{6,70},{8,72},{10,74},{12,76},{14,78},{16,80}... | collective-permute-start | bytes 12296 | tf_op jit(solution)/shard_map/ppermute | solution.py:478
  59.4 4.8 %collective-permute-start.12 = (f32[8,128]{1,0:T(8,128)S(1)}, f32[8,128]{1,0:T(8,128)S(1)}, u32[]{:S(2)}, u32[]{:S(2)}) collective-permute-start(f32[8,128]{1,0:T(8,128)S(1)} %add_add_fusion.1), channel_id=1, source_target_pairs={{0,96},{2,98},{4,100},{6,102},{8,104},{10,106},{12,108},{14,110},{... | collective-permute-start | bytes 12296 | tf_op jit(solution)/shard_map/ppermute | solution.py:478
  60.6 3.7 %collective-permute-start.11 = (f32[8,128]{1,0:T(8,128)S(1)}, f32[8,128]{1,0:T(8,128)S(1)}, u32[]{:S(2)}, u32[]{:S(2)}) collective-permute-start(f32[8,128]{1,0:T(8,128)S(1)} %add_add_fusion.1), channel_id=1, source_target_pairs={{0,32},{2,34},{4,36},{6,38},{8,40},{10,42},{12,44},{14,46},{16,48}... | collective-permute-start | bytes 12296 | tf_op jit(solution)/shard_map/ppermute | solution.py:478

commit v3 on v2

v3 whole, which is shorter than its diff:
```python
import functools

import jax
import jax.numpy as jnp
from jax import lax
from jax.experimental import pallas as pl
from jax.experimental.pallas import tpu as pltpu
from jax.sharding import PartitionSpec as P

STEPS = 8
MOMENTS = 2 * STEPS
ROWS = 16
HALO = 8
MODES = 40
GROUPS = 5
LANES = 128
COLS = 1024
BLOCKS = COLS // LANES
TILES = 64


class ModeSet:
    def __init__(self, *groups):
        self.groups = groups
        self.modes = 8 * len(groups)
        self.base = 8 * groups[0]
        self.segments = LANES // self.modes
        self.length = COLS // self.segments
        self.count = self.length // 8
        self.pitch = self.length + 8

    def rows(self, slabs):
        return slabs * self.pitch + 8


SETS = (ModeSet(0, 1), ModeSet(2, 3), ModeSet(4))
CHUNKS = ((0, 2), (1,))

f32 = jnp.float32
bf16 = jnp.bfloat16


def limits(mib):
    return pltpu.CompilerParams(vmem_limit_bytes=mib * 2**20)


def build_left(proj_ref, left_ref, level0):
    lev = lax.axis_index("lev")
    depth = left_ref.shape[1]
    pick = (
        lax.broadcasted_iota(jnp.int32, (MODES, 2 * MODES), 1)
        == lax.broadcasted_iota(jnp.int32, (MODES, 2 * MODES), 0) + lev * MODES
    ).astype(bf16)
    own = lax.dot_general(
        pick, proj_ref[...], (((1,), (1,)), ((), ())), preferred_element_type=f32
    ).astype(bf16)
    levels = proj_ref.shape[0]
    spread = (
        lax.broadcasted_iota(jnp.int32, (levels, depth), 0)
        == (lax.broadcasted_iota(jnp.int32, (levels, depth), 1) >> 4) + level0
    ).astype(bf16)
    wide = jnp.dot(own, spread, preferred_element_type=f32)
    row_of = lax.broadcasted_iota(jnp.int32, (8, depth), 1) & (ROWS - 1)
    for group in range(GROUPS):
        part = wide[group * 8:(group + 1) * 8]
        for row in range(0, ROWS, 2):
            two = jnp.concatenate(
                [jnp.where(row_of == row, part, 0.0), jnp.where(row_of == row + 1, part, 0.0)],
                axis=0,
            )
            at = group * 8 * ROWS + row * 8
            left_ref[at:at + 16, :] = two.astype(bf16)


def own_levels_kernel(proj_ref, inc_ref, acc_ref, other_left_ref, left_ref):
    lev = lax.axis_index("lev")
    count = proj_ref.shape[0] // 2

    @pl.when(pl.program_id(0) == 0)
    def _():
        build_left(proj_ref, left_ref, lev * count)
        build_left(proj_ref, other_left_ref, (1 - lev) * count)

    acc_ref[...] = jnp.dot(left_ref[...], inc_ref[...], preferred_element_type=f32)


def coded(x):
    t = x * 2.0 ** 13
    square = t * t
    eight = t * 8.0
    y = jnp.where(square < 1.0, eight * jnp.abs(eight), (square * 8.0) * ((square * 8.0) * t))
    return y.astype(bf16)


def decoded(y):
    y = y.astype(f32)
    exponent = jnp.log2(jnp.abs(y)) - 6.0
    root = jnp.exp2(exponent * jnp.where(exponent < 0.0, 0.5, 0.2) - 13.0)
    return jnp.where(y < 0.0, -root, root)


def other_levels_kernel(left_ref, inc_ref, acc_ref, modal_ref):
    modal_ref[...] = acc_ref[...] + jnp.dot(
        left_ref[...], inc_ref[...], preferred_element_type=f32
    )


def modal_product(increments, projection):
    levels = increments.shape[0]
    depth = levels * ROWS
    flat = increments.reshape(depth, COLS)
    arrived = lax.ppermute(flat, "lev", [(0, 1), (1, 0)])
    width = 256
    grid = (COLS // width,)
    count = MODES * ROWS
    column = lambda rows: pl.BlockSpec((rows, width), lambda c: (0, c))
    whole = lambda rows, cols: pl.BlockSpec((rows, cols), lambda c: (0, 0))
    acc, other_left = pl.pallas_call(
        own_levels_kernel,
        grid=grid,
        in_specs=[whole(2 * levels, 2 * MODES), column(depth)],
        out_specs=[column(count), whole(count, depth)],
        out_shape=[
            jax.ShapeDtypeStruct((count, COLS), f32),
            jax.ShapeDtypeStruct((count, depth), bf16),
        ],
        scratch_shapes=[pltpu.VMEM((count, depth), bf16)],
        compiler_params=limits(20),
        name="own_levels",
    )(projection.T, pltpu.with_memory_space_constraint(flat, pltpu.HBM))
    return pl.pallas_call(
        other_levels_kernel,
        grid=grid,
        in_specs=[whole(count, depth), column(depth), column(count)],
        out_specs=column(count),
        out_shape=jax.ShapeDtypeStruct((count, COLS), f32),
        compiler_params=limits(20),
        name="other_levels",
    )(other_left, arrived, acc)


def lanes():
    return lax.broadcasted_iota(jnp.int32, (8, LANES), 1)


def slab_ends(ref, lead, at, kind, first, last):
    after = pltpu.roll(first, LANES - kind.modes, 1)
    after = jnp.where(lanes() >= LANES - kind.modes, 0.0, after)
    before = jnp.where(lanes() < kind.modes, 0.0, pltpu.roll(last, kind.modes, 1))
    end = at + 8 + kind.length
    ref[lead, end:end + 1, :] = after[0:1, :]
    ref[lead, at + 7:at + 8, :] = before[7:8, :]


def slab_store(ref, lead, at, v, value):
    ref[lead, at + 8 + 8 * v:at + 16 + 8 * v, :] = value


def slab_load(ref, lead, at, v, offset=0):
    start = at + 8 + 8 * v + offset
    return ref[lead, start:start + 8, :]


def full(shape):
    return pl.BlockSpec(shape, lambda i: (0,) * len(shape))


def single(kernel, outs, name, mib=16, scratch=()):
    def call(*args):
        return pl.pallas_call(
            kernel,
            grid=(1,),
            in_specs=[full(x.shape) for x in args],
            out_specs=[full(x.shape) for x in outs],
            out_shape=list(outs),
            scratch_shapes=list(scratch),
            compiler_params=limits(mib),
            name=name,
        )(*args)
    return call


def turn_kernel(modal_ref, *refs):
    even = (lax.axis_index("tile") & 1) == 0
    first_refs, halo_refs = refs[:len(SETS)], refs[len(SETS):]
    for part, members in enumerate(CHUNKS):
        a_ref, b_ref = halo_refs[2 * part:2 * part + 2]
        offset = 0
        for member in members:
            kind = SETS[member]

            ref = first_refs[member]

            def columns(row):
                parts = []
                for b in range(BLOCKS):
                    for group in kind.groups:
                        at = (group * ROWS + row) * 8
                        value = modal_ref[at:at + 8, b * LANES:(b + 1) * LANES]
                        parts.append(value)
                        if len(kind.groups) == 1:
                            parts.append(pltpu.roll(value, LANES // 2, 1))
                return jnp.concatenate(parts, axis=0)

            ready = [columns(row) for row in range(4)]
            for row in range(ROWS):
                whole = ready.pop(0).T
                if row + 4 < ROWS:
                    ready.append(columns(row + 4))
                for v in range(kind.count):
                    slab_store(ref, 0, row * kind.pitch, v, whole[8 * v:8 * v + 8])
            for row in range(HALO):
                for v in range(0, kind.count, 2):
                    at = offset + row * kind.length + 8 * v
                    low, high = [
                        coded(jnp.concatenate(
                            [slab_load(ref, 0, start * kind.pitch, v + n) for n in range(2)], axis=0
                        ))
                        for start in (row, row + HALO)
                    ]
                    a_ref[at:at + 16, :] = jnp.where(even, high, low)
                    b_ref[at:at + 16, :] = jnp.where(even, low, high)
            for row in range(ROWS):
                at = row * kind.pitch
                slab_ends(
                    ref, 0, at, kind, slab_load(ref, 0, at, 0), slab_load(ref, 0, at, kind.count - 1)
                )
            offset += HALO * kind.length


def turn(modal):
    firsts = [jax.ShapeDtypeStruct((1, kind.rows(ROWS), LANES), f32) for kind in SETS]
    halos = [
        jax.ShapeDtypeStruct((sum(HALO * SETS[m].length for m in members), LANES), bf16)
        for members in CHUNKS for _ in range(2)
    ]
    out = single(turn_kernel, firsts + halos, "turn")(modal)
    halos = out[len(SETS):]
    return out[:len(SETS)], list(zip(halos[::2], halos[1::2]))


def is_inner(order, row):
    return order <= row < ROWS - order


INNER_SLOTS, OUTER_SLOTS = {}, {}
for order_ in range(1, STEPS + 1):
    for row_ in range(ROWS):
        slots_ = INNER_SLOTS if is_inner(order_, row_) else OUTER_SLOTS
        slots_[order_, row_] = len(slots_)
STRIP = 8


def sweep(kind, order, begin, end, place, sums, factor_of):
    for strip in range(0, kind.count, STRIP):
        span = range(strip, strip + STRIP)
        near = lambda row: [slab_load(*place(order - 1, row), v) for v in span]
        above, here = near(begin - 1), near(begin)
        for row in range(begin, end):
            below = near(row + 1)
            factor = factor_of(row)
            squares, crosses = [], []
            for n, v in enumerate(span):
                left = slab_load(*place(order - 1, row), v, -1)
                right = slab_load(*place(order - 1, row), v, 1)
                value = ((above[n] + below[n]) + (left + right)) * factor
                if order > 1:
                    value = value - slab_load(*place(order - 2, row), v)
                ref, lead, at = place(order, row)
                slab_store(ref, lead, at, v, value)
                if v == kind.count - 1:
                    slab_ends(ref, lead, at, kind, slab_load(ref, lead, at, 0), value)
                squares.append(value * value)
                crosses.append(value * here[n])
            if 0 <= row < ROWS:
                if 2 * order < MOMENTS:
                    accumulate(sums, 2 * order, total(squares))
                accumulate(sums, 2 * order - 1, total(crosses))
            above, here = here, below


def total(values):
    while len(values) > 1:
        values = [values[i] + values[i + 1] for i in range(0, len(values), 2)]
    return values[0]


def accumulate(sums, index, value):
    sums[index] = sums[index] + value if index in sums else value


def inner_kernel(*refs):
    count = len(SETS)
    for kind, first_ref, inner_ref, moment_ref in zip(
        SETS, refs[:count], refs[count:2 * count], refs[2 * count:]
    ):
        def place(order, row):
            if order == 0:
                return first_ref, 0, row * kind.pitch
            return inner_ref, 0, INNER_SLOTS[order, row] * kind.pitch

        sums = {}
        for row in range(ROWS):
            values = [slab_load(*place(0, row), v) for v in range(kind.count)]
            accumulate(sums, 0, total([v * v for v in values]))
        for order in range(1, STEPS):
            factor = 0.25 if order == 1 else 0.5
            sweep(kind, order, order, ROWS - order, place, sums, lambda row: factor)
        for index in range(MOMENTS):
            if index in sums:
                moment_ref[index:index + 1, :] = jnp.sum(sums[index], axis=0, keepdims=True)
            else:
                moment_ref[index:index + 1, :] = jnp.zeros((1, LANES), f32)


def inner_basis(firsts):
    outs = [jax.ShapeDtypeStruct((1, kind.rows(len(INNER_SLOTS)), LANES), f32) for kind in SETS]
    outs += [jax.ShapeDtypeStruct((MOMENTS, LANES), f32)] * len(SETS)
    out = single(inner_kernel, outs, "inner")(*firsts)
    return out[:len(SETS)], out[len(SETS):]


def outer_kernel(members, a_ref, b_ref, known_ref, *refs):
    count = len(members)
    ins, (outs, (moment_ref, *halo_refs)) = refs[:3 * count], (
        refs[3 * count:4 * count], refs[4 * count:]
    )
    tile = lax.axis_index("tile")
    even = (tile & 1) == 0
    half_low = jnp.where(tile == 0, 0.0, 0.5)
    half_high = jnp.where(tile == TILES - 1, 0.0, 0.5)
    lane = lax.broadcasted_iota(jnp.int32, (MOMENTS, LANES), 1)
    moments = known_ref[...]
    offset = 0
    for n, member in enumerate(members):
        kind = SETS[member]
        first_ref, inner_ref, part_ref = ins[3 * n:3 * n + 3]
        outer_ref, halo_ref = outs[n], halo_refs[n]
        for row in range(HALO):
            for v in range(0, kind.count, 2):
                at = offset + row * kind.length + 8 * v
                a = decoded(a_ref[at:at + 16, :])
                b = decoded(b_ref[at:at + 16, :])
                for side, both in ((0, jnp.where(even, b, a)), (3, jnp.where(even, a, b))):
                    slab_store(halo_ref, side, row * kind.pitch, v, both[:8])
                    slab_store(halo_ref, side, row * kind.pitch, v + 1, both[8:])
                    if v == 0:
                        first = {} if side == 0 else first
                        first[side] = both[:8]
                    if v + 2 == kind.count:
                        slab_ends(halo_ref, side, row * kind.pitch, kind, first[side], both[8:])
        offset += HALO * kind.length

        def place(order, row):
            if row < 0:
                return halo_ref, order % 3, (row + HALO) * kind.pitch
            if row >= ROWS:
                return halo_ref, 3 + order % 3, (row - ROWS) * kind.pitch
            if order == 0:
                return first_ref, 0, row * kind.pitch
            if is_inner(order, row):
                return inner_ref, 0, INNER_SLOTS[order, row] * kind.pitch
            return outer_ref, 0, OUTER_SLOTS[order, row] * kind.pitch

        sums = {}
        for order in range(1, STEPS + 1):
            def factor_of(row):
                half = 0.5 if 0 <= row < ROWS else half_low if row < 0 else half_high
                return half * 0.5 if order == 1 else half

            for begin, end in ((order - HALO, order), (ROWS - order, ROWS + HALO - order)):
                sweep(kind, order, begin, end, place, sums, factor_of)
        rows = [
            jnp.sum(sums[i], axis=0, keepdims=True) if i in sums else jnp.zeros((1, LANES), f32)
            for i in range(MOMENTS)
        ]
        part = part_ref[...] + jnp.concatenate(rows, axis=0)
        step = LANES // 2
        while step >= kind.modes:
            part = part + pltpu.roll(part, step, 1)
            step //= 2
        mine = (lane >= kind.base) & (lane < kind.base + kind.modes)
        moments = moments + jnp.where(mine, part, 0.0)
    moment_ref[...] = moments


def outer_basis(members, halo, known, firsts, inners, parts):
    outs = [
        jax.ShapeDtypeStruct((1, SETS[m].rows(len(OUTER_SLOTS)), LANES), f32) for m in members
    ]
    outs += [jax.ShapeDtypeStruct((MOMENTS, LANES), f32)]
    args = [x for m in members for x in (firsts[m], inners[m], parts[m])]
    scratch = [pltpu.VMEM((6, SETS[m].rows(HALO), LANES), f32) for m in members]
    out = single(functools.partial(outer_kernel, members), outs, "outer", 24, scratch)(
        *halo, known, *args
    )
    return out[:-1], out[-1]


def coefficients(nu, tau):
    half = 0.5 * tau
    rho = list(nu)
    pi = list(nu)
    one, zero = jnp.ones_like(tau), None
    r = [one]
    p = [one]
    x = [None] * STEPS
    rr = nu[0]

    def plus(a, b):
        if a is None:
            return b
        if b is None:
            return a
        return a + b

    def inner(c, v):
        terms = [ci * vi for ci, vi in zip(c, v)]
        while len(terms) > 1:
            terms = [sum(terms[i:i + 2]) for i in range(0, len(terms), 2)]
        return terms[0]

    for step in range(STEPS):
        top = MOMENTS - 1 - step
        image = []
        for l in range(top):
            near = pi[l + 1] + pi[abs(l - 1)]
            image.append(pi[l] - half * near)
        alpha = rr / inner(p, image)
        x = [plus(x[i], alpha * p[i]) if i < len(p) else x[i] for i in range(STEPS)]
        shifted = [None] * (len(p) + 1)
        for k, value in enumerate(p):
            if k == 0:
                shifted[1] = plus(shifted[1], tau * value)
            else:
                scaled = half * value
                shifted[k + 1] = plus(shifted[k + 1], scaled)
                shifted[k - 1] = plus(shifted[k - 1], scaled)
        moved = []
        for k in range(len(p) + 1):
            own = p[k] if k < len(p) else None
            if shifted[k] is None:
                moved.append(own)
            elif own is None:
                moved.append(-shifted[k])
            else:
                moved.append(own - shifted[k])
        r = [
            (r[k] - alpha * moved[k]) if k < len(r) else -(alpha * moved[k])
            for k in range(len(moved))
        ]
        if step == STEPS - 1:
            break
        rho = [rho[l] - alpha * image[l] for l in range(top)]
        fresh = inner(r, rho)
        beta = fresh / rr
        pi = [rho[l] + beta * pi[l] for l in range(top)]
        p = [plus(r[k], beta * p[k] if k < len(p) else None) for k in range(len(r))]
        rr = fresh
    return x, r


def solve_kernel(sums_ref, helm_ref, *refs):
    count = len(SETS)
    fields = [refs[3 * n:3 * n + 3] for n in range(count)]
    x_out, r_out, x_ref, r_ref, stage_ref, coef_ref, sems = refs[3 * count:]
    raw = [sums_ref[k:k + 1, :] for k in range(MOMENTS)]
    nu = raw[:2]
    for k in range(2, MOMENTS):
        nu.append(2.0 * raw[k] - nu[k & 1])
    x, r = coefficients(nu, 4.0 / (4.0 + helm_ref[...]))
    for k, value in enumerate(x + r):
        coef_ref[k:k + 1, :] = value
    coefs = coef_ref[...]
    lane_all = lax.broadcasted_iota(jnp.int32, coefs.shape, 1)
    low_half = lanes() < LANES // 2
    copies = []
    for kind, (first_ref, inner_ref, outer_ref) in zip(SETS, fields):
        mine = (lane_all >= kind.base) & (lane_all < kind.base + kind.modes)
        own = jnp.where(mine, coefs, 0.0)
        step = kind.modes
        while step < LANES:
            own = own + pltpu.roll(own, step, 1)
            step *= 2
        spread = [jnp.broadcast_to(own[k:k + 1, :], (8, LANES)) for k in range(2 * STEPS + 1)]
        cx, cr = spread[:STEPS], spread[STEPS:]

        def combined(row):
            xs, rs = [], []
            for v in range(kind.count):
                x = r = None
                for k in range(STEPS + 1):
                    if k == 0:
                        field = slab_load(first_ref, 0, row * kind.pitch, v)
                    elif is_inner(k, row):
                        field = slab_load(inner_ref, 0, INNER_SLOTS[k, row] * kind.pitch, v)
                    else:
                        field = slab_load(outer_ref, 0, OUTER_SLOTS[k, row] * kind.pitch, v)
                    if k < STEPS:
                        x = cx[k] * field if x is None else x + cx[k] * field
                    r = cr[k] * field if r is None else r + cr[k] * field
                xs.append(x)
                rs.append(r)
            return xs, rs

        for top in range(0, ROWS, 8):
            if len(kind.groups) == 2:
                for row in range(8):
                    for which, values in enumerate(combined(top + row)):
                        stage_ref[which, row] = jnp.concatenate(values, axis=0).T
            else:
                for row in range(0, 8, 2):
                    for which, (one, two) in enumerate(
                        zip(combined(top + row), combined(top + row + 1))
                    ):
                        both = jnp.concatenate(one + two, axis=0).T
                        for b in range(BLOCKS):
                            even = both[16 * b:16 * b + 8]
                            odd = both[16 * b + 8:16 * b + 16]
                            half = LANES // 2
                            stage_ref[which, row, 8 * b:8 * b + 8, :] = jnp.where(
                                low_half, even, pltpu.roll(odd, half, 1)
                            )
                            stage_ref[which, row + 1, 8 * b:8 * b + 8, :] = jnp.where(
                                low_half, pltpu.roll(even, half, 1), odd
                            )
            for which, ref in enumerate((x_ref, r_ref)):
                for b in range(BLOCKS):
                    for n, group in enumerate(kind.groups):
                        at = (b * len(kind.groups) + n) * 8
                        block = jnp.swapaxes(stage_ref[which, :, at:at + 8, :], 0, 1)
                        ref[8 * group:8 * group + 8, top:top + 8, b * LANES:(b + 1) * LANES] = block
        for ref, out in ((x_ref, x_out), (r_ref, r_out)):
            part = pl.ds(kind.base, kind.modes)
            copy = pltpu.make_async_copy(ref.at[part], out.at[part], sems.at[len(copies)])
            copy.start()
            copies.append(copy)
    for copy in copies:
        copy.wait()


def solve(sums, helm, firsts, inners, outers):
    out = jax.ShapeDtypeStruct((MODES, ROWS, COLS), f32)
    args = [sums, helm] + [x for trio in zip(firsts, inners, outers) for x in trio]
    return pl.pallas_call(
        solve_kernel,
        grid=(1,),
        in_specs=[full(x.shape) for x in args],
        out_specs=[pl.BlockSpec(memory_space=pl.ANY)] * 2,
        out_shape=[out, out],
        scratch_shapes=[
            pltpu.VMEM((MODES, ROWS, COLS), f32),
            pltpu.VMEM((MODES, ROWS, COLS), f32),
            pltpu.VMEM((2, 8, LANES, LANES), f32),
            pltpu.VMEM((24, LANES), f32),
            pltpu.SemaphoreType.DMA((2 * len(SETS),)),
        ],
        compiler_params=limits(16),
        name="solve",
    )(*args)


def of_everyone(value):
    for stride in (1, 4, 16):
        one, three, two = [
            lax.ppermute(value, "tile", [(i, i ^ (mask * stride)) for i in range(TILES)])
            for mask in (1, 3, 2)
        ]
        value = value + (one + three + two)
    return value


def shards(increments, projection, helmholtz):
    swap_a = [(i, i ^ 1) for i in range(TILES)]
    swap_b = [(i, i + 1) for i in range(1, TILES - 1, 2)]
    swap_b += [(target, source) for source, target in swap_b]
    firsts, halos = turn(modal_product(increments, projection))
    halos = [
        (lax.ppermute(a, "tile", swap_a), lax.ppermute(b, "tile", swap_b)) for a, b in halos
    ]
    inners, parts = inner_basis(firsts)
    moments = jnp.zeros((MOMENTS, LANES), f32)
    outers = {}
    for members, halo in zip(CHUNKS, halos):
        made, moments = outer_basis(members, halo, moments, firsts, inners, parts)
        outers.update(zip(members, made))
    helm = jnp.pad(helmholtz[None], ((0, 0), (0, LANES - MODES)))
    outers = [outers[n] for n in range(len(SETS))]
    return tuple(solve(of_everyone(moments), helm, firsts, inners, outers))


def solution(mesh):
    in_specs = (P("lev", "tile", None), P(), P("lev"))
    out_specs = (P("lev", "tile", None), P("lev", "tile", None))
    return jax.shard_map(shards, mesh=mesh, in_specs=in_specs, out_specs=out_specs, check_vma=False)
```

time: 70.7 us -> 66.5 us (0.941)
  Pallas kernels: 33.3 us -> 26.5 us
  waiting for transfers between devices: 9.48 us -> 10.8 us
  starting transfers between devices: 26.1 us -> 27.3 us
    pallas_call x4 -> x5, Pallas kernels: 24.6 us -> 18.4 us  [the longest x4 12.8 us: call(): pl.pallas_call(kernel, grid=(1,), in_specs=[full(x.shape) for x in args],...]
    ppermute x2, waiting for transfers between devices: 0.01 us -> 1.38 us  [shards(): lax.ppermute(a, 'tile', swap_a)]
    ppermute x9, starting transfers between devices: 18.8 us -> 19.7 us  [of_everyone(): lax.ppermute(value, 'tile', [(i, i ^ mask * stride) for i in range(TILES)])]
  transfers between devices with their start and end apart: 14 -> 14, of which waited for: 6 -> 8; matrix products, arithmetic and copies ran while one was open for 0% -> 0% of each run, Pallas kernels for 26% -> 20%
where the time goes in v3:
time: 66.5 us; the launch traced here: 66.3 us
  starting transfers between devices  27.3 us (41%)
  Pallas kernels  26.5 us (40%)
  waiting for transfers between devices  10.8 us (16%)
  between operations  0.9 us (1%)
  local copies, waits for them, and re-layouts  0.77 us (1%)
    ppermute x9, starting transfers between devices, of_everyone(): lax.ppermute(value, 'tile', [(i, i ^ mask * stride) for i in range(TILES)])  19.7 us
    pallas_call x4, Pallas kernels, call(): pl.pallas_call(kernel, grid=(1,), in_specs=[full(x.shape) for x in args],...  12.8 us
    ppermute x9, waiting for transfers between devices, of_everyone(): lax.ppermute(value, 'tile', [(i, i ^ mask * stride) for i in range(TILES)])  9.46 us
    ppermute x2, starting transfers between devices, shards(): lax.ppermute(a, 'tile', swap_a)  5.93 us
    pallas_call x1, Pallas kernels, solve(): pl.pallas_call(solve_kernel, grid=(1,), in_specs=[full(x.shape) for x in...  5.67 us
    pallas_call x1, Pallas kernels, modal_product(): pl.pallas_call(own_levels_kernel, grid=grid, in_specs=[whole(2 * levels,...  4.94 us
    pallas_call x1, Pallas kernels, modal_product(): pl.pallas_call(other_levels_kernel, grid=grid, in_specs=[whole(count, dep...  3.11 us
    ppermute x2, starting transfers between devices, shards(): lax.ppermute(b, 'tile', swap_b)  1.52 us
  transfers between devices with their start and end apart: 14, of which 8 were waited for; matrix products, arithmetic and copies ran while one was open for 0% of the time, Pallas kernels for 20%

profile of v3, /device:TPU:0, one launch (start us, length us, event | category | flops | bytes accessed | tf_op | source)
XLA Modules:
  0.0 66.3 jit_solution(1254077295911510622)
XLA Ops:
  0.6 0.1 collective-permute-start
  0.7 0.0 copy-start
  0.7 0.8 %copy-done = bf16[80,136]{0,1:T(8,128)(2,1)S(1)} copy-done((bf16[80,136]{0,1:T(8,128)(2,1)S(1)}, bf16[80,136]{0,1:T(8,128)(2,1)}, u32[]{:S(2)}) %copy-start) | copy-done | bytes 21784
  1.5 4.9 %own_levels.1 = (f32[640,1024]{1,0:T(8,128)S(1)}, bf16[640,1088]{1,0:T(8,128)(2,1)S(1)}) custom-call(bf16[136,80]{1,0:T(8,128)(2,1)S(1)} %bitcast.3, bf16[1088,1024]{1,0:T(8,128)(2,1)} %bitcast.5), custom_call_target="tpu_custom_call" | custom-call | tf_op jit(solution)/shard_map/own_levels/pallas_call | solution.py:118
  6.4 0.0 collective-permute-done.inc_ref
  6.4 3.1 %other_levels.1.modal_ref = f32[640,1024]{1,0:T(8,128)S(1)} custom-call(bf16[640,1088]{1,0:T(8,128)(2,1)S(1)} %get-tuple-element.22.left_ref, bf16[1088,1024]{1,0:T(8,128)(2,1)S(1)} %collective-permute-done.inc_ref, f32[640,1024]{1,0:T(8,128)S(1)} %get-tuple-element.23.acc_ref), custom_call_target="tpu_custom_call" | custom-call | tf_op jit(solution)/shard_map/other_levels/pallas_call | solution.py:131
  9.6 1.3 %turn.1 = (f32[1,2184,128]{2,1,0:T(8,128)S(1)}, f32[1,2184,128]{2,1,0:T(8,128)S(1)}, f32[1,1160,128]{2,1,0:T(8,128)S(1)}, bf16[1536,128]{1,0:T(8,128)(2,1)S(1)},...) custom-call(f32[640,1024]{1,0:T(8,128)S(1)} %other_levels.1.modal_ref), custom_call_target="tpu_custom_call" | custom-call | tf_op jit(solution)/shard_map/turn/pallas_call | solution.py:170
  10.9 1.8 %collective-permute-start.3 = (bf16[1536,128]{1,0:T(8,128)(2,1)S(1)}, bf16[1536,128]{1,0:T(8,128)(2,1)S(1)}, u32[]{:S(2)}, u32[]{:S(2)}) collective-permute-start(bf16[1536,128]{1,0:T(8,128)(2,1)S(1)} %get-tuple-element.26), channel_id=1, source_target_pairs={{0,2},{2,0},{4,6},{6,4},{8,10},{10,8},{12,14},{14,12},{16,18},{18,... | collective-permute-start | bytes 1179656 | tf_op jit(solution)/shard_map/ppermute | solution.py:579
  12.7 0.7 %collective-permute-start.4 = (bf16[1536,128]{1,0:T(8,128)(2,1)S(1)}, bf16[1536,128]{1,0:T(8,128)(2,1)S(1)}, u32[]{:S(2)}, u32[]{:S(2)}) collective-permute-start(bf16[1536,128]{1,0:T(8,128)(2,1)S(1)} %get-tuple-element.27), channel_id=1, source_target_pairs={{2,4},{6,8},{10,12},{14,16},{18,20},{22,24},{26,28},{30,32},{34,36... | collective-permute-start | bytes 1179656 | tf_op jit(solution)/shard_map/ppermute | solution.py:579
  13.3 4.2 %collective-permute-start.1 = (bf16[1024,128]{1,0:T(8,128)(2,1)S(1)}, bf16[1024,128]{1,0:T(8,128)(2,1)S(1)}, u32[]{:S(2)}, u32[]{:S(2)}) collective-permute-start(bf16[1024,128]{1,0:T(8,128)(2,1)S(1)} %get-tuple-element.24), channel_id=1, source_target_pairs={{0,2},{2,0},{4,6},{6,4},{8,10},{10,8},{12,14},{14,12},{16,18},{18,... | collective-permute-start | bytes 786440 | tf_op jit(solution)/shard_map/ppermute | solution.py:579
  17.5 0.8 %collective-permute-start.2 = (bf16[1024,128]{1,0:T(8,128)(2,1)S(1)}, bf16[1024,128]{1,0:T(8,128)(2,1)S(1)}, u32[]{:S(2)}, u32[]{:S(2)}) collective-permute-start(bf16[1024,128]{1,0:T(8,128)(2,1)S(1)} %get-tuple-element.25), channel_id=1, source_target_pairs={{2,4},{6,8},{10,12},{14,16},{18,20},{22,24},{26,28},{30,32},{34,36... | collective-permute-start | bytes 786440 | tf_op jit(solution)/shard_map/ppermute | solution.py:579
  18.4 3.5 %inner.1 = (f32[1,7624,128]{2,1,0:T(8,128)S(1)}, f32[1,7624,128]{2,1,0:T(8,128)S(1)}, f32[1,4040,128]{2,1,0:T(8,128)S(1)}, f32[16,128]{1,0:T(8,128)S(1)}, f32[16,128]{1,0:T(8,128)S(1)}, /*index=5*/f32[16,128]{1,0:T(8,128)S(1)}) custom-call(f32[1,2184,128]{2,1,0:T(8,128)S(1)} %get-tuple-element.28.refs_0_, ...), custom_call_target="tpu_custom_call" | custom-call | tf_op jit(solution)/shard_map/inner/pallas_call | solution.py:170
  21.8 1.1 %collective-permute-done.3.a_ref = bf16[1536,128]{1,0:T(8,128)(2,1)S(1)} collective-permute-done((bf16[1536,128]{1,0:T(8,128)(2,1)S(1)}, bf16[1536,128]{1,0:T(8,128)(2,1)S(1)}, u32[]{:S(2)}, u32[]{:S(2)}) %collective-permute-start.3) | collective-permute-done | bytes 393248 | tf_op jit(solution)/shard_map/ppermute | solution.py:579
  23.0 0.0 collective-permute-done.4.b_ref
  23.0 4.9 %outer.2 = (f32[1,9800,128]{2,1,0:T(8,128)S(1)}, f32[1,5192,128]{2,1,0:T(8,128)S(1)}, f32[16,128]{1,0:T(8,128)S(1)}) custom-call(bf16[1536,128]{1,0:T(8,128)(2,1)S(1)} %collective-permute-done.3.a_ref, bf16[1536,128]{1,0:T(8,128)(2,1)S(1)} %collective-permute-done.4.b_ref, f32[16,128]{1,0:T(8,128)S(1)} %broadcast_in_dim.6.known_ref, ...), custom_call_target="tpu_custom_call" | custom-call | tf_op jit(solution)/shard_map/outer/pallas_call | solution.py:170
  27.9 0.2 collective-permute-done.1.a_ref
  28.1 0.0 collective-permute-done.2.b_ref
  28.1 0.0 copy-start.1
  28.1 3.1 %outer.3 = (f32[1,9800,128]{2,1,0:T(8,128)S(1)}, f32[16,128]{1,0:T(8,128)S(1)}) custom-call(bf16[1024,128]{1,0:T(8,128)(2,1)S(1)} %collective-permute-done.1.a_ref, bf16[1024,128]{1,0:T(8,128)(2,1)S(1)} %collective-permute-done.2.b_ref, f32[16,128]{1,0:T(8,128)S(1)} %get-tuple-element.35.known_ref, ...), custom_call_target="tpu_custom_call" | custom-call | tf_op jit(solution)/shard_map/outer/pallas_call | solution.py:170
  31.2 6.3 %collective-permute-start.7 = (f32[16,128]{1,0:T(8,128)S(1)}, f32[16,128]{1,0:T(8,128)S(1)}, u32[]{:S(2)}, u32[]{:S(2)}) collective-permute-start(f32[16,128]{1,0:T(8,128)S(1)} %get-tuple-element.38), channel_id=1, source_target_pairs={{0,4},{2,6},{4,0},{6,2},{8,12},{10,14},{12,8},{14,10},{16,20},{18,... | collective-permute-start | bytes 24584 | tf_op jit(solution)/shard_map/ppermute | solution.py:566
  37.5 1.5 %collective-permute-start.6 = (f32[16,128]{1,0:T(8,128)S(1)}, f32[16,128]{1,0:T(8,128)S(1)}, u32[]{:S(2)}, u32[]{:S(2)}) collective-permute-start(f32[16,128]{1,0:T(8,128)S(1)} %get-tuple-element.38), channel_id=1, source_target_pairs={{0,6},{2,4},{4,2},{6,0},{8,14},{10,12},{12,10},{14,8},{16,22},{18,... | collective-permute-start | bytes 24584 | tf_op jit(solution)/shard_map/ppermute | solution.py:566
  39.0 0.8 %collective-permute-start.5 = (f32[16,128]{1,0:T(8,128)S(1)}, f32[16,128]{1,0:T(8,128)S(1)}, u32[]{:S(2)}, u32[]{:S(2)}) collective-permute-start(f32[16,128]{1,0:T(8,128)S(1)} %get-tuple-element.38), channel_id=1, source_target_pairs={{0,2},{2,0},{4,6},{6,4},{8,10},{10,8},{12,14},{14,12},{16,18},{18,... | collective-permute-start | bytes 24584 | tf_op jit(solution)/shard_map/ppermute | solution.py:566
  39.8 0.0 collective-permute-done.7
  39.8 2.6 %collective-permute-done.6 = f32[16,128]{1,0:T(8,128)S(1)} collective-permute-done((f32[16,128]{1,0:T(8,128)S(1)}, f32[16,128]{1,0:T(8,128)S(1)}, u32[]{:S(2)}, u32[]{:S(2)}) %collective-permute-start.6) | collective-permute-done | bytes 8224 | tf_op jit(solution)/shard_map/ppermute | solution.py:566
  42.4 0.3 collective-permute-done.5
  42.6 3.9 %collective-permute-start.10 = (f32[16,128]{1,0:T(8,128)S(1)}, f32[16,128]{1,0:T(8,128)S(1)}, u32[]{:S(2)}, u32[]{:S(2)}) collective-permute-start(f32[16,128]{1,0:T(8,128)S(1)} %add_add_fusion.2), channel_id=1, source_target_pairs={{0,16},{2,18},{4,20},{6,22},{8,24},{10,26},{12,28},{14,30},{16,0},... | collective-permute-start | bytes 24584 | tf_op jit(solution)/shard_map/ppermute | solution.py:566
  46.5 2.3 %collective-permute-start.9 = (f32[16,128]{1,0:T(8,128)S(1)}, f32[16,128]{1,0:T(8,128)S(1)}, u32[]{:S(2)}, u32[]{:S(2)}) collective-permute-start(f32[16,128]{1,0:T(8,128)S(1)} %add_add_fusion.2), channel_id=1, source_target_pairs={{0,24},{2,26},{4,28},{6,30},{8,16},{10,18},{12,20},{14,22},{16,8},... | collective-permute-start | bytes 24584 | tf_op jit(solution)/shard_map/ppermute | solution.py:566
  48.9 0.8 %collective-permute-start.8 = (f32[16,128]{1,0:T(8,128)S(1)}, f32[16,128]{1,0:T(8,128)S(1)}, u32[]{:S(2)}, u32[]{:S(2)}) collective-permute-start(f32[16,128]{1,0:T(8,128)S(1)} %add_add_fusion.2), channel_id=1, source_target_pairs={{0,8},{2,10},{4,12},{6,14},{8,0},{10,2},{12,4},{14,6},{16,24},{18,... | collective-permute-start | bytes 24584 | tf_op jit(solution)/shard_map/ppermute | solution.py:566
  49.6 0.0 collective-permute-done.10
  49.6 1.7 %collective-permute-done.9 = f32[16,128]{1,0:T(8,128)S(1)} collective-permute-done((f32[16,128]{1,0:T(8,128)S(1)}, f32[16,128]{1,0:T(8,128)S(1)}, u32[]{:S(2)}, u32[]{:S(2)}) %collective-permute-start.9) | collective-permute-done | bytes 8224 | tf_op jit(solution)/shard_map/ppermute | solution.py:566
  51.4 1.1 %collective-permute-done.8 = f32[16,128]{1,0:T(8,128)S(1)} collective-permute-done((f32[16,128]{1,0:T(8,128)S(1)}, f32[16,128]{1,0:T(8,128)S(1)}, u32[]{:S(2)}, u32[]{:S(2)}) %collective-permute-start.8) | collective-permute-done | bytes 8224 | tf_op jit(solution)/shard_map/ppermute | solution.py:566
  52.5 3.0 %collective-permute-start.13 = (f32[16,128]{1,0:T(8,128)S(1)}, f32[16,128]{1,0:T(8,128)S(1)}, u32[]{:S(2)}, u32[]{:S(2)}) collective-permute-start(f32[16,128]{1,0:T(8,128)S(1)} %add_add_fusion.1), channel_id=1, source_target_pairs={{0,64},{2,66},{4,68},{6,70},{8,72},{10,74},{12,76},{14,78},{16,80}... | collective-permute-start | bytes 24584 | tf_op jit(solution)/shard_map/ppermute | solution.py:566
  55.5 1.1 %collective-permute-start.12 = (f32[16,128]{1,0:T(8,128)S(1)}, f32[16,128]{1,0:T(8,128)S(1)}, u32[]{:S(2)}, u32[]{:S(2)}) collective-permute-start(f32[16,128]{1,0:T(8,128)S(1)} %add_add_fusion.1), channel_id=1, source_target_pairs={{0,96},{2,98},{4,100},{6,102},{8,104},{10,106},{12,108},{14,110},{... | collective-permute-start | bytes 24584 | tf_op jit(solution)/shard_map/ppermute | solution.py:566
  56.7 0.0 collective-permute-start.11
  56.7 0.0 copy-done.1
  56.7 1.0 %collective-permute-done.13 = f32[16,128]{1,0:T(8,128)S(1)} collective-permute-done((f32[16,128]{1,0:T(8,128)S(1)}, f32[16,128]{1,0:T(8,128)S(1)}, u32[]{:S(2)}, u32[]{:S(2)}) %collective-permute-start.13) | collective-permute-done | bytes 8224 | tf_op jit(solution)/shard_map/ppermute | solution.py:566
  57.7 2.7 %collective-permute-done.12 = f32[16,128]{1,0:T(8,128)S(1)} collective-permute-done((f32[16,128]{1,0:T(8,128)S(1)}, f32[16,128]{1,0:T(8,128)S(1)}, u32[]{:S(2)}, u32[]{:S(2)}) %collective-permute-start.12) | collective-permute-done | bytes 8224 | tf_op jit(solution)/shard_map/ppermute | solution.py:566
  60.4 0.0 collective-permute-done.11
  60.4 5.7 %solve.1 = (f32[40,16,1024]{2,1,0:T(8,128)}, f32[40,16,1024]{2,1,0:T(8,128)}) custom-call(f32[16,128]{1,0:T(8,128)S(1)} %add_add_fusion.sums_ref, f32[1,128]{1,0:T(1,128)S(1)} %pad.4.helm_ref, f32[1,2184,128]{2,1,0:T(8,128)S(1)} %get-tuple-element.28.refs_0_, f32[1,7624,128]{2,1,0:T(8,128)S(1)} %get-tuple-element.31.refs_1_, ...), custom_call_target="tpu_custom_call" | custom-call | tf_op jit(solution)/shard_map/solve/pallas_call | solution.py:545
  (5 shorter events, 0.0 us)
Async XLA Ops:
  0.6 5.8 %collective-permute-start = (bf16[1088,1024]{1,0:T(8,128)(2,1)}, bf16[1088,1024]{1,0:T(8,128)(2,1)S(1)}, u32[]{:S(2)}, u32[]{:S(2)}) collective-permute-start(bf16[1088,1024]{1,0:T(8,128)(2,1)} %bitcast.4), channel_id=1, source_target_pairs={{0,1},{1,0},{2,3},{3,2},{4,5},{5,4},{6,7},{7,6},{8,9},{9,8},{10,11... | collective-permute-start | bytes 6684680 | tf_op jit(solution)/shard_map/ppermute | solution.py:112
  0.7 0.8 %copy-start = (bf16[80,136]{0,1:T(8,128)(2,1)S(1)}, bf16[80,136]{0,1:T(8,128)(2,1)}, u32[]{:S(2)}) copy-start(bf16[80,136]{0,1:T(8,128)(2,1)} %param.4) | copy-start | bytes 65284
  10.9 12.1 %collective-permute-start.3 = (bf16[1536,128]{1,0:T(8,128)(2,1)S(1)}, bf16[1536,128]{1,0:T(8,128)(2,1)S(1)}, u32[]{:S(2)}, u32[]{:S(2)}) collective-permute-start(bf16[1536,128]{1,0:T(8,128)(2,1)S(1)} %get-tuple-element.26), channel_id=1, source_target_pairs={{0,2},{2,0},{4,6},{6,4},{8,10},{10,8},{12,14},{14,12},{16,18},{18,... | collective-permute-start | bytes 1179656 | tf_op jit(solution)/shard_map/ppermute | solution.py:579
  12.7 10.3 %collective-permute-start.4 = (bf16[1536,128]{1,0:T(8,128)(2,1)S(1)}, bf16[1536,128]{1,0:T(8,128)(2,1)S(1)}, u32[]{:S(2)}, u32[]{:S(2)}) collective-permute-start(bf16[1536,128]{1,0:T(8,128)(2,1)S(1)} %get-tuple-element.27), channel_id=1, source_target_pairs={{2,4},{6,8},{10,12},{14,16},{18,20},{22,24},{26,28},{30,32},{34,36... | collective-permute-start | bytes 1179656 | tf_op jit(solution)/shard_map/ppermute | solution.py:579
  13.3 14.8 %collective-permute-start.1 = (bf16[1024,128]{1,0:T(8,128)(2,1)S(1)}, bf16[1024,128]{1,0:T(8,128)(2,1)S(1)}, u32[]{:S(2)}, u32[]{:S(2)}) collective-permute-start(bf16[1024,128]{1,0:T(8,128)(2,1)S(1)} %get-tuple-element.24), channel_id=1, source_target_pairs={{0,2},{2,0},{4,6},{6,4},{8,10},{10,8},{12,14},{14,12},{16,18},{18,... | collective-permute-start | bytes 786440 | tf_op jit(solution)/shard_map/ppermute | solution.py:579
  17.5 10.6 %collective-permute-start.2 = (bf16[1024,128]{1,0:T(8,128)(2,1)S(1)}, bf16[1024,128]{1,0:T(8,128)(2,1)S(1)}, u32[]{:S(2)}, u32[]{:S(2)}) collective-permute-start(bf16[1024,128]{1,0:T(8,128)(2,1)S(1)} %get-tuple-element.25), channel_id=1, source_target_pairs={{2,4},{6,8},{10,12},{14,16},{18,20},{22,24},{26,28},{30,32},{34,36... | collective-permute-start | bytes 786440 | tf_op jit(solution)/shard_map/ppermute | solution.py:579
  28.1 28.6 %copy-start.1 = (f32[40]{0:T(128)S(1)}, f32[40]{0:T(128)}, u32[]{:S(2)}) copy-start(f32[40]{0:T(128)} %param.5) | copy-start | bytes 484
  31.2 8.6 %collective-permute-start.7 = (f32[16,128]{1,0:T(8,128)S(1)}, f32[16,128]{1,0:T(8,128)S(1)}, u32[]{:S(2)}, u32[]{:S(2)}) collective-permute-start(f32[16,128]{1,0:T(8,128)S(1)} %get-tuple-element.38), channel_id=1, source_target_pairs={{0,4},{2,6},{4,0},{6,2},{8,12},{10,14},{12,8},{14,10},{16,20},{18,... | collective-permute-start | bytes 24584 | tf_op jit(solution)/shard_map/ppermute | solution.py:566
  37.5 4.9 %collective-permute-start.6 = (f32[16,128]{1,0:T(8,128)S(1)}, f32[16,128]{1,0:T(8,128)S(1)}, u32[]{:S(2)}, u32[]{:S(2)}) collective-permute-start(f32[16,128]{1,0:T(8,128)S(1)} %get-tuple-element.38), channel_id=1, source_target_pairs={{0,6},{2,4},{4,2},{6,0},{8,14},{10,12},{12,10},{14,8},{16,22},{18,... | collective-permute-start | bytes 24584 | tf_op jit(solution)/shard_map/ppermute | solution.py:566
  39.0 3.7 %collective-permute-start.5 = (f32[16,128]{1,0:T(8,128)S(1)}, f32[16,128]{1,0:T(8,128)S(1)}, u32[]{:S(2)}, u32[]{:S(2)}) collective-permute-start(f32[16,128]{1,0:T(8,128)S(1)} %get-tuple-element.38), channel_id=1, source_target_pairs={{0,2},{2,0},{4,6},{6,4},{8,10},{10,8},{12,14},{14,12},{16,18},{18,... | collective-permute-start | bytes 24584 | tf_op jit(solution)/shard_map/ppermute | solution.py:566
  42.6 7.0 %collective-permute-start.10 = (f32[16,128]{1,0:T(8,128)S(1)}, f32[16,128]{1,0:T(8,128)S(1)}, u32[]{:S(2)}, u32[]{:S(2)}) collective-permute-start(f32[16,128]{1,0:T(8,128)S(1)} %add_add_fusion.2), channel_id=1, source_target_pairs={{0,16},{2,18},{4,20},{6,22},{8,24},{10,26},{12,28},{14,30},{16,0},... | collective-permute-start | bytes 24584 | tf_op jit(solution)/shard_map/ppermute | solution.py:566
  46.5 4.9 %collective-permute-start.9 = (f32[16,128]{1,0:T(8,128)S(1)}, f32[16,128]{1,0:T(8,128)S(1)}, u32[]{:S(2)}, u32[]{:S(2)}) collective-permute-start(f32[16,128]{1,0:T(8,128)S(1)} %add_add_fusion.2), channel_id=1, source_target_pairs={{0,24},{2,26},{4,28},{6,30},{8,16},{10,18},{12,20},{14,22},{16,8},... | collective-permute-start | bytes 24584 | tf_op jit(solution)/shard_map/ppermute | solution.py:566
  48.9 3.7 %collective-permute-start.8 = (f32[16,128]{1,0:T(8,128)S(1)}, f32[16,128]{1,0:T(8,128)S(1)}, u32[]{:S(2)}, u32[]{:S(2)}) collective-permute-start(f32[16,128]{1,0:T(8,128)S(1)} %add_add_fusion.2), channel_id=1, source_target_pairs={{0,8},{2,10},{4,12},{6,14},{8,0},{10,2},{12,4},{14,6},{16,24},{18,... | collective-permute-start | bytes 24584 | tf_op jit(solution)/shard_map/ppermute | solution.py:566
  52.5 5.2 %collective-permute-start.13 = (f32[16,128]{1,0:T(8,128)S(1)}, f32[16,128]{1,0:T(8,128)S(1)}, u32[]{:S(2)}, u32[]{:S(2)}) collective-permute-start(f32[16,128]{1,0:T(8,128)S(1)} %add_add_fusion.1), channel_id=1, source_target_pairs={{0,64},{2,66},{4,68},{6,70},{8,72},{10,74},{12,76},{14,78},{16,80}... | collective-permute-start | bytes 24584 | tf_op jit(solution)/shard_map/ppermute | solution.py:566
  55.5 4.9 %collective-permute-start.12 = (f32[16,128]{1,0:T(8,128)S(1)}, f32[16,128]{1,0:T(8,128)S(1)}, u32[]{:S(2)}, u32[]{:S(2)}) collective-permute-start(f32[16,128]{1,0:T(8,128)S(1)} %add_add_fusion.1), channel_id=1, source_target_pairs={{0,96},{2,98},{4,100},{6,102},{8,104},{10,106},{12,108},{14,110},{... | collective-permute-start | bytes 24584 | tf_op jit(solution)/shard_map/ppermute | solution.py:566
  56.7 3.7 %collective-permute-start.11 = (f32[16,128]{1,0:T(8,128)S(1)}, f32[16,128]{1,0:T(8,128)S(1)}, u32[]{:S(2)}, u32[]{:S(2)}) collective-permute-start(f32[16,128]{1,0:T(8,128)S(1)} %add_add_fusion.1), channel_id=1, source_target_pairs={{0,32},{2,34},{4,36},{6,38},{8,40},{10,42},{12,44},{14,46},{16,48}... | collective-permute-start | bytes 24584 | tf_op jit(solution)/shard_map/ppermute | solution.py:566

commit v4 on v3

--- a/solution.py
+++ b/solution.py
@@ -44,9 +44,8 @@
     return pltpu.CompilerParams(vmem_limit_bytes=mib * 2**20)
 
 
-def build_left(proj_ref, left_ref, level0):
+def spread_projection(proj_ref, level0, depth):
     lev = lax.axis_index("lev")
-    depth = left_ref.shape[1]
     pick = (
         lax.broadcasted_iota(jnp.int32, (MODES, 2 * MODES), 1)
         == lax.broadcasted_iota(jnp.int32, (MODES, 2 * MODES), 0) + lev * MODES
@@ -59,29 +58,49 @@
         lax.broadcasted_iota(jnp.int32, (levels, depth), 0)
         == (lax.broadcasted_iota(jnp.int32, (levels, depth), 1) >> 4) + level0
     ).astype(bf16)
-    wide = jnp.dot(own, spread, preferred_element_type=f32)
-    row_of = lax.broadcasted_iota(jnp.int32, (8, depth), 1) & (ROWS - 1)
-    for group in range(GROUPS):
-        part = wide[group * 8:(group + 1) * 8]
-        for row in range(0, ROWS, 2):
-            two = jnp.concatenate(
-                [jnp.where(row_of == row, part, 0.0), jnp.where(row_of == row + 1, part, 0.0)],
-                axis=0,
-            )
-            at = group * 8 * ROWS + row * 8
-            left_ref[at:at + 16, :] = two.astype(bf16)
-
-
-def own_levels_kernel(proj_ref, inc_ref, acc_ref, other_left_ref, left_ref):
+    return jnp.dot(own, spread, preferred_element_type=f32)
+
+
+def build_left(wide, left_refs):
+    row_of = lax.broadcasted_iota(jnp.int32, (8, wide.shape[1]), 1) & (ROWS - 1)
+    for members, ref in zip(CHUNKS, left_refs):
+        at = 0
+        for group in groups_of(members):
+            part = wide[group * 8:(group + 1) * 8]
+            for row in range(0, ROWS, 2):
+                two = jnp.concatenate(
+                    [jnp.where(row_of == row, part, 0.0), jnp.where(row_of == row + 1, part, 0.0)],
+                    axis=0,
+                )
+                ref[at:at + 16, :] = two.astype(bf16)
+                at += 16
+
+
+def groups_of(members):
+    return [group for member in members for group in SETS[member].groups]
+
+
+def own_levels_kernel(proj_ref, inc_ref, *refs):
     lev = lax.axis_index("lev")
     count = proj_ref.shape[0] // 2
+    parts = len(CHUNKS)
+    acc_refs, other_refs, left_refs = refs[:parts], refs[parts:2 * parts], refs[2 * parts:]
+    depth = left_refs[0].shape[1]
 
     @pl.when(pl.program_id(0) == 0)
     def _():
-        build_left(proj_ref, left_ref, lev * count)
-        build_left(proj_ref, other_left_ref, (1 - lev) * count)
-
-    acc_ref[...] = jnp.dot(left_ref[...], inc_ref[...], preferred_element_type=f32)
+        build_left(spread_projection(proj_ref, lev * count, depth), left_refs)
+
+    @pl.when(pl.program_id(0) == pl.num_programs(0) - 1)
+    def _():
+        build_left(spread_projection(proj_ref, (1 - lev) * count, depth), other_refs)
+        for acc_ref, left_ref in zip(acc_refs, left_refs):
+            acc_ref[...] = jnp.dot(left_ref[...], inc_ref[...], preferred_element_type=f32)
+
+    @pl.when(pl.program_id(0) < pl.num_programs(0) - 1)
+    def _():
+        for acc_ref, left_ref in zip(acc_refs, left_refs):
+            acc_ref[...] = jnp.dot(left_ref[...], inc_ref[...], preferred_element_type=f32)
 
 
 def coded(x):
@@ -112,31 +131,33 @@
     arrived = lax.ppermute(flat, "lev", [(0, 1), (1, 0)])
     width = 256
     grid = (COLS // width,)
-    count = MODES * ROWS
+    sizes = [8 * ROWS * len(groups_of(members)) for members in CHUNKS]
     column = lambda rows: pl.BlockSpec((rows, width), lambda c: (0, c))
     whole = lambda rows, cols: pl.BlockSpec((rows, cols), lambda c: (0, 0))
-    acc, other_left = pl.pallas_call(
+    in_hbm = lambda x: pltpu.with_memory_space_constraint(x, pltpu.HBM)
+    made = pl.pallas_call(
         own_levels_kernel,
         grid=grid,
         in_specs=[whole(2 * levels, 2 * MODES), column(depth)],
-        out_specs=[column(count), whole(count, depth)],
-        out_shape=[
-            jax.ShapeDtypeStruct((count, COLS), f32),
-            jax.ShapeDtypeStruct((count, depth), bf16),
-        ],
-        scratch_shapes=[pltpu.VMEM((count, depth), bf16)],
+        out_specs=[column(n) for n in sizes] + [whole(n, depth) for n in sizes],
+        out_shape=[jax.ShapeDtypeStruct((n, COLS), f32) for n in sizes]
+        + [jax.ShapeDtypeStruct((n, depth), bf16) for n in sizes],
+        scratch_shapes=[pltpu.VMEM((n, depth), bf16) for n in sizes],
         compiler_params=limits(20),
         name="own_levels",
-    )(projection.T, pltpu.with_memory_space_constraint(flat, pltpu.HBM))
-    return pl.pallas_call(
-        other_levels_kernel,
-        grid=grid,
-        in_specs=[whole(count, depth), column(depth), column(count)],
-        out_specs=column(count),
-        out_shape=jax.ShapeDtypeStruct((count, COLS), f32),
-        compiler_params=limits(20),
-        name="other_levels",
-    )(other_left, arrived, acc)
+    )(in_hbm(projection.T), in_hbm(flat))
+    return [
+        pl.pallas_call(
+            other_levels_kernel,
+            grid=grid,
+            in_specs=[whole(n, depth), column(depth), column(n)],
+            out_specs=column(n),
+            out_shape=jax.ShapeDtypeStruct((n, COLS), f32),
+            compiler_params=limits(20),
+            name="other_levels",
+        )(made[len(sizes) + part], arrived, made[part])
+        for part, n in enumerate(sizes)
+    ]
 
 
 def lanes():
@@ -153,12 +174,16 @@
 
 
 def slab_store(ref, lead, at, v, value):
-    ref[lead, at + 8 + 8 * v:at + 16 + 8 * v, :] = value
-
-
-def slab_load(ref, lead, at, v, offset=0):
+    start = at + 8 + 8 * v
+    ref[lead, start:start + value.shape[0], :] = value
+
+
+def slab_load(ref, lead, at, v, offset=0, count=1):
     start = at + 8 + 8 * v + offset
-    return ref[lead, start:start + 8, :]
+    if offset == 0 or count == 1:
+        return ref[lead, start:start + 8 * count, :]
+    parts = [ref[lead, start + 8 * n:start + 8 * n + 8, :] for n in range(count)]
+    return jnp.concatenate(parts, axis=0)
 
 
 def full(shape):
@@ -180,63 +205,54 @@
     return call
 
 
-def turn_kernel(modal_ref, *refs):
+def turn_kernel(members, modal_ref, *refs):
     even = (lax.axis_index("tile") & 1) == 0
-    first_refs, halo_refs = refs[:len(SETS)], refs[len(SETS):]
-    for part, members in enumerate(CHUNKS):
-        a_ref, b_ref = halo_refs[2 * part:2 * part + 2]
-        offset = 0
-        for member in members:
-            kind = SETS[member]
-
-            ref = first_refs[member]
-
-            def columns(row):
-                parts = []
-                for b in range(BLOCKS):
-                    for group in kind.groups:
-                        at = (group * ROWS + row) * 8
-                        value = modal_ref[at:at + 8, b * LANES:(b + 1) * LANES]
-                        parts.append(value)
-                        if len(kind.groups) == 1:
-                            parts.append(pltpu.roll(value, LANES // 2, 1))
-                return jnp.concatenate(parts, axis=0)
-
-            ready = [columns(row) for row in range(4)]
-            for row in range(ROWS):
-                whole = ready.pop(0).T
-                if row + 4 < ROWS:
-                    ready.append(columns(row + 4))
-                for v in range(kind.count):
-                    slab_store(ref, 0, row * kind.pitch, v, whole[8 * v:8 * v + 8])
-            for row in range(HALO):
-                for v in range(0, kind.count, 2):
-                    at = offset + row * kind.length + 8 * v
-                    low, high = [
-                        coded(jnp.concatenate(
-                            [slab_load(ref, 0, start * kind.pitch, v + n) for n in range(2)], axis=0
-                        ))
-                        for start in (row, row + HALO)
-                    ]
-                    a_ref[at:at + 16, :] = jnp.where(even, high, low)
-                    b_ref[at:at + 16, :] = jnp.where(even, low, high)
-            for row in range(ROWS):
-                at = row * kind.pitch
-                slab_ends(
-                    ref, 0, at, kind, slab_load(ref, 0, at, 0), slab_load(ref, 0, at, kind.count - 1)
-                )
-            offset += HALO * kind.length
-
-
-def turn(modal):
-    firsts = [jax.ShapeDtypeStruct((1, kind.rows(ROWS), LANES), f32) for kind in SETS]
-    halos = [
-        jax.ShapeDtypeStruct((sum(HALO * SETS[m].length for m in members), LANES), bf16)
-        for members in CHUNKS for _ in range(2)
-    ]
-    out = single(turn_kernel, firsts + halos, "turn")(modal)
-    halos = out[len(SETS):]
-    return out[:len(SETS)], list(zip(halos[::2], halos[1::2]))
+    first_refs, (a_ref, b_ref) = refs[:len(members)], refs[len(members):]
+    places = {group: n for n, group in enumerate(groups_of(members))}
+    offset = 0
+    for n, member in enumerate(members):
+        kind = SETS[member]
+        ref = first_refs[n]
+
+        def columns(row):
+            parts = []
+            for b in range(BLOCKS):
+                for group in kind.groups:
+                    at = (places[group] * ROWS + row) * 8
+                    value = modal_ref[at:at + 8, b * LANES:(b + 1) * LANES]
+                    parts.append(value)
+                    if len(kind.groups) == 1:
+                        parts.append(pltpu.roll(value, LANES // 2, 1))
+            return jnp.concatenate(parts, axis=0)
+
+        ready = [columns(row) for row in range(4)]
+        for row in range(ROWS):
+            whole = ready.pop(0).T
+            if row + 4 < ROWS:
+                ready.append(columns(row + 4))
+            slab_store(ref, 0, row * kind.pitch, 0, whole[:kind.length])
+        for row in range(HALO):
+            at = offset + row * kind.length
+            low, high = [
+                coded(slab_load(ref, 0, start * kind.pitch, 0, 0, kind.count))
+                for start in (row, row + HALO)
+            ]
+            a_ref[at:at + kind.length, :] = jnp.where(even, high, low)
+            b_ref[at:at + kind.length, :] = jnp.where(even, low, high)
+        for row in range(ROWS):
+            at = row * kind.pitch
+            slab_ends(
+                ref, 0, at, kind, slab_load(ref, 0, at, 0), slab_load(ref, 0, at, kind.count - 1)
+            )
+        offset += HALO * kind.length
+
+
+def turn(members, modal):
+    outs = [jax.ShapeDtypeStruct((1, SETS[m].rows(ROWS), LANES), f32) for m in members]
+    edge = sum(HALO * SETS[m].length for m in members)
+    outs += [jax.ShapeDtypeStruct((edge, LANES), bf16)] * 2
+    out = single(functools.partial(turn_kernel, members), outs, "turn")(modal)
+    return out[:-2], out[-2:]
 
 
 def is_inner(order, row):
@@ -253,36 +269,31 @@
 
 def sweep(kind, order, begin, end, place, sums, factor_of):
     for strip in range(0, kind.count, STRIP):
-        span = range(strip, strip + STRIP)
-        near = lambda row: [slab_load(*place(order - 1, row), v) for v in span]
+        near = lambda row: slab_load(*place(order - 1, row), strip, 0, STRIP)
         above, here = near(begin - 1), near(begin)
         for row in range(begin, end):
             below = near(row + 1)
-            factor = factor_of(row)
-            squares, crosses = [], []
-            for n, v in enumerate(span):
-                left = slab_load(*place(order - 1, row), v, -1)
-                right = slab_load(*place(order - 1, row), v, 1)
-                value = ((above[n] + below[n]) + (left + right)) * factor
-                if order > 1:
-                    value = value - slab_load(*place(order - 2, row), v)
-                ref, lead, at = place(order, row)
-                slab_store(ref, lead, at, v, value)
-                if v == kind.count - 1:
-                    slab_ends(ref, lead, at, kind, slab_load(ref, lead, at, 0), value)
-                squares.append(value * value)
-                crosses.append(value * here[n])
+            left = slab_load(*place(order - 1, row), strip, -1, STRIP)
+            right = slab_load(*place(order - 1, row), strip, 1, STRIP)
+            value = ((above + below) + (left + right)) * factor_of(row)
+            if order > 1:
+                value = value - slab_load(*place(order - 2, row), strip, 0, STRIP)
+            ref, lead, at = place(order, row)
+            slab_store(ref, lead, at, strip, value)
+            if strip + STRIP == kind.count:
+                slab_ends(ref, lead, at, kind, slab_load(ref, lead, at, 0), value[-8:])
             if 0 <= row < ROWS:
                 if 2 * order < MOMENTS:
-                    accumulate(sums, 2 * order, total(squares))
-                accumulate(sums, 2 * order - 1, total(crosses))
+                    accumulate(sums, 2 * order, total(value * value))
+                accumulate(sums, 2 * order - 1, total(value * here))
             above, here = here, below
 
 
 def total(values):
-    while len(values) > 1:
-        values = [values[i] + values[i + 1] for i in range(0, len(values), 2)]
-    return values[0]
+    parts = [values[at:at + 8] for at in range(0, values.shape[0], 8)]
+    while len(parts) > 1:
+        parts = [parts[i] + parts[i + 1] for i in range(0, len(parts), 2)]
+    return parts[0]
 
 
 def accumulate(sums, index, value):
@@ -301,8 +312,8 @@
 
         sums = {}
         for row in range(ROWS):
-            values = [slab_load(*place(0, row), v) for v in range(kind.count)]
-            accumulate(sums, 0, total([v * v for v in values]))
+            values = slab_load(*place(0, row), 0, 0, kind.count)
+            accumulate(sums, 0, total(values * values))
         for order in range(1, STEPS):
             factor = 0.25 if order == 1 else 0.5
             sweep(kind, order, order, ROWS - order, place, sums, lambda row: factor)
@@ -337,18 +348,12 @@
         first_ref, inner_ref, part_ref = ins[3 * n:3 * n + 3]
         outer_ref, halo_ref = outs[n], halo_refs[n]
         for row in range(HALO):
-            for v in range(0, kind.count, 2):
-                at = offset + row * kind.length + 8 * v
-                a = decoded(a_ref[at:at + 16, :])
-                b = decoded(b_ref[at:at + 16, :])
-                for side, both in ((0, jnp.where(even, b, a)), (3, jnp.where(even, a, b))):
-                    slab_store(halo_ref, side, row * kind.pitch, v, both[:8])
-                    slab_store(halo_ref, side, row * kind.pitch, v + 1, both[8:])
-                    if v == 0:
-                        first = {} if side == 0 else first
-                        first[side] = both[:8]
-                    if v + 2 == kind.count:
-                        slab_ends(halo_ref, side, row * kind.pitch, kind, first[side], both[8:])
+            at = offset + row * kind.length
+            a = decoded(a_ref[at:at + kind.length, :])
+            b = decoded(b_ref[at:at + kind.length, :])
+            for side, value in ((0, jnp.where(even, b, a)), (3, jnp.where(even, a, b))):
+                slab_store(halo_ref, side, row * kind.pitch, 0, value)
+                slab_ends(halo_ref, side, row * kind.pitch, kind, value[:8], value[-8:])
         offset += HALO * kind.length
 
         def place(order, row):
@@ -482,38 +487,40 @@
         while step < LANES:
             own = own + pltpu.roll(own, step, 1)
             step *= 2
-        spread = [jnp.broadcast_to(own[k:k + 1, :], (8, LANES)) for k in range(2 * STEPS + 1)]
+        spread = [jnp.broadcast_to(own[k:k + 1, :], (8, LANES))[None] for k in range(2 * STEPS + 1)]
         cx, cr = spread[:STEPS], spread[STEPS:]
 
         def combined(row):
             xs, rs = [], []
-            for v in range(kind.count):
+            for strip in range(0, kind.count, STRIP):
                 x = r = None
                 for k in range(STEPS + 1):
                     if k == 0:
-                        field = slab_load(first_ref, 0, row * kind.pitch, v)
+                        ref, slot = first_ref, row
                     elif is_inner(k, row):
-                        field = slab_load(inner_ref, 0, INNER_SLOTS[k, row] * kind.pitch, v)
+                        ref, slot = inner_ref, INNER_SLOTS[k, row]
                     else:
-                        field = slab_load(outer_ref, 0, OUTER_SLOTS[k, row] * kind.pitch, v)
+                        ref, slot = outer_ref, OUTER_SLOTS[k, row]
+                    field = slab_load(ref, 0, slot * kind.pitch, strip, 0, STRIP)
+                    field = field.reshape(STRIP, 8, LANES)
                     if k < STEPS:
                         x = cx[k] * field if x is None else x + cx[k] * field
                     r = cr[k] * field if r is None else r + cr[k] * field
-                xs.append(x)
-                rs.append(r)
-            return xs, rs
+                xs.append(x.reshape(STRIP * 8, LANES))
+                rs.append(r.reshape(STRIP * 8, LANES))
+            return jnp.concatenate(xs, axis=0), jnp.concatenate(rs, axis=0)
 
         for top in range(0, ROWS, 8):
             if len(kind.groups) == 2:
                 for row in range(8):
                     for which, values in enumerate(combined(top + row)):
-                        stage_ref[which, row] = jnp.concatenate(values, axis=0).T
+                        stage_ref[which, row] = values.T
             else:
                 for row in range(0, 8, 2):
                     for which, (one, two) in enumerate(
                         zip(combined(top + row), combined(top + row + 1))
                     ):
-                        both = jnp.concatenate(one + two, axis=0).T
+                        both = jnp.concatenate([one, two], axis=0).T
                         for b in range(BLOCKS):
                             even = both[16 * b:16 * b + 8]
                             odd = both[16 * b + 8:16 * b + 16]
@@ -574,10 +581,13 @@
     swap_a = [(i, i ^ 1) for i in range(TILES)]
     swap_b = [(i, i + 1) for i in range(1, TILES - 1, 2)]
     swap_b += [(target, source) for source, target in swap_b]
-    firsts, halos = turn(modal_product(increments, projection))
-    halos = [
-        (lax.ppermute(a, "tile", swap_a), lax.ppermute(b, "tile", swap_b)) for a, b in halos
-    ]
+    firsts, halos = {}, []
+    for members, modal in zip(CHUNKS, modal_product(increments, projection)):
+        made, (a, b) = turn(members, modal)
+        firsts.update(zip(members, made))
+        a = lax.ppermute(a, "tile", swap_a)
+        halos.append((a, lax.ppermute(b, "tile", swap_b)))
+    firsts = [firsts[n] for n in range(len(SETS))]
     inners, parts = inner_basis(firsts)
     moments = jnp.zeros((MOMENTS, LANES), f32)
     outers = {}

time: 66.5 us -> 64.3 us (0.967)
  waiting for transfers between devices: 10.8 us -> 9.69 us
  starting transfers between devices: 27.3 us -> 26.2 us
  Pallas kernels: 26.5 us -> 27.3 us
  local copies, waits for them, and re-layouts: 0.77 us -> 0.01 us
    ppermute x4, waiting for transfers between devices: 1.38 us -> 0.01 us  [the longest x2 0.01 us: shards(): a = lax.ppermute(a, 'tile', swap_a)]
    ppermute x9, starting transfers between devices: 19.7 us -> 18.6 us  [of_everyone(): lax.ppermute(value, 'tile', [(i, i ^ mask * stride) for i in range(TILES)])]
    pallas_call x1 -> x2, Pallas kernels: 3.11 us -> 4.1 us  [modal_product(): pl.pallas_call(other_levels_kernel, grid=grid, in_specs=[whole(n, depth),...]
    unnamed x4 -> x2, local copies, waits for them, and re-layouts: 0.76 us -> 0.01 us
    pallas_call x4 -> x5, Pallas kernels: 12.8 us -> 12.7 us  [call(): pl.pallas_call(kernel, grid=(1,), in_specs=[full(x.shape) for x in args],...]
  transfers between devices with their start and end apart: 14 -> 14, of which waited for: 8 -> 6; matrix products, arithmetic and copies ran while one was open for 0% -> 0% of each run, Pallas kernels for 20% -> 24%
where the time goes in v4:
time: 64.3 us; the launch traced here: 64.1 us
  Pallas kernels  27.3 us (42%)
  starting transfers between devices  26.2 us (41%)
  waiting for transfers between devices  9.69 us (15%)
  between operations  0.92 us (1%)
    ppermute x9, starting transfers between devices, of_everyone(): lax.ppermute(value, 'tile', [(i, i ^ mask * stride) for i in range(TILES)])  18.6 us
    pallas_call x5, Pallas kernels, call(): pl.pallas_call(kernel, grid=(1,), in_specs=[full(x.shape) for x in args],...  12.7 us
    ppermute x9, waiting for transfers between devices, of_everyone(): lax.ppermute(value, 'tile', [(i, i ^ mask * stride) for i in range(TILES)])  9.68 us
    ppermute x2, starting transfers between devices, shards(): a = lax.ppermute(a, 'tile', swap_a)  5.93 us
    pallas_call x1, Pallas kernels, solve(): pl.pallas_call(solve_kernel, grid=(1,), in_specs=[full(x.shape) for x in...  5.59 us
    pallas_call x1, Pallas kernels, modal_product(): pl.pallas_call(own_levels_kernel, grid=grid, in_specs=[whole(2 * levels,...  4.93 us
    pallas_call x2, Pallas kernels, modal_product(): pl.pallas_call(other_levels_kernel, grid=grid, in_specs=[whole(n, depth),...  4.1 us
    ppermute x2, starting transfers between devices, shards(): halos.append((a, lax.ppermute(b, 'tile', swap_b)))  1.52 us
  transfers between devices with their start and end apart: 14, of which 6 were waited for; matrix products, arithmetic and copies ran while one was open for 0% of the time, Pallas kernels for 24%

profile of v4, /device:TPU:0, one launch (start us, length us, event | category | flops | bytes accessed | tf_op | source)
XLA Modules:
  0.0 64.1 jit_solution(6332518158301135434)
XLA Ops:
  0.6 0.1 collective-permute-start
  0.7 4.9 %own_levels.1 = (f32[384,1024]{1,0:T(8,128)S(1)}, f32[256,1024]{1,0:T(8,128)S(1)}, bf16[384,1088]{1,0:T(8,128)(2,1)S(1)}, bf16[256,1088]{1,0:T(8,128)(2,1)S(1)}) custom-call(bf16[136,80]{1,0:T(8,128)(2,1)} %bitcast.5, bf16[1088,1024]{1,0:T(8,128)(2,1)} %bitcast.4), custom_call_target="tpu_custom_call" | custom-call | tf_op jit(solution)/shard_map/own_levels/pallas_call | solution.py:138
  5.7 0.0 collective-permute-done.inc_ref
  5.7 2.3 %other_levels.3.modal_ref = f32[384,1024]{1,0:T(8,128)S(1)} custom-call(bf16[384,1088]{1,0:T(8,128)(2,1)S(1)} %get-tuple-element.28.left_ref, bf16[1088,1024]{1,0:T(8,128)(2,1)S(1)} %collective-permute-done.inc_ref, f32[384,1024]{1,0:T(8,128)S(1)} %get-tuple-element.29.acc_ref), custom_call_target="tpu_custom_call" | custom-call | tf_op jit(solution)/shard_map/other_levels/pallas_call | solution.py:150
  7.9 1.0 %turn.3 = (f32[1,2184,128]{2,1,0:T(8,128)S(1)}, f32[1,1160,128]{2,1,0:T(8,128)S(1)}, bf16[1536,128]{1,0:T(8,128)(2,1)S(1)}, bf16[1536,128]{1,0:T(8,128)(2,1)S(1)}) custom-call(f32[384,1024]{1,0:T(8,128)S(1)} %other_levels.3.modal_ref), custom_call_target="tpu_custom_call" | custom-call | tf_op jit(solution)/shard_map/turn/pallas_call | solution.py:195
  8.9 1.8 %collective-permute-start.3 = (bf16[1536,128]{1,0:T(8,128)(2,1)S(1)}, bf16[1536,128]{1,0:T(8,128)(2,1)S(1)}, u32[]{:S(2)}, u32[]{:S(2)}) collective-permute-start(bf16[1536,128]{1,0:T(8,128)(2,1)S(1)} %get-tuple-element.30), channel_id=1, source_target_pairs={{0,2},{2,0},{4,6},{6,4},{8,10},{10,8},{12,14},{14,12},{16,18},{18,... | collective-permute-start | bytes 1179656 | tf_op jit(solution)/shard_map/ppermute | solution.py:588
  10.7 0.7 %collective-permute-start.4 = (bf16[1536,128]{1,0:T(8,128)(2,1)S(1)}, bf16[1536,128]{1,0:T(8,128)(2,1)S(1)}, u32[]{:S(2)}, u32[]{:S(2)}) collective-permute-start(bf16[1536,128]{1,0:T(8,128)(2,1)S(1)} %get-tuple-element.31), channel_id=1, source_target_pairs={{2,4},{6,8},{10,12},{14,16},{18,20},{22,24},{26,28},{30,32},{34,36... | collective-permute-start | bytes 1179656 | tf_op jit(solution)/shard_map/ppermute | solution.py:589
  11.4 1.8 %other_levels.2.modal_ref = f32[256,1024]{1,0:T(8,128)S(1)} custom-call(bf16[256,1088]{1,0:T(8,128)(2,1)S(1)} %get-tuple-element.24.left_ref, bf16[1088,1024]{1,0:T(8,128)(2,1)S(1)} %collective-permute-done.inc_ref, f32[256,1024]{1,0:T(8,128)S(1)} %get-tuple-element.25.acc_ref), custom_call_target="tpu_custom_call" | custom-call | tf_op jit(solution)/shard_map/other_levels/pallas_call | solution.py:150
  13.2 0.5 turn.2
  13.7 4.2 %collective-permute-start.1 = (bf16[1024,128]{1,0:T(8,128)(2,1)S(1)}, bf16[1024,128]{1,0:T(8,128)(2,1)S(1)}, u32[]{:S(2)}, u32[]{:S(2)}) collective-permute-start(bf16[1024,128]{1,0:T(8,128)(2,1)S(1)} %get-tuple-element.26), channel_id=1, source_target_pairs={{0,2},{2,0},{4,6},{6,4},{8,10},{10,8},{12,14},{14,12},{16,18},{18,... | collective-permute-start | bytes 786440 | tf_op jit(solution)/shard_map/ppermute | solution.py:588
  17.9 0.8 %collective-permute-start.2 = (bf16[1024,128]{1,0:T(8,128)(2,1)S(1)}, bf16[1024,128]{1,0:T(8,128)(2,1)S(1)}, u32[]{:S(2)}, u32[]{:S(2)}) collective-permute-start(bf16[1024,128]{1,0:T(8,128)(2,1)S(1)} %get-tuple-element.27), channel_id=1, source_target_pairs={{2,4},{6,8},{10,12},{14,16},{18,20},{22,24},{26,28},{30,32},{34,36... | collective-permute-start | bytes 786440 | tf_op jit(solution)/shard_map/ppermute | solution.py:589
  18.7 3.5 %inner.1 = (f32[1,7624,128]{2,1,0:T(8,128)S(1)}, f32[1,7624,128]{2,1,0:T(8,128)S(1)}, f32[1,4040,128]{2,1,0:T(8,128)S(1)}, f32[16,128]{1,0:T(8,128)S(1)}, f32[16,128]{1,0:T(8,128)S(1)}, /*index=5*/f32[16,128]{1,0:T(8,128)S(1)}) custom-call(f32[1,2184,128]{2,1,0:T(8,128)S(1)} %get-tuple-element.32.refs_0_, ...), custom_call_target="tpu_custom_call" | custom-call | tf_op jit(solution)/shard_map/inner/pallas_call | solution.py:195
  22.2 0.0 collective-permute-done.3.a_ref
  22.2 0.0 collective-permute-done.4.b_ref
  22.2 4.7 %outer.2 = (f32[1,9800,128]{2,1,0:T(8,128)S(1)}, f32[1,5192,128]{2,1,0:T(8,128)S(1)}, f32[16,128]{1,0:T(8,128)S(1)}) custom-call(bf16[1536,128]{1,0:T(8,128)(2,1)S(1)} %collective-permute-done.3.a_ref, bf16[1536,128]{1,0:T(8,128)(2,1)S(1)} %collective-permute-done.4.b_ref, f32[16,128]{1,0:T(8,128)S(1)} %broadcast_in_dim.6.known_ref, ...), custom_call_target="tpu_custom_call" | custom-call | tf_op jit(solution)/shard_map/outer/pallas_call | solution.py:195
  26.9 0.0 collective-permute-done.1.a_ref
  26.9 0.0 collective-permute-done.2.b_ref
  26.9 0.0 copy-start
  26.9 3.1 %outer.3 = (f32[1,9800,128]{2,1,0:T(8,128)S(1)}, f32[16,128]{1,0:T(8,128)S(1)}) custom-call(bf16[1024,128]{1,0:T(8,128)(2,1)S(1)} %collective-permute-done.1.a_ref, bf16[1024,128]{1,0:T(8,128)(2,1)S(1)} %collective-permute-done.2.b_ref, f32[16,128]{1,0:T(8,128)S(1)} %get-tuple-element.39.known_ref, ...), custom_call_target="tpu_custom_call" | custom-call | tf_op jit(solution)/shard_map/outer/pallas_call | solution.py:195
  30.0 5.4 %collective-permute-start.7 = (f32[16,128]{1,0:T(8,128)S(1)}, f32[16,128]{1,0:T(8,128)S(1)}, u32[]{:S(2)}, u32[]{:S(2)}) collective-permute-start(f32[16,128]{1,0:T(8,128)S(1)} %get-tuple-element.42), channel_id=1, source_target_pairs={{0,4},{2,6},{4,0},{6,2},{8,12},{10,14},{12,8},{14,10},{16,20},{18,... | collective-permute-start | bytes 24584 | tf_op jit(solution)/shard_map/ppermute | solution.py:573
  35.4 1.7 %collective-permute-start.6 = (f32[16,128]{1,0:T(8,128)S(1)}, f32[16,128]{1,0:T(8,128)S(1)}, u32[]{:S(2)}, u32[]{:S(2)}) collective-permute-start(f32[16,128]{1,0:T(8,128)S(1)} %get-tuple-element.42), channel_id=1, source_target_pairs={{0,6},{2,4},{4,2},{6,0},{8,14},{10,12},{12,10},{14,8},{16,22},{18,... | collective-permute-start | bytes 24584 | tf_op jit(solution)/shard_map/ppermute | solution.py:573
  37.1 0.6 collective-permute-start.5
  37.7 0.0 collective-permute-done.7
  37.7 2.6 %collective-permute-done.6 = f32[16,128]{1,0:T(8,128)S(1)} collective-permute-done((f32[16,128]{1,0:T(8,128)S(1)}, f32[16,128]{1,0:T(8,128)S(1)}, u32[]{:S(2)}, u32[]{:S(2)}) %collective-permute-start.6) | collective-permute-done | bytes 8224 | tf_op jit(solution)/shard_map/ppermute | solution.py:573
  40.3 0.5 collective-permute-done.5
  40.8 3.7 %collective-permute-start.10 = (f32[16,128]{1,0:T(8,128)S(1)}, f32[16,128]{1,0:T(8,128)S(1)}, u32[]{:S(2)}, u32[]{:S(2)}) collective-permute-start(f32[16,128]{1,0:T(8,128)S(1)} %add_add_fusion.2), channel_id=1, source_target_pairs={{0,16},{2,18},{4,20},{6,22},{8,24},{10,26},{12,28},{14,30},{16,0},... | collective-permute-start | bytes 24584 | tf_op jit(solution)/shard_map/ppermute | solution.py:573
  44.5 2.4 %collective-permute-start.9 = (f32[16,128]{1,0:T(8,128)S(1)}, f32[16,128]{1,0:T(8,128)S(1)}, u32[]{:S(2)}, u32[]{:S(2)}) collective-permute-start(f32[16,128]{1,0:T(8,128)S(1)} %add_add_fusion.2), channel_id=1, source_target_pairs={{0,24},{2,26},{4,28},{6,30},{8,16},{10,18},{12,20},{14,22},{16,8},... | collective-permute-start | bytes 24584 | tf_op jit(solution)/shard_map/ppermute | solution.py:573
  46.8 0.8 %collective-permute-start.8 = (f32[16,128]{1,0:T(8,128)S(1)}, f32[16,128]{1,0:T(8,128)S(1)}, u32[]{:S(2)}, u32[]{:S(2)}) collective-permute-start(f32[16,128]{1,0:T(8,128)S(1)} %add_add_fusion.2), channel_id=1, source_target_pairs={{0,8},{2,10},{4,12},{6,14},{8,0},{10,2},{12,4},{14,6},{16,24},{18,... | collective-permute-start | bytes 24584 | tf_op jit(solution)/shard_map/ppermute | solution.py:573
  47.6 0.0 collective-permute-done.10
  47.6 1.7 %collective-permute-done.9 = f32[16,128]{1,0:T(8,128)S(1)} collective-permute-done((f32[16,128]{1,0:T(8,128)S(1)}, f32[16,128]{1,0:T(8,128)S(1)}, u32[]{:S(2)}, u32[]{:S(2)}) %collective-permute-start.9) | collective-permute-done | bytes 8224 | tf_op jit(solution)/shard_map/ppermute | solution.py:573
  49.3 1.1 %collective-permute-done.8 = f32[16,128]{1,0:T(8,128)S(1)} collective-permute-done((f32[16,128]{1,0:T(8,128)S(1)}, f32[16,128]{1,0:T(8,128)S(1)}, u32[]{:S(2)}, u32[]{:S(2)}) %collective-permute-start.8) | collective-permute-done | bytes 8224 | tf_op jit(solution)/shard_map/ppermute | solution.py:573
  50.5 3.0 %collective-permute-start.13 = (f32[16,128]{1,0:T(8,128)S(1)}, f32[16,128]{1,0:T(8,128)S(1)}, u32[]{:S(2)}, u32[]{:S(2)}) collective-permute-start(f32[16,128]{1,0:T(8,128)S(1)} %add_add_fusion.1), channel_id=1, source_target_pairs={{0,64},{2,66},{4,68},{6,70},{8,72},{10,74},{12,76},{14,78},{16,80}... | collective-permute-start | bytes 24584 | tf_op jit(solution)/shard_map/ppermute | solution.py:573
  53.5 1.1 %collective-permute-start.12 = (f32[16,128]{1,0:T(8,128)S(1)}, f32[16,128]{1,0:T(8,128)S(1)}, u32[]{:S(2)}, u32[]{:S(2)}) collective-permute-start(f32[16,128]{1,0:T(8,128)S(1)} %add_add_fusion.1), channel_id=1, source_target_pairs={{0,96},{2,98},{4,100},{6,102},{8,104},{10,106},{12,108},{14,110},{... | collective-permute-start | bytes 24584 | tf_op jit(solution)/shard_map/ppermute | solution.py:573
  54.6 0.0 collective-permute-start.11
  54.6 0.0 copy-done
  54.7 1.0 %collective-permute-done.13 = f32[16,128]{1,0:T(8,128)S(1)} collective-permute-done((f32[16,128]{1,0:T(8,128)S(1)}, f32[16,128]{1,0:T(8,128)S(1)}, u32[]{:S(2)}, u32[]{:S(2)}) %collective-permute-start.13) | collective-permute-done | bytes 8224 | tf_op jit(solution)/shard_map/ppermute | solution.py:573
  55.6 2.7 %collective-permute-done.12 = f32[16,128]{1,0:T(8,128)S(1)} collective-permute-done((f32[16,128]{1,0:T(8,128)S(1)}, f32[16,128]{1,0:T(8,128)S(1)}, u32[]{:S(2)}, u32[]{:S(2)}) %collective-permute-start.12) | collective-permute-done | bytes 8224 | tf_op jit(solution)/shard_map/ppermute | solution.py:573
  58.4 0.0 collective-permute-done.11
  58.4 5.6 %solve.1 = (f32[40,16,1024]{2,1,0:T(8,128)}, f32[40,16,1024]{2,1,0:T(8,128)}) custom-call(f32[16,128]{1,0:T(8,128)S(1)} %add_add_fusion.sums_ref, f32[1,128]{1,0:T(1,128)S(1)} %pad.4.helm_ref, f32[1,2184,128]{2,1,0:T(8,128)S(1)} %get-tuple-element.32.refs_0_, f32[1,7624,128]{2,1,0:T(8,128)S(1)} %get-tuple-element.35.refs_1_, ...), custom_call_target="tpu_custom_call" | custom-call | tf_op jit(solution)/shard_map/solve/pallas_call | solution.py:552
  (5 shorter events, 0.0 us)
Async XLA Ops:
  0.6 5.0 %collective-permute-start = (bf16[1088,1024]{1,0:T(8,128)(2,1)}, bf16[1088,1024]{1,0:T(8,128)(2,1)S(1)}, u32[]{:S(2)}, u32[]{:S(2)}) collective-permute-start(bf16[1088,1024]{1,0:T(8,128)(2,1)} %bitcast.3), channel_id=1, source_target_pairs={{0,1},{1,0},{2,3},{3,2},{4,5},{5,4},{6,7},{7,6},{8,9},{9,8},{10,11... | collective-permute-start | bytes 6684680 | tf_op jit(solution)/shard_map/ppermute | solution.py:131
  8.9 13.3 %collective-permute-start.3 = (bf16[1536,128]{1,0:T(8,128)(2,1)S(1)}, bf16[1536,128]{1,0:T(8,128)(2,1)S(1)}, u32[]{:S(2)}, u32[]{:S(2)}) collective-permute-start(bf16[1536,128]{1,0:T(8,128)(2,1)S(1)} %get-tuple-element.30), channel_id=1, source_target_pairs={{0,2},{2,0},{4,6},{6,4},{8,10},{10,8},{12,14},{14,12},{16,18},{18,... | collective-permute-start | bytes 1179656 | tf_op jit(solution)/shard_map/ppermute | solution.py:588
  10.7 11.5 %collective-permute-start.4 = (bf16[1536,128]{1,0:T(8,128)(2,1)S(1)}, bf16[1536,128]{1,0:T(8,128)(2,1)S(1)}, u32[]{:S(2)}, u32[]{:S(2)}) collective-permute-start(bf16[1536,128]{1,0:T(8,128)(2,1)S(1)} %get-tuple-element.31), channel_id=1, source_target_pairs={{2,4},{6,8},{10,12},{14,16},{18,20},{22,24},{26,28},{30,32},{34,36... | collective-permute-start | bytes 1179656 | tf_op jit(solution)/shard_map/ppermute | solution.py:589
  13.7 13.2 %collective-permute-start.1 = (bf16[1024,128]{1,0:T(8,128)(2,1)S(1)}, bf16[1024,128]{1,0:T(8,128)(2,1)S(1)}, u32[]{:S(2)}, u32[]{:S(2)}) collective-permute-start(bf16[1024,128]{1,0:T(8,128)(2,1)S(1)} %get-tuple-element.26), channel_id=1, source_target_pairs={{0,2},{2,0},{4,6},{6,4},{8,10},{10,8},{12,14},{14,12},{16,18},{18,... | collective-permute-start | bytes 786440 | tf_op jit(solution)/shard_map/ppermute | solution.py:588
  17.9 9.1 %collective-permute-start.2 = (bf16[1024,128]{1,0:T(8,128)(2,1)S(1)}, bf16[1024,128]{1,0:T(8,128)(2,1)S(1)}, u32[]{:S(2)}, u32[]{:S(2)}) collective-permute-start(bf16[1024,128]{1,0:T(8,128)(2,1)S(1)} %get-tuple-element.27), channel_id=1, source_target_pairs={{2,4},{6,8},{10,12},{14,16},{18,20},{22,24},{26,28},{30,32},{34,36... | collective-permute-start | bytes 786440 | tf_op jit(solution)/shard_map/ppermute | solution.py:589
  26.9 27.7 %copy-start = (f32[40]{0:T(128)S(1)}, f32[40]{0:T(128)}, u32[]{:S(2)}) copy-start(f32[40]{0:T(128)} %param.5) | copy-start | bytes 484
  30.0 7.7 %collective-permute-start.7 = (f32[16,128]{1,0:T(8,128)S(1)}, f32[16,128]{1,0:T(8,128)S(1)}, u32[]{:S(2)}, u32[]{:S(2)}) collective-permute-start(f32[16,128]{1,0:T(8,128)S(1)} %get-tuple-element.42), channel_id=1, source_target_pairs={{0,4},{2,6},{4,0},{6,2},{8,12},{10,14},{12,8},{14,10},{16,20},{18,... | collective-permute-start | bytes 24584 | tf_op jit(solution)/shard_map/ppermute | solution.py:573
  35.4 4.9 %collective-permute-start.6 = (f32[16,128]{1,0:T(8,128)S(1)}, f32[16,128]{1,0:T(8,128)S(1)}, u32[]{:S(2)}, u32[]{:S(2)}) collective-permute-start(f32[16,128]{1,0:T(8,128)S(1)} %get-tuple-element.42), channel_id=1, source_target_pairs={{0,6},{2,4},{4,2},{6,0},{8,14},{10,12},{12,10},{14,8},{16,22},{18,... | collective-permute-start | bytes 24584 | tf_op jit(solution)/shard_map/ppermute | solution.py:573
  37.1 3.7 %collective-permute-start.5 = (f32[16,128]{1,0:T(8,128)S(1)}, f32[16,128]{1,0:T(8,128)S(1)}, u32[]{:S(2)}, u32[]{:S(2)}) collective-permute-start(f32[16,128]{1,0:T(8,128)S(1)} %get-tuple-element.42), channel_id=1, source_target_pairs={{0,2},{2,0},{4,6},{6,4},{8,10},{10,8},{12,14},{14,12},{16,18},{18,... | collective-permute-start | bytes 24584 | tf_op jit(solution)/shard_map/ppermute | solution.py:573
  40.8 6.8 %collective-permute-start.10 = (f32[16,128]{1,0:T(8,128)S(1)}, f32[16,128]{1,0:T(8,128)S(1)}, u32[]{:S(2)}, u32[]{:S(2)}) collective-permute-start(f32[16,128]{1,0:T(8,128)S(1)} %add_add_fusion.2), channel_id=1, source_target_pairs={{0,16},{2,18},{4,20},{6,22},{8,24},{10,26},{12,28},{14,30},{16,0},... | collective-permute-start | bytes 24584 | tf_op jit(solution)/shard_map/ppermute | solution.py:573
  44.5 4.9 %collective-permute-start.9 = (f32[16,128]{1,0:T(8,128)S(1)}, f32[16,128]{1,0:T(8,128)S(1)}, u32[]{:S(2)}, u32[]{:S(2)}) collective-permute-start(f32[16,128]{1,0:T(8,128)S(1)} %add_add_fusion.2), channel_id=1, source_target_pairs={{0,24},{2,26},{4,28},{6,30},{8,16},{10,18},{12,20},{14,22},{16,8},... | collective-permute-start | bytes 24584 | tf_op jit(solution)/shard_map/ppermute | solution.py:573
  46.8 3.7 %collective-permute-start.8 = (f32[16,128]{1,0:T(8,128)S(1)}, f32[16,128]{1,0:T(8,128)S(1)}, u32[]{:S(2)}, u32[]{:S(2)}) collective-permute-start(f32[16,128]{1,0:T(8,128)S(1)} %add_add_fusion.2), channel_id=1, source_target_pairs={{0,8},{2,10},{4,12},{6,14},{8,0},{10,2},{12,4},{14,6},{16,24},{18,... | collective-permute-start | bytes 24584 | tf_op jit(solution)/shard_map/ppermute | solution.py:573
  50.5 5.2 %collective-permute-start.13 = (f32[16,128]{1,0:T(8,128)S(1)}, f32[16,128]{1,0:T(8,128)S(1)}, u32[]{:S(2)}, u32[]{:S(2)}) collective-permute-start(f32[16,128]{1,0:T(8,128)S(1)} %add_add_fusion.1), channel_id=1, source_target_pairs={{0,64},{2,66},{4,68},{6,70},{8,72},{10,74},{12,76},{14,78},{16,80}... | collective-permute-start | bytes 24584 | tf_op jit(solution)/shard_map/ppermute | solution.py:573
  53.5 4.9 %collective-permute-start.12 = (f32[16,128]{1,0:T(8,128)S(1)}, f32[16,128]{1,0:T(8,128)S(1)}, u32[]{:S(2)}, u32[]{:S(2)}) collective-permute-start(f32[16,128]{1,0:T(8,128)S(1)} %add_add_fusion.1), channel_id=1, source_target_pairs={{0,96},{2,98},{4,100},{6,102},{8,104},{10,106},{12,108},{14,110},{... | collective-permute-start | bytes 24584 | tf_op jit(solution)/shard_map/ppermute | solution.py:573
  54.6 3.7 %collective-permute-start.11 = (f32[16,128]{1,0:T(8,128)S(1)}, f32[16,128]{1,0:T(8,128)S(1)}, u32[]{:S(2)}, u32[]{:S(2)}) collective-permute-start(f32[16,128]{1,0:T(8,128)S(1)} %add_add_fusion.1), channel_id=1, source_target_pairs={{0,32},{2,34},{4,36},{6,38},{8,40},{10,42},{12,44},{14,46},{16,48}... | collective-permute-start | bytes 24584 | tf_op jit(solution)/shard_map/ppermute | solution.py:573

commit v5 on v4

--- a/solution.py
+++ b/solution.py
@@ -7,12 +7,12 @@
 from jax.experimental.pallas import tpu as pltpu
 from jax.sharding import PartitionSpec as P
 
+
 STEPS = 8
 MOMENTS = 2 * STEPS
 ROWS = 16
 HALO = 8
 MODES = 40
-GROUPS = 5
 LANES = 128
 COLS = 1024
 BLOCKS = COLS // LANES
@@ -190,7 +190,7 @@
     return pl.BlockSpec(shape, lambda i: (0,) * len(shape))
 
 
-def single(kernel, outs, name, mib=16, scratch=()):
+def single(kernel, outs, mib=16, scratch=()):
     def call(*args):
         return pl.pallas_call(
             kernel,
@@ -200,8 +200,8 @@
             out_shape=list(outs),
             scratch_shapes=list(scratch),
             compiler_params=limits(mib),
-            name=name,
         )(*args)
+
     return call
 
 
@@ -251,7 +251,7 @@
     outs = [jax.ShapeDtypeStruct((1, SETS[m].rows(ROWS), LANES), f32) for m in members]
     edge = sum(HALO * SETS[m].length for m in members)
     outs += [jax.ShapeDtypeStruct((edge, LANES), bf16)] * 2
-    out = single(functools.partial(turn_kernel, members), outs, "turn")(modal)
+    out = single(functools.partial(turn_kernel, members), outs)(modal)
     return out[:-2], out[-2:]
 
 
@@ -264,7 +264,7 @@
     for row_ in range(ROWS):
         slots_ = INNER_SLOTS if is_inner(order_, row_) else OUTER_SLOTS
         slots_[order_, row_] = len(slots_)
-STRIP = 8
+STRIP = 4
 
 
 def sweep(kind, order, begin, end, place, sums, factor_of):
@@ -327,7 +327,7 @@
 def inner_basis(firsts):
     outs = [jax.ShapeDtypeStruct((1, kind.rows(len(INNER_SLOTS)), LANES), f32) for kind in SETS]
     outs += [jax.ShapeDtypeStruct((MOMENTS, LANES), f32)] * len(SETS)
-    out = single(inner_kernel, outs, "inner")(*firsts)
+    out = single(inner_kernel, outs)(*firsts)
     return out[:len(SETS)], out[len(SETS):]
 
 
@@ -396,9 +396,7 @@
     outs += [jax.ShapeDtypeStruct((MOMENTS, LANES), f32)]
     args = [x for m in members for x in (firsts[m], inners[m], parts[m])]
     scratch = [pltpu.VMEM((6, SETS[m].rows(HALO), LANES), f32) for m in members]
-    out = single(functools.partial(outer_kernel, members), outs, "outer", 24, scratch)(
-        *halo, known, *args
-    )
+    out = single(functools.partial(outer_kernel, members), outs, 24, scratch)(*halo, known, *args)
     return out[:-1], out[-1]
 
 
@@ -406,7 +404,7 @@
     half = 0.5 * tau
     rho = list(nu)
     pi = list(nu)
-    one, zero = jnp.ones_like(tau), None
+    one = jnp.ones_like(tau)
     r = [one]
     p = [one]
     x = [None] * STEPS
@@ -468,7 +466,7 @@
 def solve_kernel(sums_ref, helm_ref, *refs):
     count = len(SETS)
     fields = [refs[3 * n:3 * n + 3] for n in range(count)]
-    x_out, r_out, x_ref, r_ref, stage_ref, coef_ref, sems = refs[3 * count:]
+    x_out, r_out, x_ref, r_ref, mix_ref, stage_ref, coef_ref, sems = refs[3 * count:]
     raw = [sums_ref[k:k + 1, :] for k in range(MOMENTS)]
     nu = raw[:2]
     for k in range(2, MOMENTS):
@@ -490,8 +488,7 @@
         spread = [jnp.broadcast_to(own[k:k + 1, :], (8, LANES))[None] for k in range(2 * STEPS + 1)]
         cx, cr = spread[:STEPS], spread[STEPS:]
 
-        def combined(row):
-            xs, rs = [], []
+        def combine(row, at):
             for strip in range(0, kind.count, STRIP):
                 x = r = None
                 for k in range(STEPS + 1):
@@ -506,31 +503,31 @@
                     if k < STEPS:
                         x = cx[k] * field if x is None else x + cx[k] * field
                     r = cr[k] * field if r is None else r + cr[k] * field
-                xs.append(x.reshape(STRIP * 8, LANES))
-                rs.append(r.reshape(STRIP * 8, LANES))
-            return jnp.concatenate(xs, axis=0), jnp.concatenate(rs, axis=0)
+                for which, value in ((0, x), (1, r)):
+                    start = at + 8 * strip
+                    mix_ref[which, start:start + 8 * STRIP, :] = value.reshape(8 * STRIP, LANES)
 
         for top in range(0, ROWS, 8):
-            if len(kind.groups) == 2:
-                for row in range(8):
-                    for which, values in enumerate(combined(top + row)):
-                        stage_ref[which, row] = values.T
-            else:
-                for row in range(0, 8, 2):
-                    for which, (one, two) in enumerate(
-                        zip(combined(top + row), combined(top + row + 1))
-                    ):
-                        both = jnp.concatenate([one, two], axis=0).T
-                        for b in range(BLOCKS):
-                            even = both[16 * b:16 * b + 8]
-                            odd = both[16 * b + 8:16 * b + 16]
-                            half = LANES // 2
-                            stage_ref[which, row, 8 * b:8 * b + 8, :] = jnp.where(
-                                low_half, even, pltpu.roll(odd, half, 1)
-                            )
-                            stage_ref[which, row + 1, 8 * b:8 * b + 8, :] = jnp.where(
-                                low_half, pltpu.roll(even, half, 1), odd
-                            )
+            for row in range(8):
+                combine(top + row, row * kind.length)
+            step = LANES // kind.length
+            for row in range(0, 8, step):
+                start = row * kind.length
+                for which in range(2):
+                    both = mix_ref[which, start:start + LANES, :].T
+                    if step == 1:
+                        stage_ref[which, row] = both
+                        continue
+                    for b in range(BLOCKS):
+                        even = both[16 * b:16 * b + 8]
+                        odd = both[16 * b + 8:16 * b + 16]
+                        half = LANES // 2
+                        stage_ref[which, row, 8 * b:8 * b + 8, :] = jnp.where(
+                            low_half, even, pltpu.roll(odd, half, 1)
+                        )
+                        stage_ref[which, row + 1, 8 * b:8 * b + 8, :] = jnp.where(
+                            low_half, pltpu.roll(even, half, 1), odd
+                        )
             for which, ref in enumerate((x_ref, r_ref)):
                 for b in range(BLOCKS):
                     for n, group in enumerate(kind.groups):
@@ -558,6 +555,7 @@
         scratch_shapes=[
             pltpu.VMEM((MODES, ROWS, COLS), f32),
             pltpu.VMEM((MODES, ROWS, COLS), f32),
+            pltpu.VMEM((2, 8 * LANES, LANES), f32),
             pltpu.VMEM((2, 8, LANES, LANES), f32),
             pltpu.VMEM((24, LANES), f32),
             pltpu.SemaphoreType.DMA((2 * len(SETS),)),
@@ -586,7 +584,8 @@
         made, (a, b) = turn(members, modal)
         firsts.update(zip(members, made))
         a = lax.ppermute(a, "tile", swap_a)
-        halos.append((a, lax.ppermute(b, "tile", swap_b)))
+        b = lax.ppermute(b, "tile", swap_b)
+        halos.append((a, b))
     firsts = [firsts[n] for n in range(len(SETS))]
     inners, parts = inner_basis(firsts)
     moments = jnp.zeros((MOMENTS, LANES), f32)
@@ -602,4 +601,5 @@
 def solution(mesh):
     in_specs = (P("lev", "tile", None), P(), P("lev"))
     out_specs = (P("lev", "tile", None), P("lev", "tile", None))
+
     return jax.shard_map(shards, mesh=mesh, in_specs=in_specs, out_specs=out_specs, check_vma=False)

time: 64.3 us -> 64.4 us (level)
  no operation moved by 1% of the time
where the time goes in v5:
time: 64.4 us; the launch traced here: 64.2 us
  Pallas kernels  27.5 us (43%)
  starting transfers between devices  26 us (40%)
  waiting for transfers between devices  9.79 us (15%)
  between operations  0.92 us (1%)
    ppermute x9, starting transfers between devices, of_everyone(): lax.ppermute(value, 'tile', [(i, i ^ mask * stride) for i in range(TILES)])  18.4 us
    pallas_call x5, Pallas kernels, call(): pl.pallas_call(kernel, grid=(1,), in_specs=[full(x.shape) for x in args],...  12.9 us
    ppermute x9, waiting for transfers between devices, of_everyone(): lax.ppermute(value, 'tile', [(i, i ^ mask * stride) for i in range(TILES)])  9.78 us
    ppermute x2, starting transfers between devices, shards(): a = lax.ppermute(a, 'tile', swap_a)  5.93 us
    pallas_call x1, Pallas kernels, solve(): pl.pallas_call(solve_kernel, grid=(1,), in_specs=[full(x.shape) for x in...  5.59 us
    pallas_call x1, Pallas kernels, modal_product(): pl.pallas_call(own_levels_kernel, grid=grid, in_specs=[whole(2 * levels,...  4.93 us
    pallas_call x2, Pallas kernels, modal_product(): pl.pallas_call(other_levels_kernel, grid=grid, in_specs=[whole(n, depth),...  4.1 us
    ppermute x2, starting transfers between devices, shards(): b = lax.ppermute(b, 'tile', swap_b)  1.52 us
  transfers between devices with their start and end apart: 14, of which 6 were waited for; matrix products, arithmetic and copies ran while one was open for 0% of the time, Pallas kernels for 24%

profile of v5, /device:TPU:0, one launch (start us, length us, event | category | flops | bytes accessed | tf_op | source)
XLA Modules:
  0.0 64.2 jit_solution(10951667356868051759)
XLA Ops:
  0.6 0.1 collective-permute-start
  0.7 4.9 %own_levels.1 = (f32[384,1024]{1,0:T(8,128)S(1)}, f32[256,1024]{1,0:T(8,128)S(1)}, bf16[384,1088]{1,0:T(8,128)(2,1)S(1)}, bf16[256,1088]{1,0:T(8,128)(2,1)S(1)}) custom-call(bf16[136,80]{1,0:T(8,128)(2,1)} %bitcast.5, bf16[1088,1024]{1,0:T(8,128)(2,1)} %bitcast.4), custom_call_target="tpu_custom_call" | custom-call | tf_op jit(solution)/shard_map/own_levels/pallas_call | solution.py:138
  5.7 0.0 collective-permute-done.inc_ref
  5.7 2.3 %other_levels.3.modal_ref = f32[384,1024]{1,0:T(8,128)S(1)} custom-call(bf16[384,1088]{1,0:T(8,128)(2,1)S(1)} %get-tuple-element.28.left_ref, bf16[1088,1024]{1,0:T(8,128)(2,1)S(1)} %collective-permute-done.inc_ref, f32[384,1024]{1,0:T(8,128)S(1)} %get-tuple-element.29.acc_ref), custom_call_target="tpu_custom_call" | custom-call | tf_op jit(solution)/shard_map/other_levels/pallas_call | solution.py:150
  7.9 1.0 %shard_map.51 = (f32[1,2184,128]{2,1,0:T(8,128)S(1)}, f32[1,1160,128]{2,1,0:T(8,128)S(1)}, bf16[1536,128]{1,0:T(8,128)(2,1)S(1)}, bf16[1536,128]{1,0:T(8,128)(2,1)S(1)}) custom-call(f32[384,1024]{1,0:T(8,128)S(1)} %other_levels.3.modal_ref), custom_call_target="tpu_custom_call" | custom-call | tf_op jit(solution)/shard_map/pallas_call | solution.py:195
  8.9 1.8 %collective-permute-start.3 = (bf16[1536,128]{1,0:T(8,128)(2,1)S(1)}, bf16[1536,128]{1,0:T(8,128)(2,1)S(1)}, u32[]{:S(2)}, u32[]{:S(2)}) collective-permute-start(bf16[1536,128]{1,0:T(8,128)(2,1)S(1)} %get-tuple-element.30), channel_id=1, source_target_pairs={{0,2},{2,0},{4,6},{6,4},{8,10},{10,8},{12,14},{14,12},{16,18},{18,... | collective-permute-start | bytes 1179656 | tf_op jit(solution)/shard_map/ppermute | solution.py:586
  10.7 0.7 %collective-permute-start.4 = (bf16[1536,128]{1,0:T(8,128)(2,1)S(1)}, bf16[1536,128]{1,0:T(8,128)(2,1)S(1)}, u32[]{:S(2)}, u32[]{:S(2)}) collective-permute-start(bf16[1536,128]{1,0:T(8,128)(2,1)S(1)} %get-tuple-element.31), channel_id=1, source_target_pairs={{2,4},{6,8},{10,12},{14,16},{18,20},{22,24},{26,28},{30,32},{34,36... | collective-permute-start | bytes 1179656 | tf_op jit(solution)/shard_map/ppermute | solution.py:587
  11.4 1.8 %other_levels.2.modal_ref = f32[256,1024]{1,0:T(8,128)S(1)} custom-call(bf16[256,1088]{1,0:T(8,128)(2,1)S(1)} %get-tuple-element.24.left_ref, bf16[1088,1024]{1,0:T(8,128)(2,1)S(1)} %collective-permute-done.inc_ref, f32[256,1024]{1,0:T(8,128)S(1)} %get-tuple-element.25.acc_ref), custom_call_target="tpu_custom_call" | custom-call | tf_op jit(solution)/shard_map/other_levels/pallas_call | solution.py:150
  13.2 0.5 shard_map.50
  13.7 4.2 %collective-permute-start.1 = (bf16[1024,128]{1,0:T(8,128)(2,1)S(1)}, bf16[1024,128]{1,0:T(8,128)(2,1)S(1)}, u32[]{:S(2)}, u32[]{:S(2)}) collective-permute-start(bf16[1024,128]{1,0:T(8,128)(2,1)S(1)} %get-tuple-element.26), channel_id=1, source_target_pairs={{0,2},{2,0},{4,6},{6,4},{8,10},{10,8},{12,14},{14,12},{16,18},{18,... | collective-permute-start | bytes 786440 | tf_op jit(solution)/shard_map/ppermute | solution.py:586
  17.9 0.8 %collective-permute-start.2 = (bf16[1024,128]{1,0:T(8,128)(2,1)S(1)}, bf16[1024,128]{1,0:T(8,128)(2,1)S(1)}, u32[]{:S(2)}, u32[]{:S(2)}) collective-permute-start(bf16[1024,128]{1,0:T(8,128)(2,1)S(1)} %get-tuple-element.27), channel_id=1, source_target_pairs={{2,4},{6,8},{10,12},{14,16},{18,20},{22,24},{26,28},{30,32},{34,36... | collective-permute-start | bytes 786440 | tf_op jit(solution)/shard_map/ppermute | solution.py:587
  18.7 3.6 %shard_map.52 = (f32[1,7624,128]{2,1,0:T(8,128)S(1)}, f32[1,7624,128]{2,1,0:T(8,128)S(1)}, f32[1,4040,128]{2,1,0:T(8,128)S(1)}, f32[16,128]{1,0:T(8,128)S(1)}, f...) custom-call(f32[1,2184,128]{2,1,0:T(8,128)S(1)} %get-tuple-element.32.refs_0_, ...), custom_call_target="tpu_custom_call" | custom-call | tf_op jit(solution)/shard_map/pallas_call | solution.py:195
  22.3 0.0 collective-permute-done.3.a_ref
  22.3 0.0 collective-permute-done.4.b_ref
  22.3 4.7 %shard_map.53 = (f32[1,9800,128]{2,1,0:T(8,128)S(1)}, f32[1,5192,128]{2,1,0:T(8,128)S(1)}, f32[16,128]{1,0:T(8,128)S(1)}) custom-call(bf16[1536,128]{1,0:T(8,128)(2,1)S(1)} %collective-permute-done.3.a_ref, bf16[1536,128]{1,0:T(8,128)(2,1)S(1)} %collective-permute-done.4.b_ref, f32[16,128]{1,0:T(8,128)S(1)} %broadcast_in_dim.6.known_ref, ...), custom_call_target="tpu_custom_call" | custom-call | tf_op jit(solution)/shard_map/pallas_call | solution.py:195
  27.0 0.0 collective-permute-done.1.a_ref
  27.0 0.0 collective-permute-done.2.b_ref
  27.0 0.0 copy-start
  27.0 3.1 %shard_map.54 = (f32[1,9800,128]{2,1,0:T(8,128)S(1)}, f32[16,128]{1,0:T(8,128)S(1)}) custom-call(bf16[1024,128]{1,0:T(8,128)(2,1)S(1)} %collective-permute-done.1.a_ref, bf16[1024,128]{1,0:T(8,128)(2,1)S(1)} %collective-permute-done.2.b_ref, f32[16,128]{1,0:T(8,128)S(1)} %get-tuple-element.39.known_ref, ...), custom_call_target="tpu_custom_call" | custom-call | tf_op jit(solution)/shard_map/pallas_call | solution.py:195
  30.2 5.3 %collective-permute-start.7 = (f32[16,128]{1,0:T(8,128)S(1)}, f32[16,128]{1,0:T(8,128)S(1)}, u32[]{:S(2)}, u32[]{:S(2)}) collective-permute-start(f32[16,128]{1,0:T(8,128)S(1)} %get-tuple-element.42), channel_id=1, source_target_pairs={{0,4},{2,6},{4,0},{6,2},{8,12},{10,14},{12,8},{14,10},{16,20},{18,... | collective-permute-start | bytes 24584 | tf_op jit(solution)/shard_map/ppermute | solution.py:571
  35.5 1.8 %collective-permute-start.6 = (f32[16,128]{1,0:T(8,128)S(1)}, f32[16,128]{1,0:T(8,128)S(1)}, u32[]{:S(2)}, u32[]{:S(2)}) collective-permute-start(f32[16,128]{1,0:T(8,128)S(1)} %get-tuple-element.42), channel_id=1, source_target_pairs={{0,6},{2,4},{4,2},{6,0},{8,14},{10,12},{12,10},{14,8},{16,22},{18,... | collective-permute-start | bytes 24584 | tf_op jit(solution)/shard_map/ppermute | solution.py:571
  37.3 0.5 collective-permute-start.5
  37.8 0.0 collective-permute-done.7
  37.8 2.6 %collective-permute-done.6 = f32[16,128]{1,0:T(8,128)S(1)} collective-permute-done((f32[16,128]{1,0:T(8,128)S(1)}, f32[16,128]{1,0:T(8,128)S(1)}, u32[]{:S(2)}, u32[]{:S(2)}) %collective-permute-start.6) | collective-permute-done | bytes 8224 | tf_op jit(solution)/shard_map/ppermute | solution.py:571
  40.4 0.6 collective-permute-done.5
  41.0 3.6 %collective-permute-start.10 = (f32[16,128]{1,0:T(8,128)S(1)}, f32[16,128]{1,0:T(8,128)S(1)}, u32[]{:S(2)}, u32[]{:S(2)}) collective-permute-start(f32[16,128]{1,0:T(8,128)S(1)} %add_add_fusion.2), channel_id=1, source_target_pairs={{0,16},{2,18},{4,20},{6,22},{8,24},{10,26},{12,28},{14,30},{16,0},... | collective-permute-start | bytes 24584 | tf_op jit(solution)/shard_map/ppermute | solution.py:571
  44.5 2.3 %collective-permute-start.9 = (f32[16,128]{1,0:T(8,128)S(1)}, f32[16,128]{1,0:T(8,128)S(1)}, u32[]{:S(2)}, u32[]{:S(2)}) collective-permute-start(f32[16,128]{1,0:T(8,128)S(1)} %add_add_fusion.2), channel_id=1, source_target_pairs={{0,24},{2,26},{4,28},{6,30},{8,16},{10,18},{12,20},{14,22},{16,8},... | collective-permute-start | bytes 24584 | tf_op jit(solution)/shard_map/ppermute | solution.py:571
  46.9 0.8 %collective-permute-start.8 = (f32[16,128]{1,0:T(8,128)S(1)}, f32[16,128]{1,0:T(8,128)S(1)}, u32[]{:S(2)}, u32[]{:S(2)}) collective-permute-start(f32[16,128]{1,0:T(8,128)S(1)} %add_add_fusion.2), channel_id=1, source_target_pairs={{0,8},{2,10},{4,12},{6,14},{8,0},{10,2},{12,4},{14,6},{16,24},{18,... | collective-permute-start | bytes 24584 | tf_op jit(solution)/shard_map/ppermute | solution.py:571
  47.7 0.0 collective-permute-done.10
  47.7 1.7 %collective-permute-done.9 = f32[16,128]{1,0:T(8,128)S(1)} collective-permute-done((f32[16,128]{1,0:T(8,128)S(1)}, f32[16,128]{1,0:T(8,128)S(1)}, u32[]{:S(2)}, u32[]{:S(2)}) %collective-permute-start.9) | collective-permute-done | bytes 8224 | tf_op jit(solution)/shard_map/ppermute | solution.py:571
  49.4 1.1 %collective-permute-done.8 = f32[16,128]{1,0:T(8,128)S(1)} collective-permute-done((f32[16,128]{1,0:T(8,128)S(1)}, f32[16,128]{1,0:T(8,128)S(1)}, u32[]{:S(2)}, u32[]{:S(2)}) %collective-permute-start.8) | collective-permute-done | bytes 8224 | tf_op jit(solution)/shard_map/ppermute | solution.py:571
  50.5 3.0 %collective-permute-start.13 = (f32[16,128]{1,0:T(8,128)S(1)}, f32[16,128]{1,0:T(8,128)S(1)}, u32[]{:S(2)}, u32[]{:S(2)}) collective-permute-start(f32[16,128]{1,0:T(8,128)S(1)} %add_add_fusion.1), channel_id=1, source_target_pairs={{0,64},{2,66},{4,68},{6,70},{8,72},{10,74},{12,76},{14,78},{16,80}... | collective-permute-start | bytes 24584 | tf_op jit(solution)/shard_map/ppermute | solution.py:571
  53.6 1.1 %collective-permute-start.12 = (f32[16,128]{1,0:T(8,128)S(1)}, f32[16,128]{1,0:T(8,128)S(1)}, u32[]{:S(2)}, u32[]{:S(2)}) collective-permute-start(f32[16,128]{1,0:T(8,128)S(1)} %add_add_fusion.1), channel_id=1, source_target_pairs={{0,96},{2,98},{4,100},{6,102},{8,104},{10,106},{12,108},{14,110},{... | collective-permute-start | bytes 24584 | tf_op jit(solution)/shard_map/ppermute | solution.py:571
  54.7 0.0 collective-permute-start.11
  54.7 0.0 copy-done
  54.7 1.0 %collective-permute-done.13 = f32[16,128]{1,0:T(8,128)S(1)} collective-permute-done((f32[16,128]{1,0:T(8,128)S(1)}, f32[16,128]{1,0:T(8,128)S(1)}, u32[]{:S(2)}, u32[]{:S(2)}) %collective-permute-start.13) | collective-permute-done | bytes 8224 | tf_op jit(solution)/shard_map/ppermute | solution.py:571
  55.7 2.7 %collective-permute-done.12 = f32[16,128]{1,0:T(8,128)S(1)} collective-permute-done((f32[16,128]{1,0:T(8,128)S(1)}, f32[16,128]{1,0:T(8,128)S(1)}, u32[]{:S(2)}, u32[]{:S(2)}) %collective-permute-start.12) | collective-permute-done | bytes 8224 | tf_op jit(solution)/shard_map/ppermute | solution.py:571
  58.4 0.0 collective-permute-done.11
  58.4 5.6 %solve.1 = (f32[40,16,1024]{2,1,0:T(8,128)}, f32[40,16,1024]{2,1,0:T(8,128)}) custom-call(f32[16,128]{1,0:T(8,128)S(1)} %add_add_fusion.sums_ref, f32[1,128]{1,0:T(1,128)S(1)} %pad.4.helm_ref, f32[1,2184,128]{2,1,0:T(8,128)S(1)} %get-tuple-element.32.refs_0_, f32[1,7624,128]{2,1,0:T(8,128)S(1)} %get-tuple-element.35.refs_1_, ...), custom_call_target="tpu_custom_call" | custom-call | tf_op jit(solution)/shard_map/solve/pallas_call | solution.py:549
  (5 shorter events, 0.0 us)
Async XLA Ops:
  0.6 5.0 %collective-permute-start = (bf16[1088,1024]{1,0:T(8,128)(2,1)}, bf16[1088,1024]{1,0:T(8,128)(2,1)S(1)}, u32[]{:S(2)}, u32[]{:S(2)}) collective-permute-start(bf16[1088,1024]{1,0:T(8,128)(2,1)} %bitcast.3), channel_id=1, source_target_pairs={{0,1},{1,0},{2,3},{3,2},{4,5},{5,4},{6,7},{7,6},{8,9},{9,8},{10,11... | collective-permute-start | bytes 6684680 | tf_op jit(solution)/shard_map/ppermute | solution.py:131
  8.9 13.4 %collective-permute-start.3 = (bf16[1536,128]{1,0:T(8,128)(2,1)S(1)}, bf16[1536,128]{1,0:T(8,128)(2,1)S(1)}, u32[]{:S(2)}, u32[]{:S(2)}) collective-permute-start(bf16[1536,128]{1,0:T(8,128)(2,1)S(1)} %get-tuple-element.30), channel_id=1, source_target_pairs={{0,2},{2,0},{4,6},{6,4},{8,10},{10,8},{12,14},{14,12},{16,18},{18,... | collective-permute-start | bytes 1179656 | tf_op jit(solution)/shard_map/ppermute | solution.py:586
  10.7 11.6 %collective-permute-start.4 = (bf16[1536,128]{1,0:T(8,128)(2,1)S(1)}, bf16[1536,128]{1,0:T(8,128)(2,1)S(1)}, u32[]{:S(2)}, u32[]{:S(2)}) collective-permute-start(bf16[1536,128]{1,0:T(8,128)(2,1)S(1)} %get-tuple-element.31), channel_id=1, source_target_pairs={{2,4},{6,8},{10,12},{14,16},{18,20},{22,24},{26,28},{30,32},{34,36... | collective-permute-start | bytes 1179656 | tf_op jit(solution)/shard_map/ppermute | solution.py:587
  13.7 13.3 %collective-permute-start.1 = (bf16[1024,128]{1,0:T(8,128)(2,1)S(1)}, bf16[1024,128]{1,0:T(8,128)(2,1)S(1)}, u32[]{:S(2)}, u32[]{:S(2)}) collective-permute-start(bf16[1024,128]{1,0:T(8,128)(2,1)S(1)} %get-tuple-element.26), channel_id=1, source_target_pairs={{0,2},{2,0},{4,6},{6,4},{8,10},{10,8},{12,14},{14,12},{16,18},{18,... | collective-permute-start | bytes 786440 | tf_op jit(solution)/shard_map/ppermute | solution.py:586
  17.9 9.2 %collective-permute-start.2 = (bf16[1024,128]{1,0:T(8,128)(2,1)S(1)}, bf16[1024,128]{1,0:T(8,128)(2,1)S(1)}, u32[]{:S(2)}, u32[]{:S(2)}) collective-permute-start(bf16[1024,128]{1,0:T(8,128)(2,1)S(1)} %get-tuple-element.27), channel_id=1, source_target_pairs={{2,4},{6,8},{10,12},{14,16},{18,20},{22,24},{26,28},{30,32},{34,36... | collective-permute-start | bytes 786440 | tf_op jit(solution)/shard_map/ppermute | solution.py:587
  27.0 27.7 %copy-start = (f32[40]{0:T(128)S(1)}, f32[40]{0:T(128)}, u32[]{:S(2)}) copy-start(f32[40]{0:T(128)} %param.5) | copy-start | bytes 484
  30.2 7.6 %collective-permute-start.7 = (f32[16,128]{1,0:T(8,128)S(1)}, f32[16,128]{1,0:T(8,128)S(1)}, u32[]{:S(2)}, u32[]{:S(2)}) collective-permute-start(f32[16,128]{1,0:T(8,128)S(1)} %get-tuple-element.42), channel_id=1, source_target_pairs={{0,4},{2,6},{4,0},{6,2},{8,12},{10,14},{12,8},{14,10},{16,20},{18,... | collective-permute-start | bytes 24584 | tf_op jit(solution)/shard_map/ppermute | solution.py:571
  35.5 4.9 %collective-permute-start.6 = (f32[16,128]{1,0:T(8,128)S(1)}, f32[16,128]{1,0:T(8,128)S(1)}, u32[]{:S(2)}, u32[]{:S(2)}) collective-permute-start(f32[16,128]{1,0:T(8,128)S(1)} %get-tuple-element.42), channel_id=1, source_target_pairs={{0,6},{2,4},{4,2},{6,0},{8,14},{10,12},{12,10},{14,8},{16,22},{18,... | collective-permute-start | bytes 24584 | tf_op jit(solution)/shard_map/ppermute | solution.py:571
  37.3 3.7 %collective-permute-start.5 = (f32[16,128]{1,0:T(8,128)S(1)}, f32[16,128]{1,0:T(8,128)S(1)}, u32[]{:S(2)}, u32[]{:S(2)}) collective-permute-start(f32[16,128]{1,0:T(8,128)S(1)} %get-tuple-element.42), channel_id=1, source_target_pairs={{0,2},{2,0},{4,6},{6,4},{8,10},{10,8},{12,14},{14,12},{16,18},{18,... | collective-permute-start | bytes 24584 | tf_op jit(solution)/shard_map/ppermute | solution.py:571
  41.0 6.7 %collective-permute-start.10 = (f32[16,128]{1,0:T(8,128)S(1)}, f32[16,128]{1,0:T(8,128)S(1)}, u32[]{:S(2)}, u32[]{:S(2)}) collective-permute-start(f32[16,128]{1,0:T(8,128)S(1)} %add_add_fusion.2), channel_id=1, source_target_pairs={{0,16},{2,18},{4,20},{6,22},{8,24},{10,26},{12,28},{14,30},{16,0},... | collective-permute-start | bytes 24584 | tf_op jit(solution)/shard_map/ppermute | solution.py:571
  44.5 4.9 %collective-permute-start.9 = (f32[16,128]{1,0:T(8,128)S(1)}, f32[16,128]{1,0:T(8,128)S(1)}, u32[]{:S(2)}, u32[]{:S(2)}) collective-permute-start(f32[16,128]{1,0:T(8,128)S(1)} %add_add_fusion.2), channel_id=1, source_target_pairs={{0,24},{2,26},{4,28},{6,30},{8,16},{10,18},{12,20},{14,22},{16,8},... | collective-permute-start | bytes 24584 | tf_op jit(solution)/shard_map/ppermute | solution.py:571
  46.9 3.7 %collective-permute-start.8 = (f32[16,128]{1,0:T(8,128)S(1)}, f32[16,128]{1,0:T(8,128)S(1)}, u32[]{:S(2)}, u32[]{:S(2)}) collective-permute-start(f32[16,128]{1,0:T(8,128)S(1)} %add_add_fusion.2), channel_id=1, source_target_pairs={{0,8},{2,10},{4,12},{6,14},{8,0},{10,2},{12,4},{14,6},{16,24},{18,... | collective-permute-start | bytes 24584 | tf_op jit(solution)/shard_map/ppermute | solution.py:571
  50.5 5.2 %collective-permute-start.13 = (f32[16,128]{1,0:T(8,128)S(1)}, f32[16,128]{1,0:T(8,128)S(1)}, u32[]{:S(2)}, u32[]{:S(2)}) collective-permute-start(f32[16,128]{1,0:T(8,128)S(1)} %add_add_fusion.1), channel_id=1, source_target_pairs={{0,64},{2,66},{4,68},{6,70},{8,72},{10,74},{12,76},{14,78},{16,80}... | collective-permute-start | bytes 24584 | tf_op jit(solution)/shard_map/ppermute | solution.py:571
  53.6 4.9 %collective-permute-start.12 = (f32[16,128]{1,0:T(8,128)S(1)}, f32[16,128]{1,0:T(8,128)S(1)}, u32[]{:S(2)}, u32[]{:S(2)}) collective-permute-start(f32[16,128]{1,0:T(8,128)S(1)} %add_add_fusion.1), channel_id=1, source_target_pairs={{0,96},{2,98},{4,100},{6,102},{8,104},{10,106},{12,108},{14,110},{... | collective-permute-start | bytes 24584 | tf_op jit(solution)/shard_map/ppermute | solution.py:571
  54.7 3.7 %collective-permute-start.11 = (f32[16,128]{1,0:T(8,128)S(1)}, f32[16,128]{1,0:T(8,128)S(1)}, u32[]{:S(2)}, u32[]{:S(2)}) collective-permute-start(f32[16,128]{1,0:T(8,128)S(1)} %add_add_fusion.1), channel_id=1, source_target_pairs={{0,32},{2,34},{4,36},{6,38},{8,40},{10,42},{12,44},{14,46},{16,48}... | collective-permute-start | bytes 24584 | tf_op jit(solution)/shard_map/ppermute | solution.py:571

commit v6 on v5

--- a/solution.py
+++ b/solution.py
@@ -463,11 +463,14 @@
     return x, r
 
 
-def solve_kernel(sums_ref, helm_ref, *refs):
+def solve_kernel(*refs):
     count = len(SETS)
+    (own_ref, *term_refs), helm_ref, refs = refs[:4], refs[4], refs[5:]
     fields = [refs[3 * n:3 * n + 3] for n in range(count)]
     x_out, r_out, x_ref, r_ref, mix_ref, stage_ref, coef_ref, sems = refs[3 * count:]
-    raw = [sums_ref[k:k + 1, :] for k in range(MOMENTS)]
+    one, three, two = [ref[...] for ref in term_refs]
+    moments = own_ref[...] + (one + three + two)
+    raw = [moments[k:k + 1, :] for k in range(MOMENTS)]
     nu = raw[:2]
     for k in range(2, MOMENTS):
         nu.append(2.0 * raw[k] - nu[k & 1])
@@ -543,9 +546,9 @@
         copy.wait()
 
 
-def solve(sums, helm, firsts, inners, outers):
+def solve(terms, helm, firsts, inners, outers):
     out = jax.ShapeDtypeStruct((MODES, ROWS, COLS), f32)
-    args = [sums, helm] + [x for trio in zip(firsts, inners, outers) for x in trio]
+    args = [*terms, helm] + [x for trio in zip(firsts, inners, outers) for x in trio]
     return pl.pallas_call(
         solve_kernel,
         grid=(1,),
@@ -571,8 +574,9 @@
             lax.ppermute(value, "tile", [(i, i ^ (mask * stride)) for i in range(TILES)])
             for mask in (1, 3, 2)
         ]
+        terms = (value, one, three, two)
         value = value + (one + three + two)
-    return value
+    return terms
 
 
 def shards(increments, projection, helmholtz):

time: 64.4 us -> 64.5 us (level)
  no operation moved by 1% of the time
where the time goes in v6:
time: 64.5 us; the launch traced here: 64.3 us
  Pallas kernels  27.7 us (43%)
  starting transfers between devices  25.7 us (40%)
  waiting for transfers between devices  9.9 us (15%)
  between operations  0.92 us (1%)
    ppermute x9, starting transfers between devices, of_everyone(): lax.ppermute(value, 'tile', [(i, i ^ mask * stride) for i in range(TILES)])  18.2 us
    pallas_call x5, Pallas kernels, call(): pl.pallas_call(kernel, grid=(1,), in_specs=[full(x.shape) for x in args],...  12.9 us
    ppermute x9, waiting for transfers between devices, of_everyone(): lax.ppermute(value, 'tile', [(i, i ^ mask * stride) for i in range(TILES)])  9.89 us
    ppermute x2, starting transfers between devices, shards(): a = lax.ppermute(a, 'tile', swap_a)  5.93 us
    pallas_call x1, Pallas kernels, solve(): pl.pallas_call(solve_kernel, grid=(1,), in_specs=[full(x.shape) for x in...  5.72 us
    pallas_call x1, Pallas kernels, modal_product(): pl.pallas_call(own_levels_kernel, grid=grid, in_specs=[whole(2 * levels,...  4.94 us
    pallas_call x2, Pallas kernels, modal_product(): pl.pallas_call(other_levels_kernel, grid=grid, in_specs=[whole(n, depth),...  4.13 us
    ppermute x2, starting transfers between devices, shards(): b = lax.ppermute(b, 'tile', swap_b)  1.52 us
  transfers between devices with their start and end apart: 14, of which 6 were waited for; matrix products, arithmetic and copies ran while one was open for 0% of the time, Pallas kernels for 24%

profile of v6, /device:TPU:0, one launch (start us, length us, event | category | flops | bytes accessed | tf_op | source)
XLA Modules:
  0.0 64.3 jit_solution(7047055689864018378)
XLA Ops:
  0.6 0.1 collective-permute-start
  0.7 4.9 %own_levels.1 = (f32[384,1024]{1,0:T(8,128)S(1)}, f32[256,1024]{1,0:T(8,128)S(1)}, bf16[384,1088]{1,0:T(8,128)(2,1)S(1)}, bf16[256,1088]{1,0:T(8,128)(2,1)S(1)}) custom-call(bf16[136,80]{1,0:T(8,128)(2,1)} %bitcast.5, bf16[1088,1024]{1,0:T(8,128)(2,1)} %bitcast.4), custom_call_target="tpu_custom_call" | custom-call | tf_op jit(solution)/shard_map/own_levels/pallas_call | solution.py:138
  5.7 0.0 collective-permute-done.inc_ref
  5.7 2.3 %other_levels.3.modal_ref = f32[384,1024]{1,0:T(8,128)S(1)} custom-call(bf16[384,1088]{1,0:T(8,128)(2,1)S(1)} %get-tuple-element.28.left_ref, bf16[1088,1024]{1,0:T(8,128)(2,1)S(1)} %collective-permute-done.inc_ref, f32[384,1024]{1,0:T(8,128)S(1)} %get-tuple-element.29.acc_ref), custom_call_target="tpu_custom_call" | custom-call | tf_op jit(solution)/shard_map/other_levels/pallas_call | solution.py:150
  7.9 1.0 %shard_map.51 = (f32[1,2184,128]{2,1,0:T(8,128)S(1)}, f32[1,1160,128]{2,1,0:T(8,128)S(1)}, bf16[1536,128]{1,0:T(8,128)(2,1)S(1)}, bf16[1536,128]{1,0:T(8,128)(2,1)S(1)}) custom-call(f32[384,1024]{1,0:T(8,128)S(1)} %other_levels.3.modal_ref), custom_call_target="tpu_custom_call" | custom-call | tf_op jit(solution)/shard_map/pallas_call | solution.py:195
  8.9 1.8 %collective-permute-start.3 = (bf16[1536,128]{1,0:T(8,128)(2,1)S(1)}, bf16[1536,128]{1,0:T(8,128)(2,1)S(1)}, u32[]{:S(2)}, u32[]{:S(2)}) collective-permute-start(bf16[1536,128]{1,0:T(8,128)(2,1)S(1)} %get-tuple-element.30), channel_id=1, source_target_pairs={{0,2},{2,0},{4,6},{6,4},{8,10},{10,8},{12,14},{14,12},{16,18},{18,... | collective-permute-start | bytes 1179656 | tf_op jit(solution)/shard_map/ppermute | solution.py:590
  10.7 0.7 %collective-permute-start.4 = (bf16[1536,128]{1,0:T(8,128)(2,1)S(1)}, bf16[1536,128]{1,0:T(8,128)(2,1)S(1)}, u32[]{:S(2)}, u32[]{:S(2)}) collective-permute-start(bf16[1536,128]{1,0:T(8,128)(2,1)S(1)} %get-tuple-element.31), channel_id=1, source_target_pairs={{2,4},{6,8},{10,12},{14,16},{18,20},{22,24},{26,28},{30,32},{34,36... | collective-permute-start | bytes 1179656 | tf_op jit(solution)/shard_map/ppermute | solution.py:591
  11.4 1.9 %other_levels.2.modal_ref = f32[256,1024]{1,0:T(8,128)S(1)} custom-call(bf16[256,1088]{1,0:T(8,128)(2,1)S(1)} %get-tuple-element.24.left_ref, bf16[1088,1024]{1,0:T(8,128)(2,1)S(1)} %collective-permute-done.inc_ref, f32[256,1024]{1,0:T(8,128)S(1)} %get-tuple-element.25.acc_ref), custom_call_target="tpu_custom_call" | custom-call | tf_op jit(solution)/shard_map/other_levels/pallas_call | solution.py:150
  13.2 0.5 shard_map.50
  13.7 4.2 %collective-permute-start.1 = (bf16[1024,128]{1,0:T(8,128)(2,1)S(1)}, bf16[1024,128]{1,0:T(8,128)(2,1)S(1)}, u32[]{:S(2)}, u32[]{:S(2)}) collective-permute-start(bf16[1024,128]{1,0:T(8,128)(2,1)S(1)} %get-tuple-element.26), channel_id=1, source_target_pairs={{0,2},{2,0},{4,6},{6,4},{8,10},{10,8},{12,14},{14,12},{16,18},{18,... | collective-permute-start | bytes 786440 | tf_op jit(solution)/shard_map/ppermute | solution.py:590
  17.9 0.8 %collective-permute-start.2 = (bf16[1024,128]{1,0:T(8,128)(2,1)S(1)}, bf16[1024,128]{1,0:T(8,128)(2,1)S(1)}, u32[]{:S(2)}, u32[]{:S(2)}) collective-permute-start(bf16[1024,128]{1,0:T(8,128)(2,1)S(1)} %get-tuple-element.27), channel_id=1, source_target_pairs={{2,4},{6,8},{10,12},{14,16},{18,20},{22,24},{26,28},{30,32},{34,36... | collective-permute-start | bytes 786440 | tf_op jit(solution)/shard_map/ppermute | solution.py:591
  18.8 3.6 %shard_map.52 = (f32[1,7624,128]{2,1,0:T(8,128)S(1)}, f32[1,7624,128]{2,1,0:T(8,128)S(1)}, f32[1,4040,128]{2,1,0:T(8,128)S(1)}, f32[16,128]{1,0:T(8,128)S(1)}, f...) custom-call(f32[1,2184,128]{2,1,0:T(8,128)S(1)} %get-tuple-element.32.refs_0_.refs_5_, ...), custom_call_target="tpu_custom_call" | custom-call | tf_op jit(solution)/shard_map/pallas_call | solution.py:195
  22.4 0.0 collective-permute-done.3.a_ref
  22.4 0.0 collective-permute-done.4.b_ref
  22.4 4.7 %shard_map.53 = (f32[1,9800,128]{2,1,0:T(8,128)S(1)}, f32[1,5192,128]{2,1,0:T(8,128)S(1)}, f32[16,128]{1,0:T(8,128)S(1)}) custom-call(bf16[1536,128]{1,0:T(8,128)(2,1)S(1)} %collective-permute-done.3.a_ref, bf16[1536,128]{1,0:T(8,128)(2,1)S(1)} %collective-permute-done.4.b_ref, f32[16,128]{1,0:T(8,128)S(1)} %broadcast_in_dim.6.known_ref, ...), custom_call_target="tpu_custom_call" | custom-call | tf_op jit(solution)/shard_map/pallas_call | solution.py:195
  27.1 0.0 collective-permute-done.1.a_ref
  27.1 0.0 collective-permute-done.2.b_ref
  27.1 0.0 copy-start
  27.2 3.1 %shard_map.54 = (f32[1,9800,128]{2,1,0:T(8,128)S(1)}, f32[16,128]{1,0:T(8,128)S(1)}) custom-call(bf16[1024,128]{1,0:T(8,128)(2,1)S(1)} %collective-permute-done.1.a_ref, bf16[1024,128]{1,0:T(8,128)(2,1)S(1)} %collective-permute-done.2.b_ref, f32[16,128]{1,0:T(8,128)S(1)} %get-tuple-element.39.known_ref, ...), custom_call_target="tpu_custom_call" | custom-call | tf_op jit(solution)/shard_map/pallas_call | solution.py:195
  30.3 5.2 %collective-permute-start.7 = (f32[16,128]{1,0:T(8,128)S(1)}, f32[16,128]{1,0:T(8,128)S(1)}, u32[]{:S(2)}, u32[]{:S(2)}) collective-permute-start(f32[16,128]{1,0:T(8,128)S(1)} %get-tuple-element.42), channel_id=1, source_target_pairs={{0,4},{2,6},{4,0},{6,2},{8,12},{10,14},{12,8},{14,10},{16,20},{18,... | collective-permute-start | bytes 24584 | tf_op jit(solution)/shard_map/ppermute | solution.py:574
  35.5 1.9 %collective-permute-start.6 = (f32[16,128]{1,0:T(8,128)S(1)}, f32[16,128]{1,0:T(8,128)S(1)}, u32[]{:S(2)}, u32[]{:S(2)}) collective-permute-start(f32[16,128]{1,0:T(8,128)S(1)} %get-tuple-element.42), channel_id=1, source_target_pairs={{0,6},{2,4},{4,2},{6,0},{8,14},{10,12},{12,10},{14,8},{16,22},{18,... | collective-permute-start | bytes 24584 | tf_op jit(solution)/shard_map/ppermute | solution.py:574
  37.4 0.3 collective-permute-start.5
  37.7 0.0 collective-permute-done.7
  37.7 2.6 %collective-permute-done.6 = f32[16,128]{1,0:T(8,128)S(1)} collective-permute-done((f32[16,128]{1,0:T(8,128)S(1)}, f32[16,128]{1,0:T(8,128)S(1)}, u32[]{:S(2)}, u32[]{:S(2)}) %collective-permute-start.6) | collective-permute-done | bytes 8224 | tf_op jit(solution)/shard_map/ppermute | solution.py:574
  40.3 0.7 %collective-permute-done.5 = f32[16,128]{1,0:T(8,128)S(1)} collective-permute-done((f32[16,128]{1,0:T(8,128)S(1)}, f32[16,128]{1,0:T(8,128)S(1)}, u32[]{:S(2)}, u32[]{:S(2)}) %collective-permute-start.5) | collective-permute-done | bytes 8224 | tf_op jit(solution)/shard_map/ppermute | solution.py:574
  41.1 3.6 %collective-permute-start.10 = (f32[16,128]{1,0:T(8,128)S(1)}, f32[16,128]{1,0:T(8,128)S(1)}, u32[]{:S(2)}, u32[]{:S(2)}) collective-permute-start(f32[16,128]{1,0:T(8,128)S(1)} %add_add_fusion.1), channel_id=1, source_target_pairs={{0,16},{2,18},{4,20},{6,22},{8,24},{10,26},{12,28},{14,30},{16,0},... | collective-permute-start | bytes 24584 | tf_op jit(solution)/shard_map/ppermute | solution.py:574
  44.6 2.2 %collective-permute-start.9 = (f32[16,128]{1,0:T(8,128)S(1)}, f32[16,128]{1,0:T(8,128)S(1)}, u32[]{:S(2)}, u32[]{:S(2)}) collective-permute-start(f32[16,128]{1,0:T(8,128)S(1)} %add_add_fusion.1), channel_id=1, source_target_pairs={{0,24},{2,26},{4,28},{6,30},{8,16},{10,18},{12,20},{14,22},{16,8},... | collective-permute-start | bytes 24584 | tf_op jit(solution)/shard_map/ppermute | solution.py:574
  46.9 0.8 %collective-permute-start.8 = (f32[16,128]{1,0:T(8,128)S(1)}, f32[16,128]{1,0:T(8,128)S(1)}, u32[]{:S(2)}, u32[]{:S(2)}) collective-permute-start(f32[16,128]{1,0:T(8,128)S(1)} %add_add_fusion.1), channel_id=1, source_target_pairs={{0,8},{2,10},{4,12},{6,14},{8,0},{10,2},{12,4},{14,6},{16,24},{18,... | collective-permute-start | bytes 24584 | tf_op jit(solution)/shard_map/ppermute | solution.py:574
  47.6 0.0 collective-permute-done.10
  47.6 1.9 %collective-permute-done.9 = f32[16,128]{1,0:T(8,128)S(1)} collective-permute-done((f32[16,128]{1,0:T(8,128)S(1)}, f32[16,128]{1,0:T(8,128)S(1)}, u32[]{:S(2)}, u32[]{:S(2)}) %collective-permute-start.9) | collective-permute-done | bytes 8224 | tf_op jit(solution)/shard_map/ppermute | solution.py:574
  49.5 1.0 %collective-permute-done.8 = f32[16,128]{1,0:T(8,128)S(1)} collective-permute-done((f32[16,128]{1,0:T(8,128)S(1)}, f32[16,128]{1,0:T(8,128)S(1)}, u32[]{:S(2)}, u32[]{:S(2)}) %collective-permute-start.8) | collective-permute-done | bytes 8224 | tf_op jit(solution)/shard_map/ppermute | solution.py:574
  50.5 3.0 %collective-permute-start.13 = (f32[16,128]{1,0:T(8,128)S(1)}, f32[16,128]{1,0:T(8,128)S(1)}, u32[]{:S(2)}, u32[]{:S(2)}) collective-permute-start(f32[16,128]{1,0:T(8,128)S(1)} %add_add_fusion.refs_0_), channel_id=1, source_target_pairs={{0,64},{2,66},{4,68},{6,70},{8,72},{10,74},{12,76},{14,78},{16,80}... | collective-permute-start | bytes 24584 | tf_op jit(solution)/shard_map/ppermute | solution.py:574
  53.5 1.1 %collective-permute-start.12 = (f32[16,128]{1,0:T(8,128)S(1)}, f32[16,128]{1,0:T(8,128)S(1)}, u32[]{:S(2)}, u32[]{:S(2)}) collective-permute-start(f32[16,128]{1,0:T(8,128)S(1)} %add_add_fusion.refs_0_), channel_id=1, source_target_pairs={{0,96},{2,98},{4,100},{6,102},{8,104},{10,106},{12,108},{14,110},{... | collective-permute-start | bytes 24584 | tf_op jit(solution)/shard_map/ppermute | solution.py:574
  54.7 0.0 collective-permute-start.11
  54.7 0.0 copy-done
  54.7 1.0 %collective-permute-done.13.refs_3_ = f32[16,128]{1,0:T(8,128)S(1)} collective-permute-done((f32[16,128]{1,0:T(8,128)S(1)}, f32[16,128]{1,0:T(8,128)S(1)}, u32[]{:S(2)}, u32[]{:S(2)}) %collective-permute-start.13) | collective-permute-done | bytes 8224 | tf_op jit(solution)/shard_map/ppermute | solution.py:574
  55.7 2.7 %collective-permute-done.12.refs_2_ = f32[16,128]{1,0:T(8,128)S(1)} collective-permute-done((f32[16,128]{1,0:T(8,128)S(1)}, f32[16,128]{1,0:T(8,128)S(1)}, u32[]{:S(2)}, u32[]{:S(2)}) %collective-permute-start.12) | collective-permute-done | bytes 8224 | tf_op jit(solution)/shard_map/ppermute | solution.py:574
  58.4 0.0 collective-permute-done.11.refs_1_
  58.4 5.7 %solve.1 = (f32[40,16,1024]{2,1,0:T(8,128)}, f32[40,16,1024]{2,1,0:T(8,128)}) custom-call(f32[16,128]{1,0:T(8,128)S(1)} %add_add_fusion.refs_0_, f32[16,128]{1,0:T(8,128)S(1)} %collective-permute-done.11.refs_1_, f32[16,128]{1,0:T(8,128)S(1)} %collective-permute-done.12.refs_2_, f32[16,128]{1,0:T(8,128)S(1)} %collective-permute-done.13.refs_3_, ...), custom_call_target="tpu_custom_call" | custom-call | tf_op jit(solution)/shard_map/solve/pallas_call | solution.py:552
  (4 shorter events, 0.0 us)
Async XLA Ops:
  0.6 5.0 %collective-permute-start = (bf16[1088,1024]{1,0:T(8,128)(2,1)}, bf16[1088,1024]{1,0:T(8,128)(2,1)S(1)}, u32[]{:S(2)}, u32[]{:S(2)}) collective-permute-start(bf16[1088,1024]{1,0:T(8,128)(2,1)} %bitcast.3), channel_id=1, source_target_pairs={{0,1},{1,0},{2,3},{3,2},{4,5},{5,4},{6,7},{7,6},{8,9},{9,8},{10,11... | collective-permute-start | bytes 6684680 | tf_op jit(solution)/shard_map/ppermute | solution.py:131
  8.9 13.5 %collective-permute-start.3 = (bf16[1536,128]{1,0:T(8,128)(2,1)S(1)}, bf16[1536,128]{1,0:T(8,128)(2,1)S(1)}, u32[]{:S(2)}, u32[]{:S(2)}) collective-permute-start(bf16[1536,128]{1,0:T(8,128)(2,1)S(1)} %get-tuple-element.30), channel_id=1, source_target_pairs={{0,2},{2,0},{4,6},{6,4},{8,10},{10,8},{12,14},{14,12},{16,18},{18,... | collective-permute-start | bytes 1179656 | tf_op jit(solution)/shard_map/ppermute | solution.py:590
  10.7 11.7 %collective-permute-start.4 = (bf16[1536,128]{1,0:T(8,128)(2,1)S(1)}, bf16[1536,128]{1,0:T(8,128)(2,1)S(1)}, u32[]{:S(2)}, u32[]{:S(2)}) collective-permute-start(bf16[1536,128]{1,0:T(8,128)(2,1)S(1)} %get-tuple-element.31), channel_id=1, source_target_pairs={{2,4},{6,8},{10,12},{14,16},{18,20},{22,24},{26,28},{30,32},{34,36... | collective-permute-start | bytes 1179656 | tf_op jit(solution)/shard_map/ppermute | solution.py:591
  13.7 13.4 %collective-permute-start.1 = (bf16[1024,128]{1,0:T(8,128)(2,1)S(1)}, bf16[1024,128]{1,0:T(8,128)(2,1)S(1)}, u32[]{:S(2)}, u32[]{:S(2)}) collective-permute-start(bf16[1024,128]{1,0:T(8,128)(2,1)S(1)} %get-tuple-element.26), channel_id=1, source_target_pairs={{0,2},{2,0},{4,6},{6,4},{8,10},{10,8},{12,14},{14,12},{16,18},{18,... | collective-permute-start | bytes 786440 | tf_op jit(solution)/shard_map/ppermute | solution.py:590
  17.9 9.2 %collective-permute-start.2 = (bf16[1024,128]{1,0:T(8,128)(2,1)S(1)}, bf16[1024,128]{1,0:T(8,128)(2,1)S(1)}, u32[]{:S(2)}, u32[]{:S(2)}) collective-permute-start(bf16[1024,128]{1,0:T(8,128)(2,1)S(1)} %get-tuple-element.27), channel_id=1, source_target_pairs={{2,4},{6,8},{10,12},{14,16},{18,20},{22,24},{26,28},{30,32},{34,36... | collective-permute-start | bytes 786440 | tf_op jit(solution)/shard_map/ppermute | solution.py:591
  27.1 27.5 %copy-start = (f32[40]{0:T(128)S(1)}, f32[40]{0:T(128)}, u32[]{:S(2)}) copy-start(f32[40]{0:T(128)} %param.5) | copy-start | bytes 484
  30.3 7.5 %collective-permute-start.7 = (f32[16,128]{1,0:T(8,128)S(1)}, f32[16,128]{1,0:T(8,128)S(1)}, u32[]{:S(2)}, u32[]{:S(2)}) collective-permute-start(f32[16,128]{1,0:T(8,128)S(1)} %get-tuple-element.42), channel_id=1, source_target_pairs={{0,4},{2,6},{4,0},{6,2},{8,12},{10,14},{12,8},{14,10},{16,20},{18,... | collective-permute-start | bytes 24584 | tf_op jit(solution)/shard_map/ppermute | solution.py:574
  35.5 4.9 %collective-permute-start.6 = (f32[16,128]{1,0:T(8,128)S(1)}, f32[16,128]{1,0:T(8,128)S(1)}, u32[]{:S(2)}, u32[]{:S(2)}) collective-permute-start(f32[16,128]{1,0:T(8,128)S(1)} %get-tuple-element.42), channel_id=1, source_target_pairs={{0,6},{2,4},{4,2},{6,0},{8,14},{10,12},{12,10},{14,8},{16,22},{18,... | collective-permute-start | bytes 24584 | tf_op jit(solution)/shard_map/ppermute | solution.py:574
  37.4 3.7 %collective-permute-start.5 = (f32[16,128]{1,0:T(8,128)S(1)}, f32[16,128]{1,0:T(8,128)S(1)}, u32[]{:S(2)}, u32[]{:S(2)}) collective-permute-start(f32[16,128]{1,0:T(8,128)S(1)} %get-tuple-element.42), channel_id=1, source_target_pairs={{0,2},{2,0},{4,6},{6,4},{8,10},{10,8},{12,14},{14,12},{16,18},{18,... | collective-permute-start | bytes 24584 | tf_op jit(solution)/shard_map/ppermute | solution.py:574
  41.1 6.6 %collective-permute-start.10 = (f32[16,128]{1,0:T(8,128)S(1)}, f32[16,128]{1,0:T(8,128)S(1)}, u32[]{:S(2)}, u32[]{:S(2)}) collective-permute-start(f32[16,128]{1,0:T(8,128)S(1)} %add_add_fusion.1), channel_id=1, source_target_pairs={{0,16},{2,18},{4,20},{6,22},{8,24},{10,26},{12,28},{14,30},{16,0},... | collective-permute-start | bytes 24584 | tf_op jit(solution)/shard_map/ppermute | solution.py:574
  44.6 4.9 %collective-permute-start.9 = (f32[16,128]{1,0:T(8,128)S(1)}, f32[16,128]{1,0:T(8,128)S(1)}, u32[]{:S(2)}, u32[]{:S(2)}) collective-permute-start(f32[16,128]{1,0:T(8,128)S(1)} %add_add_fusion.1), channel_id=1, source_target_pairs={{0,24},{2,26},{4,28},{6,30},{8,16},{10,18},{12,20},{14,22},{16,8},... | collective-permute-start | bytes 24584 | tf_op jit(solution)/shard_map/ppermute | solution.py:574
  46.9 3.7 %collective-permute-start.8 = (f32[16,128]{1,0:T(8,128)S(1)}, f32[16,128]{1,0:T(8,128)S(1)}, u32[]{:S(2)}, u32[]{:S(2)}) collective-permute-start(f32[16,128]{1,0:T(8,128)S(1)} %add_add_fusion.1), channel_id=1, source_target_pairs={{0,8},{2,10},{4,12},{6,14},{8,0},{10,2},{12,4},{14,6},{16,24},{18,... | collective-permute-start | bytes 24584 | tf_op jit(solution)/shard_map/ppermute | solution.py:574
  50.5 5.2 %collective-permute-start.13 = (f32[16,128]{1,0:T(8,128)S(1)}, f32[16,128]{1,0:T(8,128)S(1)}, u32[]{:S(2)}, u32[]{:S(2)}) collective-permute-start(f32[16,128]{1,0:T(8,128)S(1)} %add_add_fusion.refs_0_), channel_id=1, source_target_pairs={{0,64},{2,66},{4,68},{6,70},{8,72},{10,74},{12,76},{14,78},{16,80}... | collective-permute-start | bytes 24584 | tf_op jit(solution)/shard_map/ppermute | solution.py:574
  53.5 4.9 %collective-permute-start.12 = (f32[16,128]{1,0:T(8,128)S(1)}, f32[16,128]{1,0:T(8,128)S(1)}, u32[]{:S(2)}, u32[]{:S(2)}) collective-permute-start(f32[16,128]{1,0:T(8,128)S(1)} %add_add_fusion.refs_0_), channel_id=1, source_target_pairs={{0,96},{2,98},{4,100},{6,102},{8,104},{10,106},{12,108},{14,110},{... | collective-permute-start | bytes 24584 | tf_op jit(solution)/shard_map/ppermute | solution.py:574
  54.7 3.7 %collective-permute-start.11 = (f32[16,128]{1,0:T(8,128)S(1)}, f32[16,128]{1,0:T(8,128)S(1)}, u32[]{:S(2)}, u32[]{:S(2)}) collective-permute-start(f32[16,128]{1,0:T(8,128)S(1)} %add_add_fusion.refs_0_), channel_id=1, source_target_pairs={{0,32},{2,34},{4,36},{6,38},{8,40},{10,42},{12,44},{14,46},{16,48}... | collective-permute-start | bytes 24584 | tf_op jit(solution)/shard_map/ppermute | solution.py:574
